TPU v7x, 32 devices: a whole 2x2x4 slice. The times are simulated.
32 devices in a mesh: gx: 4 (over y, x), gy: 2 (over core), ha: 4 (over z).
Axes of the slice: x: 2, y: 2, z: 4, core: 2. Of those that a mesh axis runs over, the one named last changes fastest.
Arguments:
- level_set: float32 [32, 32, 40, 128], P('gx', 'gy', 'ha'), may hold values from -4 to 4
- wind_field: float32 [2, 32, 32], P(None, 'gx', 'gy'), may hold values from -3 to 3
Outputs:
- increment: float32 [32, 32, 40, 128], P('gx', 'gy', 'ha')
All inputs are finite; a program needn't handle non-finite values.
Results may differ from a plain program's by a relative error of at most 0.000073.
Values sent between devices are 32-bit elements; how exact they have to be, the bound alone decides.
No kernel may reach another device: no remote copies, remote signals or barrier semaphores. Data moves between devices by JAX's collectives and lax.ppermute only.
A program may use at most 128 MiB of HBM per device.

v0:
```python
import math

import jax
import jax.numpy as jnp
from jax import lax
from jax.sharding import PartitionSpec as P

CELL_SIZE = 0.05
SPEED_LOW = 0.1
SPEED_SPAN = 0.4
TURN_MAX = 1.0
ACCEL_MAX = 0.05
CFL_NUMBER = 0.5
WENO_EPS = 1e-06


def with_halo(cells, sides, width, closed):
    for axis, dim in sides:
        count = lax.axis_size(axis)
        ends = count if closed else count - 1
        head = lax.slice_in_dim(cells, 0, width, axis=dim)
        tail = lax.slice_in_dim(cells, cells.shape[dim] - width, cells.shape[dim], axis=dim)
        cells = jnp.concatenate(
            [
                lax.ppermute(tail, axis, [(i, (i + 1) % count) for i in range(ends)]),
                cells,
                lax.ppermute(head, axis, [((i + 1) % count, i) for i in range(ends)]),
            ],
            axis=dim,
        )
    return cells


def ghost_rows(values, along, at_low):
    length = values.shape[along]
    if at_low:
        edge_row = lax.slice_in_dim(values, 0, 1, axis=along)
        next_row = lax.slice_in_dim(values, 1, 2, axis=along)
        reaches = (3.0, 2.0, 1.0)
    else:
        edge_row = lax.slice_in_dim(values, length - 1, length, axis=along)
        next_row = lax.slice_in_dim(values, length - 2, length - 1, axis=along)
        reaches = (1.0, 2.0, 3.0)
    slope_edge = edge_row - next_row
    return jnp.concatenate([edge_row + distance * slope_edge for distance in reaches], axis=along)


def fix_edges(extended, along, at_start, at_end, length):
    interior = lax.slice_in_dim(extended, 3, 3 + length, axis=along)
    below_rows = jnp.where(
        at_start, ghost_rows(interior, along, True), lax.slice_in_dim(extended, 0, 3, axis=along)
    )
    above_rows = jnp.where(
        at_end,
        ghost_rows(interior, along, False),
        lax.slice_in_dim(extended, 3 + length, 6 + length, axis=along),
    )
    return jnp.concatenate([below_rows, interior, above_rows], axis=along)


def speed_shifts(values):
    length = values.shape[3]
    below_rows = ghost_rows(values, 3, True)
    above_rows = ghost_rows(values, 3, False)
    shifted = []
    for displace in range(-3, 4):
        pieces = []
        if displace < 0:
            pieces.append(lax.slice_in_dim(below_rows, 3 + displace, 3, axis=3))
        pieces.append(lax.slice_in_dim(values, max(displace, 0), length + min(displace, 0), axis=3))
        if displace > 0:
            pieces.append(lax.slice_in_dim(above_rows, 0, displace, axis=3))
        shifted.append(jnp.concatenate(pieces, axis=3) if len(pieces) > 1 else pieces[0])
    return shifted


def weno_side(left_far, left_near, middle, right_near, right_far):
    guess_one = left_far * (1.0 / 3.0) - left_near * (7.0 / 6.0) + middle * (11.0 / 6.0)
    guess_two = -left_near * (1.0 / 6.0) + middle * (5.0 / 6.0) + right_near * (1.0 / 3.0)
    guess_three = middle * (1.0 / 3.0) + right_near * (5.0 / 6.0) - right_far * (1.0 / 6.0)
    smooth_one = 13.0 / 12.0 * jnp.square(left_far - 2.0 * left_near + middle) + 0.25 * jnp.square(
        left_far - 4.0 * left_near + 3.0 * middle
    )
    smooth_two = 13.0 / 12.0 * jnp.square(
        left_near - 2.0 * middle + right_near
    ) + 0.25 * jnp.square(left_near - right_near)
    smooth_three = 13.0 / 12.0 * jnp.square(
        middle - 2.0 * right_near + right_far
    ) + 0.25 * jnp.square(3.0 * middle - 4.0 * right_near + right_far)
    weight_one = 0.1 / jnp.square(smooth_one + WENO_EPS)
    weight_two = 0.6 / jnp.square(smooth_two + WENO_EPS)
    weight_three = 0.3 / jnp.square(smooth_three + WENO_EPS)
    return (weight_one * guess_one + weight_two * guess_two + weight_three * guess_three) / (
        weight_one + weight_two + weight_three
    )


def weno_pair(shifted, spacing):
    slopes = [(shifted[position + 1] - shifted[position]) / spacing for position in range(6)]
    left_slope = weno_side(slopes[0], slopes[1], slopes[2], slopes[3], slopes[4])
    right_slope = weno_side(slopes[5], slopes[4], slopes[3], slopes[2], slopes[1])
    return (left_slope, right_slope)


def cell_rates(cos_head, sin_head, speeds, wind_x, wind_y, d_theta, d_speed):
    along_x = speeds[None, None, None, :] * cos_head[None, None, :, None] + wind_x[:, :, None, None]
    along_y = speeds[None, None, None, :] * sin_head[None, None, :, None] + wind_y[:, :, None, None]
    return (
        jnp.abs(along_x) / CELL_SIZE
        + jnp.abs(along_y) / CELL_SIZE
        + TURN_MAX / d_theta
        + ACCEL_MAX / d_speed
    )


def hamilton(x_pair, y_pair, head_pair, speed_pair, cos_head, sin_head, speeds, wind_x, wind_y):
    flow_x = speeds[None, None, None, :] * cos_head[None, None, :, None] + wind_x[:, :, None, None]
    flow_y = speeds[None, None, None, :] * sin_head[None, None, :, None] + wind_y[:, :, None, None]
    mean_x = 0.5 * (x_pair[0] + x_pair[1])
    mean_y = 0.5 * (y_pair[0] + y_pair[1])
    mean_head = 0.5 * (head_pair[0] + head_pair[1])
    mean_speed = 0.5 * (speed_pair[0] + speed_pair[1])
    value = -(
        flow_x * mean_x
        + flow_y * mean_y
        + TURN_MAX * jnp.abs(mean_head)
        + ACCEL_MAX * jnp.abs(mean_speed)
    )
    damping = 0.5 * (
        jnp.abs(flow_x) * (x_pair[1] - x_pair[0])
        + jnp.abs(flow_y) * (y_pair[1] - y_pair[0])
        + TURN_MAX * (head_pair[1] - head_pair[0])
        + ACCEL_MAX * (speed_pair[1] - speed_pair[0])
    )
    return -jnp.maximum(value - damping, 0.0)


def body(level_set, wind_field):
    cells_x, cells_y, cells_h, cells_v = level_set.shape
    n_head = cells_h * lax.axis_size("ha")
    head_base = lax.axis_index("ha") * cells_h
    start_x = lax.axis_index("gx") == 0
    end_x = lax.axis_index("gx") == lax.axis_size("gx") - 1
    start_y = lax.axis_index("gy") == 0
    end_y = lax.axis_index("gy") == lax.axis_size("gy") - 1
    wind_x = wind_field[0]
    wind_y = wind_field[1]
    d_theta = 2.0 * math.pi / n_head
    d_speed = SPEED_SPAN / cells_v
    speeds = (
        SPEED_LOW
        + SPEED_SPAN * (jnp.arange(cells_v, dtype=jnp.int32).astype(jnp.float32) + 0.5) / cells_v
    )

    def headings(offset, height):
        slots = (head_base - offset + jnp.arange(height, dtype=jnp.int32) + n_head) % n_head
        angles = slots.astype(jnp.float32) * d_theta
        return (jnp.cos(angles), jnp.sin(angles))

    every_angle = jnp.arange(n_head, dtype=jnp.int32).astype(jnp.float32) * d_theta
    end_speeds = jnp.stack([speeds[0], speeds[cells_v - 1]])
    local_top = jnp.max(
        cell_rates(
            jnp.cos(every_angle), jnp.sin(every_angle), end_speeds, wind_x, wind_y, d_theta, d_speed
        )
    )
    top_rate = lax.pmax(local_top, ("gx", "gy"))
    time_step = CFL_NUMBER / top_rate

    def slope_field(center, around, offset):
        height = center.shape[2]
        extended = with_halo(center, (("gx", 0), ("gy", 1)), 3, False)
        extended = fix_edges(extended, 0, start_x, end_x, cells_x)
        extended = fix_edges(extended, 1, start_y, end_y, cells_y)
        x_shifted = [
            extended[3 + displace : 3 + displace + cells_x, 3 : 3 + cells_y]
            for displace in range(-3, 4)
        ]
        y_shifted = [
            extended[3 : 3 + cells_x, 3 + displace : 3 + displace + cells_y]
            for displace in range(-3, 4)
        ]
        head_shifted = [
            around[:, :, 3 + displace : 3 + displace + height] for displace in range(-3, 4)
        ]
        cos_head, sin_head = headings(offset, height)
        return hamilton(
            weno_pair(x_shifted, CELL_SIZE),
            weno_pair(y_shifted, CELL_SIZE),
            weno_pair(head_shifted, d_theta),
            weno_pair(speed_shifts(center), d_speed),
            cos_head,
            sin_head,
            speeds,
            wind_x,
            wind_y,
        )

    def around_heads(surface):
        return with_halo(surface, (("ha", 2),), 3, True)

    section_one = level_set + time_step * slope_field(level_set, around_heads(level_set), 0)
    section_two = 0.75 * level_set + 0.25 * (
        section_one + time_step * slope_field(section_one, around_heads(section_one), 0)
    )
    advanced = 1.0 / 3.0 * level_set + 2.0 / 3.0 * (
        section_two + time_step * slope_field(section_two, around_heads(section_two), 0)
    )
    return advanced - level_set


def solution(mesh):
    return jax.shard_map(
        body,
        mesh=mesh,
        in_specs=(P("gx", "gy", "ha", None), P(None, "gx", "gy")),
        out_specs=P("gx", "gy", "ha", None),
        check_vma=False,
    )
```

profile of v0, /device:TPU:0, one launch (start us, length us, event | category | flops | bytes accessed | tf_op | source)
XLA Modules:
  0.0 161.7 jit_solution(9486974208186733224)
XLA Ops:
  0.0 1.8 %fusion.560 = (f32[8,16,3,128]{3,1,2,0:T(8,128)S(1)}, f32[8,16,3,128]{3,1,2,0:T(8,128)}) fusion(f32[8,16,10,128]{3,1,2,0:T(8,128)} %param.2), kind=kLoop, calls=%fused_computation.890 | loop fusion | bytes 786432 | tf_op jit(solution)/shard_map/slice | solution.py:22
  1.8 3.1 %collective-permute-start.4 = (f32[8,16,3,128]{3,1,2,0:T(8,128)S(1)}, f32[8,16,3,128]{3,1,2,0:T(8,128)S(1)}, u32[]{:S(2)}, u32[]{:S(2)}) collective-permute-start(f32[8,16,3,128]{3,1,2,0:T(8,128)S(1)} %get-tuple-element.108), channel_id=1, source_target_pairs={{0,1},{1,2},{2,3},{3,0},{4,5},{5,6},{6,7},{7,4},{8,9},{9,10},{10,1... | collective-permute-start | bytes 589832 | tf_op jit(solution)/shard_map/ppermute | solution.py:25
  4.9 2.0 %collective-permute-start.5 = (f32[8,16,3,128]{3,1,2,0:T(8,128)}, f32[8,16,3,128]{3,1,2,0:T(8,128)}, u32[]{:S(2)}, u32[]{:S(2)}) collective-permute-start(f32[8,16,3,128]{3,1,2,0:T(8,128)} %get-tuple-element.109), channel_id=1, source_target_pairs={{1,0},{2,1},{3,2},{0,3},{5,4},{6,5},{7,6},{4,7},{9,8},{10,9},{11,1... | collective-permute-start | bytes 589832 | tf_op jit(solution)/shard_map/ppermute | solution.py:27
  6.9 1.8 %fusion.559 = (f32[3,16,10,128]{3,1,2,0:T(8,128)}, f32[3,16,10,128]{3,1,2,0:T(8,128)S(1)}) fusion(f32[8,16,10,128]{3,1,2,0:T(8,128)} %param.2), kind=kLoop, calls=%fused_computation.889 | loop fusion | bytes 983040 | tf_op jit(solution)/shard_map/slice | solution.py:21
  8.7 1.3 collective-permute-start.1
  10.0 4.6 %collective-permute-start = (f32[3,16,10,128]{3,1,2,0:T(8,128)S(1)}, f32[3,16,10,128]{3,1,2,0:T(8,128)S(1)}, u32[]{:S(2)}, u32[]{:S(2)}) collective-permute-start(f32[3,16,10,128]{3,1,2,0:T(8,128)S(1)} %get-tuple-element.104), channel_id=1, source_target_pairs={{0,8},{8,16},{16,24},{1,9},{9,17},{17,25},{2,10},{10,18},{18,26},{... | collective-permute-start | bytes 737288 | tf_op jit(solution)/shard_map/ppermute | solution.py:25
  14.6 1.3 fusion.561
  15.9 1.3 fusion.562
  17.2 1.3 fusion.563
  18.5 2.5 %multiply_add_fusion.28 = (f32[8,16,10,1]{3,1,2,0:T(8,128)}, f32[8,16,10,1]{3,1,2,0:T(8,128)}, f32[8,16,10,1]{3,1,2,0:T(8,128)}, f32[8,16,10,1]{3,1,2,0:T(8,128)...) fusion(f32[8,16,10,128]{3,1,2,0:T(8,128)S(1)} %copy-done), kind=kLoop, calls=%fused_computation.658 | loop fusion | flops 15360 | bytes 51200 | tf_op jit(solution)/shard_map/add | solution.py:45
  21.6 1.2 pad_maximum_fusion.52
  26.5 1.3 collective-permute-start.3
  27.8 4.5 %collective-permute-start.2 = (f32[14,3,10,128]{3,0,2,1:T(8,128)}, f32[14,3,10,128]{3,0,2,1:T(8,128)}, u32[]{:S(2)}, u32[]{:S(2)}) collective-permute-start(f32[14,3,10,128]{3,0,2,1:T(8,128)} %copy.175), channel_id=1, source_target_pairs={{0,4},{1,5},{2,6},{3,7},{8,12},{9,13},{10,14},{11,15},{16,20},{17,... | collective-permute-start | bytes 645128 | tf_op jit(solution)/shard_map/ppermute | solution.py:25
  32.4 12.9 %pmax.7 = f32[]{:T(128)} all-reduce(f32[]{:T(128)} %fusion.530), channel_id=1, replica_groups=mesh['gx'=4,'gy'=2,'ha'=4] {'gx','gy'}, use_global_device_ids=true, to_apply=%region_1.0 | all-reduce | flops 1 | bytes 8 | tf_op jit(solution)/shard_map/pmax | solution.py:167
  47.0 1.1 copy.178
  53.5 17.6 %fusion.24 = f32[8,16,10,128]{3,1,2,0:T(8,128)S(1)} fusion(f32[8,16,10,128]{3,1,2,0:T(8,128)S(1)} %copy-done, f32[8,16,10,1]{3,1,2,0:T(8,128)S(1)} %copy-done.11, f32[8,16,10,1]{3,1,2,0:T(8,128)S(1)} %copy-done.9, f32[8,16,10,1]{3,1,2,0:T(8,128)S(1)} %copy-done.12, f32[8,16,10,125]{3,1,2,0:T(8,128)S(1)} %copy-done.6, f32[8,16,10,126]{3,1,2,0:T(8,128)S(1)} %copy-done.4, ...), kind=kLoop, calls=%fused_computation.102 | loop fusion | flops 99123200 | bytes 12309508 | tf_op jit(solution)/shard_map/add | solution.py:202
  72.2 3.8 %collective-permute-start.11 = (f32[8,16,3,128]{3,1,2,0:T(8,128)S(1)}, f32[8,16,3,128]{3,1,2,0:T(8,128)S(1)}, u32[]{:S(2)}, u32[]{:S(2)}) collective-permute-start(f32[8,16,3,128]{3,1,2,0:T(8,128)S(1)} %get-tuple-element.90), channel_id=1, source_target_pairs={{1,0},{2,1},{3,2},{0,3},{5,4},{6,5},{7,6},{4,7},{9,8},{10,9},{11,1... | collective-permute-start | bytes 589832 | tf_op jit(solution)/shard_map/ppermute | solution.py:27
  76.0 2.3 %collective-permute-start.6 = (f32[3,16,10,128]{3,1,2,0:T(8,128)S(1)}, f32[3,16,10,128]{3,1,2,0:T(8,128)S(1)}, u32[]{:S(2)}, u32[]{:S(2)}) collective-permute-start(f32[3,16,10,128]{3,1,2,0:T(8,128)S(1)} %get-tuple-element.87), channel_id=1, source_target_pairs={{0,8},{8,16},{16,24},{1,9},{9,17},{17,25},{2,10},{10,18},{18,26},{... | collective-permute-start | bytes 737288 | tf_op jit(solution)/shard_map/ppermute | solution.py:25
  78.3 1.3 collective-permute-start.7
  79.9 3.2 %collective-permute-done.6 = f32[3,16,10,128]{3,1,2,0:T(8,128)S(1)} collective-permute-done((f32[3,16,10,128]{3,1,2,0:T(8,128)S(1)}, f32[3,16,10,128]{3,1,2,0:T(8,128)S(1)}, u32[]{:S(2)}, u32[]{:S(2)}) %collective-permute-start.6) | collective-permute-done | bytes 245792 | tf_op jit(solution)/shard_map/ppermute | solution.py:25
  83.1 8.6 %collective-permute-done.7 = f32[3,16,10,128]{3,1,2,0:T(8,128)S(1)} collective-permute-done((f32[3,16,10,128]{3,1,2,0:T(8,128)S(1)}, f32[3,16,10,128]{3,1,2,0:T(8,128)S(1)}, u32[]{:S(2)}, u32[]{:S(2)}) %collective-permute-start.7) | collective-permute-done | bytes 245792 | tf_op jit(solution)/shard_map/ppermute | solution.py:27
  92.0 1.3 collective-permute-start.9
  93.3 3.2 %collective-permute-start.8 = (f32[14,3,10,128]{3,0,2,1:T(8,128)S(1)}, f32[14,3,10,128]{3,0,2,1:T(8,128)S(1)}, u32[]{:S(2)}, u32[]{:S(2)}) collective-permute-start(f32[14,3,10,128]{3,0,2,1:T(8,128)S(1)} %copy.179), channel_id=1, source_target_pairs={{0,4},{1,5},{2,6},{3,7},{8,12},{9,13},{10,14},{11,15},{16,20},{17,... | collective-permute-start | bytes 645128 | tf_op jit(solution)/shard_map/ppermute | solution.py:25
  99.6 17.6 %fusion.35 = f32[8,16,10,128]{3,1,2,0:T(8,128)S(1)} fusion(f32[8,16,10,128]{3,1,2,0:T(8,128)S(1)} %fusion.24, f32[8,16,10,1]{3,1,2,0:T(8,128)S(1)} %get-tuple-element.96, f32[8,16,10,1]{3,1,2,0:T(8,128)S(1)} %get-tuple-element.100, f32[8,16,10,1]{3,1,2,0:T(8,128)S(1)} %get-tuple-element.97, f32[8,16,10,125]{3,1,2,0:T(8,128)S(1)} %get-tuple-element.102, ...), kind=kLoop, calls=%fused_computation.113 | loop fusion | flops 100597760 | bytes 9425924 | tf_op jit(solution)/shard_map/add | solution.py:203
  118.2 3.8 %collective-permute-start.17 = (f32[8,16,3,128]{3,1,2,0:T(8,128)S(1)}, f32[8,16,3,128]{3,1,2,0:T(8,128)S(1)}, u32[]{:S(2)}, u32[]{:S(2)}) collective-permute-start(f32[8,16,3,128]{3,1,2,0:T(8,128)S(1)} %get-tuple-element.74), channel_id=1, source_target_pairs={{1,0},{2,1},{3,2},{0,3},{5,4},{6,5},{7,6},{4,7},{9,8},{10,9},{11,1... | collective-permute-start | bytes 589832 | tf_op jit(solution)/shard_map/ppermute | solution.py:27
  122.0 2.2 %collective-permute-start.12 = (f32[3,16,10,128]{3,1,2,0:T(8,128)S(1)}, f32[3,16,10,128]{3,1,2,0:T(8,128)S(1)}, u32[]{:S(2)}, u32[]{:S(2)}) collective-permute-start(f32[3,16,10,128]{3,1,2,0:T(8,128)S(1)} %get-tuple-element.71), channel_id=1, source_target_pairs={{0,8},{8,16},{16,24},{1,9},{9,17},{17,25},{2,10},{10,18},{18,26},{... | collective-permute-start | bytes 737288 | tf_op jit(solution)/shard_map/ppermute | solution.py:25
  124.3 1.3 collective-permute-start.13
  125.8 3.6 %collective-permute-done.12 = f32[3,16,10,128]{3,1,2,0:T(8,128)S(1)} collective-permute-done((f32[3,16,10,128]{3,1,2,0:T(8,128)S(1)}, f32[3,16,10,128]{3,1,2,0:T(8,128)S(1)}, u32[]{:S(2)}, u32[]{:S(2)}) %collective-permute-start.12) | collective-permute-done | bytes 245792 | tf_op jit(solution)/shard_map/ppermute | solution.py:25
  129.4 6.0 %collective-permute-done.13 = f32[3,16,10,128]{3,1,2,0:T(8,128)S(1)} collective-permute-done((f32[3,16,10,128]{3,1,2,0:T(8,128)S(1)}, f32[3,16,10,128]{3,1,2,0:T(8,128)S(1)}, u32[]{:S(2)}, u32[]{:S(2)}) %collective-permute-start.13) | collective-permute-done | bytes 245792 | tf_op jit(solution)/shard_map/ppermute | solution.py:27
  135.6 1.3 collective-permute-start.15
  136.9 3.1 %collective-permute-start.14 = (f32[14,3,10,128]{3,0,2,1:T(8,128)S(1)}, f32[14,3,10,128]{3,0,2,1:T(8,128)S(1)}, u32[]{:S(2)}, u32[]{:S(2)}) collective-permute-start(f32[14,3,10,128]{3,0,2,1:T(8,128)S(1)} %copy.183), channel_id=1, source_target_pairs={{0,4},{1,5},{2,6},{3,7},{8,12},{9,13},{10,14},{11,15},{16,20},{17,... | collective-permute-start | bytes 645128 | tf_op jit(solution)/shard_map/ppermute | solution.py:25
  143.3 18.4 %fusion.47 = f32[8,16,10,128]{3,1,2,0:T(8,128)} fusion(f32[8,16,10,128]{3,1,2,0:T(8,128)S(1)} %copy-done, f32[8,16,10,128]{3,1,2,0:T(8,128)S(1)} %fusion.35, f32[8,16,10,1]{3,1,2,0:T(8,128)S(1)} %get-tuple-element.80, f32[8,16,10,1]{3,1,2,0:T(8,128)S(1)} %get-tuple-element.84, f32[8,16,10,1]{3,1,2,0:T(8,128)S(1)} %get-tuple-element.81, ...), kind=kLoop, calls=%fused_computation.125 | loop fusion | flops 100761600 | bytes 9425924 | tf_op jit(solution)/shard_map/sub | solution.py:209
  (122 shorter events, 19.8 us)
Async XLA Ops:
  0.0 14.6 %copy-start = (f32[8,16,10,128]{3,1,2,0:T(8,128)S(1)}, f32[8,16,10,128]{3,1,2,0:T(8,128)}, u32[]{:S(2)}) copy-start(f32[8,16,10,128]{3,1,2,0:T(8,128)} %param.2) | copy-start | bytes 1966084
  1.8 21.9 %collective-permute-start.4 = (f32[8,16,3,128]{3,1,2,0:T(8,128)S(1)}, f32[8,16,3,128]{3,1,2,0:T(8,128)S(1)}, u32[]{:S(2)}, u32[]{:S(2)}) collective-permute-start(f32[8,16,3,128]{3,1,2,0:T(8,128)S(1)} %get-tuple-element.108), channel_id=1, source_target_pairs={{0,1},{1,2},{2,3},{3,0},{4,5},{5,6},{6,7},{7,4},{8,9},{9,10},{10,1... | collective-permute-start | bytes 589832 | tf_op jit(solution)/shard_map/ppermute | solution.py:25
  4.9 41.1 %collective-permute-start.5 = (f32[8,16,3,128]{3,1,2,0:T(8,128)}, f32[8,16,3,128]{3,1,2,0:T(8,128)}, u32[]{:S(2)}, u32[]{:S(2)}) collective-permute-start(f32[8,16,3,128]{3,1,2,0:T(8,128)} %get-tuple-element.109), channel_id=1, source_target_pairs={{1,0},{2,1},{3,2},{0,3},{5,4},{6,5},{7,6},{4,7},{9,8},{10,9},{11,1... | collective-permute-start | bytes 589832 | tf_op jit(solution)/shard_map/ppermute | solution.py:27
  8.7 15.2 %collective-permute-start.1 = (f32[3,16,10,128]{3,1,2,0:T(8,128)}, f32[3,16,10,128]{3,1,2,0:T(8,128)}, u32[]{:S(2)}, u32[]{:S(2)}) collective-permute-start(f32[3,16,10,128]{3,1,2,0:T(8,128)} %get-tuple-element.103), channel_id=1, source_target_pairs={{8,0},{16,8},{24,16},{9,1},{17,9},{25,17},{10,2},{18,10},{26,18},{... | collective-permute-start | bytes 737288 | tf_op jit(solution)/shard_map/ppermute | solution.py:27
  10.0 13.7 %collective-permute-start = (f32[3,16,10,128]{3,1,2,0:T(8,128)S(1)}, f32[3,16,10,128]{3,1,2,0:T(8,128)S(1)}, u32[]{:S(2)}, u32[]{:S(2)}) collective-permute-start(f32[3,16,10,128]{3,1,2,0:T(8,128)S(1)} %get-tuple-element.104), channel_id=1, source_target_pairs={{0,8},{8,16},{16,24},{1,9},{9,17},{17,25},{2,10},{10,18},{18,26},{... | collective-permute-start | bytes 737288 | tf_op jit(solution)/shard_map/ppermute | solution.py:25
  18.5 3.1 %copy-start.13 = (f32[2,8,16]{2,1,0:T(8,128)S(1)}, f32[2,8,16]{2,1,0:T(8,128)}, u32[]{:S(2)}) copy-start(f32[2,8,16]{2,1,0:T(8,128)} %param.3) | copy-start | bytes 3076
  26.5 20.4 %collective-permute-start.3 = (f32[14,3,10,128]{3,0,2,1:T(8,128)}, f32[14,3,10,128]{3,0,2,1:T(8,128)}, u32[]{:S(2)}, u32[]{:S(2)}) collective-permute-start(f32[14,3,10,128]{3,0,2,1:T(8,128)} %copy.176), channel_id=1, source_target_pairs={{4,0},{5,1},{6,2},{7,3},{12,8},{13,9},{14,10},{15,11},{20,16},{21,... | collective-permute-start | bytes 645128 | tf_op jit(solution)/shard_map/ppermute | solution.py:27
  27.8 20.2 %collective-permute-start.2 = (f32[14,3,10,128]{3,0,2,1:T(8,128)}, f32[14,3,10,128]{3,0,2,1:T(8,128)}, u32[]{:S(2)}, u32[]{:S(2)}) collective-permute-start(f32[14,3,10,128]{3,0,2,1:T(8,128)} %copy.175), channel_id=1, source_target_pairs={{0,4},{1,5},{2,6},{3,7},{8,12},{9,13},{10,14},{11,15},{16,20},{17,... | collective-permute-start | bytes 645128 | tf_op jit(solution)/shard_map/ppermute | solution.py:25
  50.2 1.1 copy-start.9
  50.2 1.3 copy-start.10
  50.2 1.5 copy-start.11
  50.2 1.7 %copy-start.12 = (f32[8,16,10,1]{3,1,2,0:T(8,128)S(1)}, f32[8,16,10,1]{3,1,2,0:T(8,128)}, u32[]{:S(2)}) copy-start(f32[8,16,10,1]{3,1,2,0:T(8,128)} %get-tuple-element.119) | copy-start | bytes 15364
  50.3 1.8 %copy-start.6 = (f32[8,16,10,125]{3,1,2,0:T(8,128)S(1)}, f32[8,16,10,125]{3,1,2,0:T(8,128)}, u32[]{:S(2)}) copy-start(f32[8,16,10,125]{3,1,2,0:T(8,128)} %get-tuple-element.121) | copy-start | bytes 1920004
  50.3 1.9 %copy-start.7 = (f32[8,16,10,1]{3,1,2,0:T(8,128)S(1)}, f32[8,16,10,1]{3,1,2,0:T(8,128)}, u32[]{:S(2)}) copy-start(f32[8,16,10,1]{3,1,2,0:T(8,128)} %get-tuple-element.114) | copy-start | bytes 15364
  50.3 2.1 %copy-start.8 = (f32[8,16,10,1]{3,1,2,0:T(8,128)S(1)}, f32[8,16,10,1]{3,1,2,0:T(8,128)}, u32[]{:S(2)}) copy-start(f32[8,16,10,1]{3,1,2,0:T(8,128)} %get-tuple-element.115) | copy-start | bytes 15364
  50.5 2.2 %copy-start.1 = (f32[8,16,10,127]{3,1,2,0:T(8,128)S(1)}, f32[8,16,10,127]{3,1,2,0:T(8,128)}, u32[]{:S(2)}) copy-start(f32[8,16,10,127]{3,1,2,0:T(8,128)} %get-tuple-element.110) | copy-start | bytes 1950724
  50.5 2.4 %copy-start.2 = (f32[8,16,10,127]{3,1,2,0:T(8,128)S(1)}, f32[8,16,10,127]{3,1,2,0:T(8,128)}, u32[]{:S(2)}) copy-start(f32[8,16,10,127]{3,1,2,0:T(8,128)} %get-tuple-element.111) | copy-start | bytes 1950724
  50.5 2.6 %copy-start.3 = (f32[8,16,10,126]{3,1,2,0:T(8,128)S(1)}, f32[8,16,10,126]{3,1,2,0:T(8,128)}, u32[]{:S(2)}) copy-start(f32[8,16,10,126]{3,1,2,0:T(8,128)} %get-tuple-element.112) | copy-start | bytes 1935364
  50.5 2.8 %copy-start.4 = (f32[8,16,10,126]{3,1,2,0:T(8,128)S(1)}, f32[8,16,10,126]{3,1,2,0:T(8,128)}, u32[]{:S(2)}) copy-start(f32[8,16,10,126]{3,1,2,0:T(8,128)} %get-tuple-element.113) | copy-start | bytes 1935364
  50.5 2.9 %copy-start.5 = (f32[8,16,10,125]{3,1,2,0:T(8,128)S(1)}, f32[8,16,10,125]{3,1,2,0:T(8,128)}, u32[]{:S(2)}) copy-start(f32[8,16,10,125]{3,1,2,0:T(8,128)} %get-tuple-element.120) | copy-start | bytes 1920004
  72.1 27.5 %collective-permute-start.10 = (f32[8,16,3,128]{3,1,2,0:T(8,128)S(1)}, f32[8,16,3,128]{3,1,2,0:T(8,128)S(1)}, u32[]{:S(2)}, u32[]{:S(2)}) collective-permute-start(f32[8,16,3,128]{3,1,2,0:T(8,128)S(1)} %get-tuple-element.89), channel_id=1, source_target_pairs={{0,1},{1,2},{2,3},{3,0},{4,5},{5,6},{6,7},{7,4},{8,9},{9,10},{10,1... | collective-permute-start | bytes 589832 | tf_op jit(solution)/shard_map/ppermute | solution.py:25
  72.2 27.5 %collective-permute-start.11 = (f32[8,16,3,128]{3,1,2,0:T(8,128)S(1)}, f32[8,16,3,128]{3,1,2,0:T(8,128)S(1)}, u32[]{:S(2)}, u32[]{:S(2)}) collective-permute-start(f32[8,16,3,128]{3,1,2,0:T(8,128)S(1)} %get-tuple-element.90), channel_id=1, source_target_pairs={{1,0},{2,1},{3,2},{0,3},{5,4},{6,5},{7,6},{4,7},{9,8},{10,9},{11,1... | collective-permute-start | bytes 589832 | tf_op jit(solution)/shard_map/ppermute | solution.py:27
  76.0 7.1 %collective-permute-start.6 = (f32[3,16,10,128]{3,1,2,0:T(8,128)S(1)}, f32[3,16,10,128]{3,1,2,0:T(8,128)S(1)}, u32[]{:S(2)}, u32[]{:S(2)}) collective-permute-start(f32[3,16,10,128]{3,1,2,0:T(8,128)S(1)} %get-tuple-element.87), channel_id=1, source_target_pairs={{0,8},{8,16},{16,24},{1,9},{9,17},{17,25},{2,10},{10,18},{18,26},{... | collective-permute-start | bytes 737288 | tf_op jit(solution)/shard_map/ppermute | solution.py:25
  78.3 13.4 %collective-permute-start.7 = (f32[3,16,10,128]{3,1,2,0:T(8,128)S(1)}, f32[3,16,10,128]{3,1,2,0:T(8,128)S(1)}, u32[]{:S(2)}, u32[]{:S(2)}) collective-permute-start(f32[3,16,10,128]{3,1,2,0:T(8,128)S(1)} %get-tuple-element.88), channel_id=1, source_target_pairs={{8,0},{16,8},{24,16},{9,1},{17,9},{25,17},{10,2},{18,10},{26,18},{... | collective-permute-start | bytes 737288 | tf_op jit(solution)/shard_map/ppermute | solution.py:27
  92.0 4.8 %collective-permute-start.9 = (f32[14,3,10,128]{3,0,2,1:T(8,128)S(1)}, f32[14,3,10,128]{3,0,2,1:T(8,128)S(1)}, u32[]{:S(2)}, u32[]{:S(2)}) collective-permute-start(f32[14,3,10,128]{3,0,2,1:T(8,128)S(1)} %copy.180), channel_id=1, source_target_pairs={{4,0},{5,1},{6,2},{7,3},{12,8},{13,9},{14,10},{15,11},{20,16},{21,... | collective-permute-start | bytes 645128 | tf_op jit(solution)/shard_map/ppermute | solution.py:27
  93.3 4.2 %collective-permute-start.8 = (f32[14,3,10,128]{3,0,2,1:T(8,128)S(1)}, f32[14,3,10,128]{3,0,2,1:T(8,128)S(1)}, u32[]{:S(2)}, u32[]{:S(2)}) collective-permute-start(f32[14,3,10,128]{3,0,2,1:T(8,128)S(1)} %copy.179), channel_id=1, source_target_pairs={{0,4},{1,5},{2,6},{3,7},{8,12},{9,13},{10,14},{11,15},{16,20},{17,... | collective-permute-start | bytes 645128 | tf_op jit(solution)/shard_map/ppermute | solution.py:25
  118.2 25.1 %collective-permute-start.16 = (f32[8,16,3,128]{3,1,2,0:T(8,128)S(1)}, f32[8,16,3,128]{3,1,2,0:T(8,128)S(1)}, u32[]{:S(2)}, u32[]{:S(2)}) collective-permute-start(f32[8,16,3,128]{3,1,2,0:T(8,128)S(1)} %get-tuple-element.73), channel_id=1, source_target_pairs={{0,1},{1,2},{2,3},{3,0},{4,5},{5,6},{6,7},{7,4},{8,9},{9,10},{10,1... | collective-permute-start | bytes 589832 | tf_op jit(solution)/shard_map/ppermute | solution.py:25
  118.2 25.1 %collective-permute-start.17 = (f32[8,16,3,128]{3,1,2,0:T(8,128)S(1)}, f32[8,16,3,128]{3,1,2,0:T(8,128)S(1)}, u32[]{:S(2)}, u32[]{:S(2)}) collective-permute-start(f32[8,16,3,128]{3,1,2,0:T(8,128)S(1)} %get-tuple-element.74), channel_id=1, source_target_pairs={{1,0},{2,1},{3,2},{0,3},{5,4},{6,5},{7,6},{4,7},{9,8},{10,9},{11,1... | collective-permute-start | bytes 589832 | tf_op jit(solution)/shard_map/ppermute | solution.py:27
  122.0 7.4 %collective-permute-start.12 = (f32[3,16,10,128]{3,1,2,0:T(8,128)S(1)}, f32[3,16,10,128]{3,1,2,0:T(8,128)S(1)}, u32[]{:S(2)}, u32[]{:S(2)}) collective-permute-start(f32[3,16,10,128]{3,1,2,0:T(8,128)S(1)} %get-tuple-element.71), channel_id=1, source_target_pairs={{0,8},{8,16},{16,24},{1,9},{9,17},{17,25},{2,10},{10,18},{18,26},{... | collective-permute-start | bytes 737288 | tf_op jit(solution)/shard_map/ppermute | solution.py:25
  124.3 11.2 %collective-permute-start.13 = (f32[3,16,10,128]{3,1,2,0:T(8,128)S(1)}, f32[3,16,10,128]{3,1,2,0:T(8,128)S(1)}, u32[]{:S(2)}, u32[]{:S(2)}) collective-permute-start(f32[3,16,10,128]{3,1,2,0:T(8,128)S(1)} %get-tuple-element.72), channel_id=1, source_target_pairs={{8,0},{16,8},{24,16},{9,1},{17,9},{25,17},{10,2},{18,10},{26,18},{... | collective-permute-start | bytes 737288 | tf_op jit(solution)/shard_map/ppermute | solution.py:27
  135.6 4.6 %collective-permute-start.15 = (f32[14,3,10,128]{3,0,2,1:T(8,128)S(1)}, f32[14,3,10,128]{3,0,2,1:T(8,128)S(1)}, u32[]{:S(2)}, u32[]{:S(2)}) collective-permute-start(f32[14,3,10,128]{3,0,2,1:T(8,128)S(1)} %copy.184), channel_id=1, source_target_pairs={{4,0},{5,1},{6,2},{7,3},{12,8},{13,9},{14,10},{15,11},{20,16},{21,... | collective-permute-start | bytes 645128 | tf_op jit(solution)/shard_map/ppermute | solution.py:27
  136.9 4.2 %collective-permute-start.14 = (f32[14,3,10,128]{3,0,2,1:T(8,128)S(1)}, f32[14,3,10,128]{3,0,2,1:T(8,128)S(1)}, u32[]{:S(2)}, u32[]{:S(2)}) collective-permute-start(f32[14,3,10,128]{3,0,2,1:T(8,128)S(1)} %copy.183), channel_id=1, source_target_pairs={{0,4},{1,5},{2,6},{3,7},{8,12},{9,13},{10,14},{11,15},{16,20},{17,... | collective-permute-start | bytes 645128 | tf_op jit(solution)/shard_map/ppermute | solution.py:25
where the time goes:
time: 162 us
  other arithmetic  65.1 us (40%)
  starting transfers between devices  40.4 us (25%)
  waiting for transfers between devices  22.8 us (14%)
  local copies, waits for them, and re-layouts  19.1 us (12%)
  blocking collectives  12.9 us (8%)
    ppermute x9, starting transfers between devices, with_halo(): lax.ppermute(tail, axis, [(i, (i + 1) % count) for i in range(ends)])  23 us
    sub x1, other arithmetic, body(): return advanced - level_set  18.4 us
    add x1, other arithmetic, body(): level_set + time_step * slope_field(level_set, around_heads(level_set), 0)  17.6 us
    add x1, other arithmetic, body(): 0.75 * level_set  17.6 us
    ppermute x9, starting transfers between devices, with_halo(): lax.ppermute(head, axis, [((i + 1) % count, i) for i in range(ends)])  17.4 us
    ppermute x9, waiting for transfers between devices, with_halo(): lax.ppermute(head, axis, [((i + 1) % count, i) for i in range(ends)])  14.7 us
    pmax x1, blocking collectives, body(): top_rate = lax.pmax(local_top, ('gx', 'gy'))  12.9 us
    ppermute x9, waiting for transfers between devices, with_halo(): lax.ppermute(tail, axis, [(i, (i + 1) % count) for i in range(ends)])  8.09 us
  transfers between devices with their start and end apart: 18, of which 6 were waited for; matrix products, arithmetic and copies ran while one was open for 13% of the time, Pallas kernels for 0%

commit v1 on v0

v1 whole, which is shorter than its diff:
```python
import functools
import math

import jax
import jax.numpy as jnp
import numpy as np
from jax import lax
from jax.experimental import pallas as pl
from jax.experimental.pallas import tpu as pltpu
from jax.sharding import PartitionSpec as P

CELL_SIZE = 0.05
SPEED_LOW = 0.1
SPEED_SPAN = 0.4
TURN_MAX = 1.0
ACCEL_MAX = 0.05
CFL_NUMBER = 0.5
WENO_EPS = 1e-06
SUB = 8
LANES = 128


def weno_terms(us, eps):
    n = len(us) - 6
    u = {i - 3: v for i, v in enumerate(us)}
    q = {r: u[r] - u[r - 1] for r in range(-2, n + 3)}
    p = {m: q[m + 1] - q[m] for m in range(-2, n + 2)}
    t, alpha, beta, gamma, a3, g3 = {}, {}, {}, {}, {}, {}
    for r in range(-1, n + 2):
        t[r] = p[r] - p[r - 1]
        z = 1.5 * t[r]
        base = t[r] * t[r] + ((0.75 * p[r - 1]) * p[r] + eps)
        if r <= n - 1:
            s = base + p[r] * z
            alpha[r] = pl.reciprocal(s * s, approx=APPROX)
            a3[r] = (1.0 / 3.0) * alpha[r]
        if r >= 1:
            s = base - p[r - 1] * z
            gamma[r] = pl.reciprocal(s * s, approx=APPROX)
            g3[r] = (1.0 / 3.0) * gamma[r]
        if 0 <= r <= n:
            beta[r] = pl.reciprocal(0.5 * (base * base), approx=APPROX)
    f = {m: t[m] - t[m + 1] for m in range(-1, n + 1)}
    f2 = {m: f[m] + f[m] for m in range(-1, n + 1)}
    return n, q, p, alpha, beta, gamma, a3, g3, f, f2


APPROX = True


def line_max(us, eps, scale):
    n, q, p, alpha, beta, gamma, a3, g3, f, f2 = weno_terms(us, eps)
    outs = []
    for i in range(n):
        er = (g3[i + 2] * f2[i + 1] + alpha[i] * f[i]) * pl.reciprocal(
            g3[i + 2] + beta[i + 1] + alpha[i], approx=APPROX
        )
        el = (a3[i - 1] * f2[i - 1] + gamma[i + 1] * f[i]) * pl.reciprocal(
            a3[i - 1] + beta[i] + gamma[i + 1], approx=APPROX
        )
        p2 = p[i] + p[i]
        right = (6.0 * q[i + 1] - p2) - (p[i + 1] + er)
        minus_left = -(6.0 * q[i] + p2) - (p[i - 1] + el)
        outs.append(scale * jnp.maximum(right, minus_left))
    return outs


def line_upwind(us, eps, flows):
    n, q, p, alpha, beta, gamma, a3, g3, f, f2 = weno_terms(us, eps)
    outs = []
    for i in range(n):
        flow = flows(i)
        right = flow > 0.0
        w1 = jnp.where(right, g3[i + 2], a3[i - 1])
        w2 = jnp.where(right, beta[i + 1], beta[i])
        w3 = jnp.where(right, alpha[i], gamma[i + 1])
        f1 = jnp.where(right, f2[i + 1], f2[i - 1])
        pn = jnp.where(right, p[i + 1], p[i - 1])
        qn = jnp.where(right, q[i + 1], q[i])
        e = (w1 * f1 + w3 * f[i]) * pl.reciprocal(w1 + w2 + w3, approx=APPROX)
        x = pn + (p[i] + p[i]) + e
        outs.append(flow * qn - jnp.abs((1.0 / 6.0) * flow) * x)
    return outs


def edge_fix(low, center_low, center_high, high, flags):
    first, last = flags
    slope = center_low[0] - center_low[1]
    low = [
        jnp.where(first, center_low[0] + reach * slope, got)
        for reach, got in zip((3.0, 2.0, 1.0), low)
    ]
    slope = center_high[1] - center_high[0]
    high = [
        jnp.where(last, center_high[1] + reach * slope, got)
        for reach, got in zip((1.0, 2.0, 3.0), high)
    ]
    return low, high


def speed_kernel(u_ref, acc_ref, line_ref, out_ref, *, eps, scale):
    rows = u_ref.shape[0]
    count = LANES // SUB

    def group(g, carry):
        base = pl.multiple_of(g * LANES, LANES)
        turned = u_ref[pl.ds(base, LANES), :].T
        line_ref[pl.ds(SUB, LANES), :] = turned
        slope = turned[0:1] - turned[1:2]
        for reach in (1, 2, 3):
            line_ref[pl.ds(SUB - reach, 1), :] = turned[0:1] + float(reach) * slope
        slope = turned[LANES - 1 :] - turned[LANES - 2 : LANES - 1]
        for reach in (1, 2, 3):
            line_ref[pl.ds(SUB + LANES - 1 + reach, 1), :] = turned[LANES - 1 :] + float(reach) * slope
        us = [line_ref[pl.ds(SUB + j, SUB, stride=count), :] for j in range(-3, count + 3)]
        for j, value in enumerate(line_max(us, eps, scale)):
            out_ref[pl.ds(j, SUB, stride=count), :] = value
        acc_ref[pl.ds(base, LANES), :] = out_ref[...].T
        return carry

    lax.fori_loop(0, rows // LANES, group, 0)


def y_kernel(u_ref, low_ref, high_ref, flag_ref, wind_ref, speed_ref, acc_in, acc_ref, *, sizes, eps):
    nx, nh, ny = sizes
    first = flag_ref[0:SUB] > 0.0
    last = flag_ref[SUB : 2 * SUB] > 0.0
    for xg in range(nx // SUB):

        def column(h, carry):
            def rows(y):
                return pl.ds((xg * SUB * nh + h) * ny + y, SUB, stride=nh * ny)

            center = [u_ref[rows(y), :] for y in range(ny)]

            def halo(ref, k):
                return ref[pl.ds(pl.multiple_of((k * nh + h) * nx + xg * SUB, SUB), SUB), :]

            low = [halo(low_ref, k) for k in range(3)]
            high = [halo(high_ref, k) for k in range(3)]
            low, high = edge_fix(low, center[:2], center[-2:], high, (first, last))
            speed = speed_ref[pl.ds(pl.multiple_of(h * SUB, SUB), SUB), :]
            flows = lambda y: speed + wind_ref[pl.ds(y * nx + xg * SUB, SUB), :]
            for y, value in enumerate(line_upwind(low + center + high, eps, flows)):
                acc_ref[rows(y), :] = acc_in[rows(y), :] + value
            return carry

        lax.fori_loop(0, nh, column, 0)


def head_kernel(u_ref, low_ref, high_ref, acc_in, acc_ref, *, sizes, eps, scale):
    nx, nh, ny = sizes

    def line(x, carry):
        for yg in range(ny // SUB):

            def rows(h, height=nh):
                return pl.ds(pl.multiple_of((x * height + h) * ny + yg * SUB, SUB), SUB)

            us = [low_ref[rows(k, 3), :] for k in range(3)]
            us += [u_ref[rows(h), :] for h in range(nh)]
            us += [high_ref[rows(k, 3), :] for k in range(3)]
            for h, value in enumerate(line_max(us, eps, scale)):
                acc_ref[rows(h), :] = acc_in[rows(h), :] + value
        return carry

    lax.fori_loop(0, nx, line, 0)


def x_kernel(*refs, sizes, eps, stage, swap_y):
    nx, nh, ny = sizes
    it = iter(refs)
    u_ref, low_ref, high_ref, flag_ref, wind_ref, speed_ref, acc_in, rate_ref = (next(it) for _ in range(8))
    first_ref = next(it) if stage > 1 else u_ref
    next_ref = next(it)
    first = flag_ref[2 * SUB : 3 * SUB] > 0.0
    last = flag_ref[3 * SUB : 4 * SUB] > 0.0
    step = CFL_NUMBER / rate_ref[...]

    def line(h, carry):
        for yg in range(ny // SUB):

            def rows(x):
                return pl.ds(pl.multiple_of((x * nh + h) * ny + yg * SUB, SUB), SUB)

            center = [u_ref[rows(x), :] for x in range(nx)]
            low = [low_ref[rows(k), :] for k in range(3)]
            high = [high_ref[rows(k), :] for k in range(3)]
            low, high = edge_fix(low, center[:2], center[-2:], high, (first, last))
            speed = speed_ref[pl.ds(pl.multiple_of(h * SUB, SUB), SUB), :]
            flows = lambda x: speed + wind_ref[pl.ds(x * ny + yg * SUB, SUB), :]
            for x, value in enumerate(line_upwind(low + center + high, eps, flows)):
                change = step * jnp.minimum(acc_in[rows(x), :] + value, 0.0)
                if stage == 1:
                    new = center[x] + change
                elif stage == 2:
                    new = 0.75 * first_ref[rows(x), :] + 0.25 * (center[x] + change)
                else:
                    start = first_ref[rows(x), :]
                    new = (2.0 / 3.0) * ((center[x] - start) + change)
                next_ref[rows(x), :] = new
        return carry

    lax.fori_loop(0, nh, line, 0)
    if stage < 3:
        pack_faces(next_ref, list(it), flag_ref, sizes, swap_y)


def pack_faces(u_ref, faces, flag_ref, sizes, swap_y):
    nx, nh, ny = sizes
    plane = nh * ny
    xlo, xhi, hlo, hhi = faces[:4]
    xlo[...] = u_ref[pl.ds(0, 3 * plane), :]
    xhi[...] = u_ref[pl.ds((nx - 3) * plane, 3 * plane), :]
    for x in range(nx):
        hlo[pl.ds(x * 3 * ny, 3 * ny), :] = u_ref[pl.ds(x * plane, 3 * ny), :]
        hhi[pl.ds(x * 3 * ny, 3 * ny), :] = u_ref[pl.ds(x * plane + (nh - 3) * ny, 3 * ny), :]
    first = flag_ref[0:SUB] > 0.0
    for xg in range(nx // SUB):

        def column(h, carry):
            for k in range(3):

                def rows(y):
                    return pl.ds((xg * SUB * nh + h) * ny + y, SUB, stride=plane)

                at = pl.ds(pl.multiple_of((k * nh + h) * nx + xg * SUB, SUB), SUB)
                low = u_ref[rows(k), :]
                high = u_ref[rows(ny - 3 + k), :]
                if swap_y:
                    faces[4][at, :] = jnp.where(first, high, low)
                else:
                    faces[4][at, :] = low
                    faces[5][at, :] = high
            return carry

        lax.fori_loop(0, nh, column, 0)


def pack_kernel(u_ref, flag_ref, *faces, sizes, swap_y):
    pack_faces(u_ref, list(faces), flag_ref, sizes, swap_y)


VM = pl.BlockSpec(memory_space=pltpu.VMEM)


def call(kernel, name, ins, outs, flops, scratch=()):
    shapes = [jax.ShapeDtypeStruct(s, jnp.float32) for s in outs]
    got = pl.pallas_call(
        kernel,
        out_shape=shapes,
        in_specs=[VM] * len(ins),
        out_specs=[VM] * len(outs),
        scratch_shapes=[pltpu.VMEM(s, jnp.float32) for s in scratch],
        name=name,
        cost_estimate=pl.CostEstimate(flops=flops, transcendentals=0, bytes_accessed=1024),
    )(*ins)
    return got


def neighbours(low_face, high_face, axis, closed):
    count = lax.axis_size(axis)
    ends = count if closed else count - 1
    from_low = lax.ppermute(high_face, axis, [(i, (i + 1) % count) for i in range(ends)])
    from_high = lax.ppermute(low_face, axis, [((i + 1) % count, i) for i in range(ends)])
    return from_low, from_high


def all_max(value, axes):
    for axis in axes:
        count = lax.axis_size(axis)
        if count & (count - 1):
            value = lax.pmax(value, axis)
            continue
        reach = 1
        while reach < count:
            value = jnp.maximum(
                value, lax.ppermute(value, axis, [(i, i ^ reach) for i in range(count)])
            )
            reach *= 2
    return value


def body(level_set, wind_field):
    nx, ny, nh, nv = level_set.shape
    sizes = (nx, nh, ny)
    rows = nx * nh * ny
    n_head = nh * lax.axis_size("ha")
    d_theta = 2.0 * math.pi / n_head
    d_speed = SPEED_SPAN / nv
    count_y = lax.axis_size("gy")
    swap_y = count_y == 2

    angles = np.arange(n_head) * d_theta
    cosines, sines = np.cos(angles), np.sin(angles)
    speeds = SPEED_LOW + SPEED_SPAN * (np.arange(nv) + 0.5) / nv

    def edge(axis, at):
        return (lax.axis_index(axis) == at).astype(jnp.float32)

    flags = jnp.stack(
        [edge("gy", 0), edge("gy", count_y - 1), edge("gx", 0), edge("gx", lax.axis_size("gx") - 1)]
    )
    flags = jnp.broadcast_to(flags[:, None, None], (4, SUB, nv)).reshape(4 * SUB, nv)

    ends = np.array([speeds[0], speeds[-1]])
    cos_ends = jnp.asarray((ends[:, None] * cosines).reshape(-1, 1, 1), jnp.float32)
    sin_ends = jnp.asarray((ends[:, None] * sines).reshape(-1, 1, 1), jnp.float32)
    top = jnp.max(
        jnp.abs(cos_ends + wind_field[0]) / CELL_SIZE + jnp.abs(sin_ends + wind_field[1]) / CELL_SIZE
    )
    top = jnp.broadcast_to(top + (TURN_MAX / d_theta + ACCEL_MAX / d_speed), (SUB, nv))

    head = lax.axis_index("ha") * nh

    def flow_rows(table):
        full = jnp.asarray(table[:, None] * speeds / CELL_SIZE, jnp.float32)
        mine = lax.dynamic_slice_in_dim(full, head, nh, 0)
        return jnp.broadcast_to(mine[:, None, :], (nh, SUB, nv)).reshape(nh * SUB, nv)

    speed_x, speed_y = flow_rows(cosines), flow_rows(sines)
    wind = wind_field * (1.0 / CELL_SIZE)
    wind_x = jnp.broadcast_to(wind[0][:, :, None], (nx, ny, nv)).reshape(nx * ny, nv)
    wind_y = jnp.broadcast_to(wind[1].T[:, :, None], (ny, nx, nv)).reshape(ny * nx, nv)

    start = level_set.transpose(0, 2, 1, 3).reshape(rows, nv)
    x_face, h_face, y_face = (3 * nh * ny, nv), (nx * 3 * ny, nv), (3 * nh * nx, nv)
    face_shapes = [x_face, x_face, h_face, h_face] + [y_face] * (1 if swap_y else 2)
    vregs = rows // SUB
    flops = vregs * 40 * SUB * LANES

    eps_g = 0.75 * WENO_EPS * CELL_SIZE**2
    eps_h = 0.75 * WENO_EPS * d_theta**2
    eps_v = 0.75 * WENO_EPS * d_speed**2

    faces = call(
        functools.partial(pack_kernel, sizes=sizes, swap_y=swap_y), "pack", [start, flags], face_shapes, 1000
    )
    rate = all_max(top, ("gy", "gx"))
    u = start
    for stage in (1, 2, 3):
        from_xl, from_xh = neighbours(faces[0], faces[1], "gx", False)
        from_hl, from_hh = neighbours(faces[2], faces[3], "ha", True)
        if swap_y:
            from_yl = from_yh = lax.ppermute(faces[4], "gy", [(0, 1), (1, 0)])
        else:
            from_yl, from_yh = neighbours(faces[4], faces[5], "gy", False)
        (acc,) = call(
            functools.partial(speed_kernel, eps=eps_v, scale=ACCEL_MAX / (6.0 * d_speed)),
            f"speed{stage}",
            [u],
            [(rows, nv)],
            flops,
            [(LANES + 2 * SUB, LANES), (LANES, LANES)],
        )
        (acc,) = call(
            functools.partial(y_kernel, sizes=sizes, eps=eps_g),
            f"y{stage}",
            [u, from_yl, from_yh, flags, wind_y, speed_y, acc],
            [(rows, nv)],
            flops,
        )
        (acc,) = call(
            functools.partial(head_kernel, sizes=sizes, eps=eps_h, scale=TURN_MAX / (6.0 * d_theta)),
            f"head{stage}",
            [u, from_hl, from_hh, acc],
            [(rows, nv)],
            flops,
        )
        ins = [u, from_xl, from_xh, flags, wind_x, speed_x, acc, rate]
        if stage > 1:
            ins.append(start)
        got = call(
            functools.partial(x_kernel, sizes=sizes, eps=eps_g, stage=stage, swap_y=swap_y),
            f"x{stage}",
            ins,
            [(rows, nv)] + (face_shapes if stage < 3 else []),
            flops,
        )
        u, faces = got[0], got[1:]
    return u.reshape(nx, nh, ny, nv).transpose(0, 2, 1, 3)


def solution(mesh):
    return jax.shard_map(
        body,
        mesh=mesh,
        in_specs=(P("gx", "gy", "ha", None), P(None, "gx", "gy")),
        out_specs=P("gx", "gy", "ha", None),
        check_vma=False,
    )
```

time: 162 us -> 114 us (0.70)
  the two profiles are of different devices: /device:TPU:0 before, /device:TPU:4 now
where the time goes in v1:
time: 114 us; the launch traced here: 112 us
  Pallas kernels  54.6 us (48%)
  starting transfers between devices  35.4 us (31%)
  local copies, waits for them, and re-layouts  14.8 us (13%)
  waiting for transfers between devices  5.32 us (5%)
  other arithmetic  1.38 us (1%)
    pallas_call x13, Pallas kernels, call(): pl.pallas_call(kernel, out_shape=shapes, in_specs=[VM] * len(ins), out_sp...  54.6 us
    ppermute x6, starting transfers between devices, neighbours(): lax.ppermute(low_face, axis, [((i + 1) % count, i) for i in range(ends)])  22.9 us
    ppermute x6, starting transfers between devices, neighbours(): lax.ppermute(high_face, axis, [(i, (i + 1) % count) for i in range(ends)])  8.91 us
    unnamed x38, local copies, waits for them, and re-layouts  8.82 us
    ppermute x3, waiting for transfers between devices, all_max(): lax.ppermute(value, axis, [(i, i ^ reach) for i in range(count)])  5.28 us
    ppermute x3, starting transfers between devices, all_max(): lax.ppermute(value, axis, [(i, i ^ reach) for i in range(count)])  3.13 us
  transfers between devices with their start and end apart: 18, of which 1 were waited for; matrix products, arithmetic and copies ran while one was open for 5% of the time, Pallas kernels for 37%

profile of v1, /device:TPU:4, one launch (start us, length us, event | category | flops | bytes accessed | tf_op | source)
XLA Modules:
  0.0 112.3 jit_solution(6025140808518543066)
XLA Ops:
  0.0 0.7 slice_bitcast_fusion.2
  1.4 0.7 multiply_reduce_fusion
  3.7 2.3 %pack.1 = (f32[480,128]{1,0:T(8,128)}, f32[480,128]{1,0:T(8,128)}, f32[384,128]{1,0:T(8,128)}, f32[384,128]{1,0:T(8,128)}, f32[240,128]{1,0:T(8,128)}) custom-call(f32[1280,128]{1,0:T(8,128)} %bitcast.22, f32[32,128]{1,0:T(8,128)} %broadcast_in_dim.42.flag_ref.refs_3_), custom_call_target="tpu_custom_call" | custom-call | flops 1000 | bytes 1024 | tf_op jit(solution)/shard_map/pack/pallas_call | solution.py:249
  6.5 1.6 %collective-permute-start.2 = (f32[384,128]{1,0:T(8,128)}, f32[384,128]{1,0:T(8,128)S(1)}, u32[]{:S(2)}, u32[]{:S(2)}) collective-permute-start(f32[384,128]{1,0:T(8,128)} %get-tuple-element.24), channel_id=1, source_target_pairs={{0,1},{1,2},{2,3},{3,0},{4,5},{5,6},{6,7},{7,4},{8,9},{9,10},{10,1... | collective-permute-start | bytes 589832 | tf_op jit(solution)/shard_map/ppermute | solution.py:264
  8.1 3.4 %collective-permute-start = (f32[480,128]{1,0:T(8,128)}, f32[480,128]{1,0:T(8,128)S(1)}, u32[]{:S(2)}, u32[]{:S(2)}) collective-permute-start(f32[480,128]{1,0:T(8,128)} %get-tuple-element.22), channel_id=1, source_target_pairs={{0,8},{8,16},{16,24},{1,9},{9,17},{17,25},{2,10},{10,18},{18,26},{... | collective-permute-start | bytes 737288 | tf_op jit(solution)/shard_map/ppermute | solution.py:264
  11.5 3.3 %collective-permute-start.1 = (f32[480,128]{1,0:T(8,128)}, f32[480,128]{1,0:T(8,128)S(1)}, u32[]{:S(2)}, u32[]{:S(2)}) collective-permute-start(f32[480,128]{1,0:T(8,128)} %get-tuple-element.23), channel_id=1, source_target_pairs={{8,0},{16,8},{24,16},{9,1},{17,9},{25,17},{10,2},{18,10},{26,18},{... | collective-permute-start | bytes 737288 | tf_op jit(solution)/shard_map/ppermute | solution.py:265
  14.9 0.7 constant_dynamic-slice_fusion
  17.0 5.3 %collective-permute-done.6 = f32[8,128]{1,0:T(8,128)S(1)} collective-permute-done((f32[8,128]{1,0:T(8,128)S(1)}, f32[8,128]{1,0:T(8,128)S(1)}, u32[]{:S(2)}, u32[]{:S(2)}) %collective-permute-start.6) | collective-permute-done | bytes 4128 | tf_op jit(solution)/shard_map/ppermute | solution.py:278
  22.3 2.4 %collective-permute-start.7 = (f32[8,128]{1,0:T(8,128)S(1)}, f32[8,128]{1,0:T(8,128)S(1)}, u32[]{:S(2)}, u32[]{:S(2)}) collective-permute-start(f32[8,128]{1,0:T(8,128)S(1)} %fusion), channel_id=1, source_target_pairs={{0,16},{8,24},{16,0},{24,8},{1,17},{9,25},{17,1},{25,9},{2,18},{10... | collective-permute-start | bytes 12296 | tf_op jit(solution)/shard_map/ppermute | solution.py:278
  24.6 0.7 constant_dynamic-slice_fusion.1
  25.6 5.4 %speed1.1.acc_in = f32[1280,128]{1,0:T(8,128)} custom-call(f32[1280,128]{1,0:T(8,128)} %bitcast.23), custom_call_target="tpu_custom_call" | custom-call | flops 6553600 | bytes 1024 | tf_op jit(solution)/shard_map/speed1/pallas_call | solution.py:249
  31.0 2.3 %collective-permute-start.3 = (f32[384,128]{1,0:T(8,128)S(1)}, f32[384,128]{1,0:T(8,128)S(1)}, u32[]{:S(2)}, u32[]{:S(2)}) collective-permute-start(f32[384,128]{1,0:T(8,128)S(1)} %copy-done.18), channel_id=1, source_target_pairs={{1,0},{2,1},{3,2},{0,3},{5,4},{6,5},{7,6},{4,7},{9,8},{10,9},{11,1... | collective-permute-start | bytes 589832 | tf_op jit(solution)/shard_map/ppermute | solution.py:265
  34.5 0.7 broadcast_in_dim.47.wind_ref
  35.2 4.1 %y1.1.acc_in = f32[1280,128]{1,0:T(8,128)} custom-call(f32[1280,128]{1,0:T(8,128)} %bitcast.24, f32[240,128]{1,0:T(8,128)} %copy-done, f32[240,128]{1,0:T(8,128)} %copy-done, f32[32,128]{1,0:T(8,128)} %broadcast_in_dim.42.flag_ref.refs_3_, f32[128,128]{1,0:T(8,128)} %broadcast_in_dim.47.wind_ref, f32[80,128]{1,0:T(8,128)} %broadcast_bitcast_fusion.speed_ref, ...), custom_call_target="tpu_custom_call" | custom-call | flops 6553600 | bytes 1024 | tf_op jit(solution)/shard_map/y1/pallas_call | solution.py:249
  40.6 3.6 %head1.1.refs_6_ = f32[1280,128]{1,0:T(8,128)} custom-call(f32[1280,128]{1,0:T(8,128)} %bitcast.25, f32[384,128]{1,0:T(8,128)} %copy-done.9, f32[384,128]{1,0:T(8,128)} %copy-done.13, f32[1280,128]{1,0:T(8,128)} %y1.1.acc_in), custom_call_target="tpu_custom_call" | custom-call | flops 6553600 | bytes 1024 | tf_op jit(solution)/shard_map/head1/pallas_call | solution.py:249
  44.2 0.8 broadcast_in_dim.44.refs_4_
  45.0 4.5 %x1.1 = (f32[1280,128]{1,0:T(8,128)}, f32[480,128]{1,0:T(8,128)}, f32[480,128]{1,0:T(8,128)}, f32[384,128]{1,0:T(8,128)}, f32[384,128]{1,0:T(8,128)}, /*index=5*/f32[240,128]{1,0:T(8,128)}) custom-call(f32[1280,128]{1,0:T(8,128)} %bitcast.26, f32[480,128]{1,0:T(8,128)} %copy-done.7, f32[480,128]{1,0:T(8,128)} %copy-done.8, ...), custom_call_target="tpu_custom_call" | custom-call | flops 6553600 | bytes 1024 | tf_op jit(solution)/shard_map/x1/pallas_call | solution.py:249
  49.5 1.9 %collective-permute-start.8 = (f32[480,128]{1,0:T(8,128)}, f32[480,128]{1,0:T(8,128)S(1)}, u32[]{:S(2)}, u32[]{:S(2)}) collective-permute-start(f32[480,128]{1,0:T(8,128)} %get-tuple-element.28), channel_id=1, source_target_pairs={{0,8},{8,16},{16,24},{1,9},{9,17},{17,25},{2,10},{10,18},{18,26},{... | collective-permute-start | bytes 737288 | tf_op jit(solution)/shard_map/ppermute | solution.py:264
  51.4 4.8 %collective-permute-start.9 = (f32[480,128]{1,0:T(8,128)}, f32[480,128]{1,0:T(8,128)S(1)}, u32[]{:S(2)}, u32[]{:S(2)}) collective-permute-start(f32[480,128]{1,0:T(8,128)} %get-tuple-element.29), channel_id=1, source_target_pairs={{8,0},{16,8},{24,16},{9,1},{17,9},{25,17},{10,2},{18,10},{26,18},{... | collective-permute-start | bytes 737288 | tf_op jit(solution)/shard_map/ppermute | solution.py:265
  56.3 3.8 %collective-permute-start.11 = (f32[384,128]{1,0:T(8,128)}, f32[384,128]{1,0:T(8,128)S(1)}, u32[]{:S(2)}, u32[]{:S(2)}) collective-permute-start(f32[384,128]{1,0:T(8,128)} %get-tuple-element.31), channel_id=1, source_target_pairs={{1,0},{2,1},{3,2},{0,3},{5,4},{6,5},{7,6},{4,7},{9,8},{10,9},{11,1... | collective-permute-start | bytes 589832 | tf_op jit(solution)/shard_map/ppermute | solution.py:265
  60.1 5.3 %speed2.1.acc_in = f32[1280,128]{1,0:T(8,128)} custom-call(f32[1280,128]{1,0:T(8,128)} %get-tuple-element.27.u_ref.refs_0_), custom_call_target="tpu_custom_call" | custom-call | flops 6553600 | bytes 1024 | tf_op jit(solution)/shard_map/speed2/pallas_call | solution.py:249
  66.1 4.1 %y2.1.acc_in = f32[1280,128]{1,0:T(8,128)} custom-call(f32[1280,128]{1,0:T(8,128)} %get-tuple-element.27.u_ref.refs_0_, f32[240,128]{1,0:T(8,128)} %copy-done.2, f32[240,128]{1,0:T(8,128)} %copy-done.2, f32[32,128]{1,0:T(8,128)} %broadcast_in_dim.42.flag_ref.refs_3_, f32[128,128]{1,0:T(8,128)} %broadcast_in_dim.47.wind_ref, ...), custom_call_target="tpu_custom_call" | custom-call | flops 6553600 | bytes 1024 | tf_op jit(solution)/shard_map/y2/pallas_call | solution.py:249
  71.5 3.6 %head2.1.refs_6_ = f32[1280,128]{1,0:T(8,128)} custom-call(f32[1280,128]{1,0:T(8,128)} %get-tuple-element.27.u_ref.refs_0_, f32[384,128]{1,0:T(8,128)} %copy-done.11, f32[384,128]{1,0:T(8,128)} %copy-done.14, f32[1280,128]{1,0:T(8,128)} %y2.1.acc_in), custom_call_target="tpu_custom_call" | custom-call | flops 6553600 | bytes 1024 | tf_op jit(solution)/shard_map/head2/pallas_call | solution.py:249
  75.8 0.7 copy-done.5
  76.4 4.8 %x2.1 = (f32[1280,128]{1,0:T(8,128)}, f32[480,128]{1,0:T(8,128)}, f32[480,128]{1,0:T(8,128)}, f32[384,128]{1,0:T(8,128)}, f32[384,128]{1,0:T(8,128)}, /*index=5*/f32[240,128]{1,0:T(8,128)}) custom-call(f32[1280,128]{1,0:T(8,128)} %get-tuple-element.27.u_ref.refs_0_, f32[480,128]{1,0:T(8,128)} %copy-done.3, f32[480,128]{1,0:T(8,128)} %copy-done.5, ...), custom_call_target="tpu_custom_call" | custom-call | flops 6553600 | bytes 1024 | tf_op jit(solution)/shard_map/x2/pallas_call | solution.py:249
  81.2 1.9 %collective-permute-start.13 = (f32[480,128]{1,0:T(8,128)}, f32[480,128]{1,0:T(8,128)S(1)}, u32[]{:S(2)}, u32[]{:S(2)}) collective-permute-start(f32[480,128]{1,0:T(8,128)} %get-tuple-element.34), channel_id=1, source_target_pairs={{0,8},{8,16},{16,24},{1,9},{9,17},{17,25},{2,10},{10,18},{18,26},{... | collective-permute-start | bytes 737288 | tf_op jit(solution)/shard_map/ppermute | solution.py:264
  83.1 4.8 %collective-permute-start.14 = (f32[480,128]{1,0:T(8,128)}, f32[480,128]{1,0:T(8,128)S(1)}, u32[]{:S(2)}, u32[]{:S(2)}) collective-permute-start(f32[480,128]{1,0:T(8,128)} %get-tuple-element.35), channel_id=1, source_target_pairs={{8,0},{16,8},{24,16},{9,1},{17,9},{25,17},{10,2},{18,10},{26,18},{... | collective-permute-start | bytes 737288 | tf_op jit(solution)/shard_map/ppermute | solution.py:265
  88.0 3.8 %collective-permute-start.16 = (f32[384,128]{1,0:T(8,128)}, f32[384,128]{1,0:T(8,128)S(1)}, u32[]{:S(2)}, u32[]{:S(2)}) collective-permute-start(f32[384,128]{1,0:T(8,128)} %get-tuple-element.37), channel_id=1, source_target_pairs={{1,0},{2,1},{3,2},{0,3},{5,4},{6,5},{7,6},{4,7},{9,8},{10,9},{11,1... | collective-permute-start | bytes 589832 | tf_op jit(solution)/shard_map/ppermute | solution.py:265
  91.9 5.3 %speed3.1.acc_in = f32[1280,128]{1,0:T(8,128)} custom-call(f32[1280,128]{1,0:T(8,128)} %get-tuple-element.33.u_ref.refs_0_), custom_call_target="tpu_custom_call" | custom-call | flops 6553600 | bytes 1024 | tf_op jit(solution)/shard_map/speed3/pallas_call | solution.py:249
  97.8 4.0 %y3.1.acc_in = f32[1280,128]{1,0:T(8,128)} custom-call(f32[1280,128]{1,0:T(8,128)} %get-tuple-element.33.u_ref.refs_0_, f32[240,128]{1,0:T(8,128)} %copy-done.1, f32[240,128]{1,0:T(8,128)} %copy-done.1, f32[32,128]{1,0:T(8,128)} %broadcast_in_dim.42.flag_ref.refs_3_, f32[128,128]{1,0:T(8,128)} %broadcast_in_dim.47.wind_ref, ...), custom_call_target="tpu_custom_call" | custom-call | flops 6553600 | bytes 1024 | tf_op jit(solution)/shard_map/y3/pallas_call | solution.py:249
  103.2 3.6 %head3.1.refs_6_ = f32[1280,128]{1,0:T(8,128)} custom-call(f32[1280,128]{1,0:T(8,128)} %get-tuple-element.33.u_ref.refs_0_, f32[384,128]{1,0:T(8,128)} %copy-done.10, f32[384,128]{1,0:T(8,128)} %copy-done.12, f32[1280,128]{1,0:T(8,128)} %y3.1.acc_in), custom_call_target="tpu_custom_call" | custom-call | flops 6553600 | bytes 1024 | tf_op jit(solution)/shard_map/head3/pallas_call | solution.py:249
  108.2 4.1 %x3.1 = f32[1280,128]{1,0:T(8,128)} custom-call(f32[1280,128]{1,0:T(8,128)} %get-tuple-element.33.u_ref.refs_0_, f32[480,128]{1,0:T(8,128)} %copy-done.4, f32[480,128]{1,0:T(8,128)} %copy-done.6, f32[32,128]{1,0:T(8,128)} %broadcast_in_dim.42.flag_ref.refs_3_, f32[128,128]{1,0:T(8,128)} %broadcast_in_dim.44.refs_4_, ...), custom_call_target="tpu_custom_call" | custom-call | flops 6553600 | bytes 1024 | tf_op jit(solution)/shard_map/x3/pallas_call | solution.py:249
  (76 shorter events, 12.5 us)
Async XLA Ops:
  2.7 13.6 %collective-permute-start.5 = (f32[8,128]{1,0:T(8,128)S(1)}, f32[8,128]{1,0:T(8,128)S(1)}, u32[]{:S(2)}, u32[]{:S(2)}) collective-permute-start(f32[8,128]{1,0:T(8,128)S(1)} %broadcast_in_dim.49), channel_id=1, source_target_pairs={{0,4},{4,0},{1,5},{5,1},{2,6},{6,2},{3,7},{7,3},{8,12},{12,8},{9,1... | collective-permute-start | bytes 12296 | tf_op jit(solution)/shard_map/ppermute | solution.py:278
  6.1 28.4 %collective-permute-start.4 = (f32[240,128]{1,0:T(8,128)}, f32[240,128]{1,0:T(8,128)S(1)}, u32[]{:S(2)}, u32[]{:S(2)}) collective-permute-start(f32[240,128]{1,0:T(8,128)} %get-tuple-element.26), channel_id=1, source_target_pairs={{0,4},{4,0},{1,5},{5,1},{2,6},{6,2},{3,7},{7,3},{8,12},{12,8},{9,1... | collective-permute-start | bytes 368648 | tf_op jit(solution)/shard_map/ppermute | solution.py:345
  6.5 32.7 %collective-permute-start.2 = (f32[384,128]{1,0:T(8,128)}, f32[384,128]{1,0:T(8,128)S(1)}, u32[]{:S(2)}, u32[]{:S(2)}) collective-permute-start(f32[384,128]{1,0:T(8,128)} %get-tuple-element.24), channel_id=1, source_target_pairs={{0,1},{1,2},{2,3},{3,0},{4,5},{5,6},{6,7},{7,4},{8,9},{9,10},{10,1... | collective-permute-start | bytes 589832 | tf_op jit(solution)/shard_map/ppermute | solution.py:264
  8.1 36.1 %collective-permute-start = (f32[480,128]{1,0:T(8,128)}, f32[480,128]{1,0:T(8,128)S(1)}, u32[]{:S(2)}, u32[]{:S(2)}) collective-permute-start(f32[480,128]{1,0:T(8,128)} %get-tuple-element.22), channel_id=1, source_target_pairs={{0,8},{8,16},{16,24},{1,9},{9,17},{17,25},{2,10},{10,18},{18,26},{... | collective-permute-start | bytes 737288 | tf_op jit(solution)/shard_map/ppermute | solution.py:264
  11.5 32.7 %collective-permute-start.1 = (f32[480,128]{1,0:T(8,128)}, f32[480,128]{1,0:T(8,128)S(1)}, u32[]{:S(2)}, u32[]{:S(2)}) collective-permute-start(f32[480,128]{1,0:T(8,128)} %get-tuple-element.23), channel_id=1, source_target_pairs={{8,0},{16,8},{24,16},{9,1},{17,9},{25,17},{10,2},{18,10},{26,18},{... | collective-permute-start | bytes 737288 | tf_op jit(solution)/shard_map/ppermute | solution.py:265
  15.6 0.7 copy-start.15
  16.3 5.9 %collective-permute-start.6 = (f32[8,128]{1,0:T(8,128)S(1)}, f32[8,128]{1,0:T(8,128)S(1)}, u32[]{:S(2)}, u32[]{:S(2)}) collective-permute-start(f32[8,128]{1,0:T(8,128)S(1)} %broadcast_maximum_fusion), channel_id=1, source_target_pairs={{0,8},{8,0},{16,24},{24,16},{1,9},{9,1},{17,25},{25,17},{2,10},{10... | collective-permute-start | bytes 12296 | tf_op jit(solution)/shard_map/ppermute | solution.py:278
  22.3 8.7 %collective-permute-start.7 = (f32[8,128]{1,0:T(8,128)S(1)}, f32[8,128]{1,0:T(8,128)S(1)}, u32[]{:S(2)}, u32[]{:S(2)}) collective-permute-start(f32[8,128]{1,0:T(8,128)S(1)} %fusion), channel_id=1, source_target_pairs={{0,16},{8,24},{16,0},{24,8},{1,17},{9,25},{17,1},{25,9},{2,18},{10... | collective-permute-start | bytes 12296 | tf_op jit(solution)/shard_map/ppermute | solution.py:278
  25.6 5.4 %copy-start.18 = (f32[384,128]{1,0:T(8,128)S(1)}, f32[384,128]{1,0:T(8,128)}, u32[]{:S(2)}) copy-start(f32[384,128]{1,0:T(8,128)} %get-tuple-element.25) | copy-start | bytes 589828
  31.0 8.3 %collective-permute-start.3 = (f32[384,128]{1,0:T(8,128)S(1)}, f32[384,128]{1,0:T(8,128)S(1)}, u32[]{:S(2)}, u32[]{:S(2)}) collective-permute-start(f32[384,128]{1,0:T(8,128)S(1)} %copy-done.18), channel_id=1, source_target_pairs={{1,0},{2,1},{3,2},{0,3},{5,4},{6,5},{7,6},{4,7},{9,8},{10,9},{11,1... | collective-permute-start | bytes 589832 | tf_op jit(solution)/shard_map/ppermute | solution.py:265
  34.5 0.7 copy-start
  39.9 0.7 copy-start.13
  44.2 0.8 copy-start.7
  44.2 0.8 copy-start.8
  49.5 25.6 %collective-permute-start.8 = (f32[480,128]{1,0:T(8,128)}, f32[480,128]{1,0:T(8,128)S(1)}, u32[]{:S(2)}, u32[]{:S(2)}) collective-permute-start(f32[480,128]{1,0:T(8,128)} %get-tuple-element.28), channel_id=1, source_target_pairs={{0,8},{8,16},{16,24},{1,9},{9,17},{17,25},{2,10},{10,18},{18,26},{... | collective-permute-start | bytes 737288 | tf_op jit(solution)/shard_map/ppermute | solution.py:264
  51.4 23.7 %collective-permute-start.9 = (f32[480,128]{1,0:T(8,128)}, f32[480,128]{1,0:T(8,128)S(1)}, u32[]{:S(2)}, u32[]{:S(2)}) collective-permute-start(f32[480,128]{1,0:T(8,128)} %get-tuple-element.29), channel_id=1, source_target_pairs={{8,0},{16,8},{24,16},{9,1},{17,9},{25,17},{10,2},{18,10},{26,18},{... | collective-permute-start | bytes 737288 | tf_op jit(solution)/shard_map/ppermute | solution.py:265
  56.2 13.9 %collective-permute-start.10 = (f32[384,128]{1,0:T(8,128)}, f32[384,128]{1,0:T(8,128)S(1)}, u32[]{:S(2)}, u32[]{:S(2)}) collective-permute-start(f32[384,128]{1,0:T(8,128)} %get-tuple-element.30), channel_id=1, source_target_pairs={{0,1},{1,2},{2,3},{3,0},{4,5},{5,6},{6,7},{7,4},{8,9},{9,10},{10,1... | collective-permute-start | bytes 589832 | tf_op jit(solution)/shard_map/ppermute | solution.py:264
  56.3 13.9 %collective-permute-start.11 = (f32[384,128]{1,0:T(8,128)}, f32[384,128]{1,0:T(8,128)S(1)}, u32[]{:S(2)}, u32[]{:S(2)}) collective-permute-start(f32[384,128]{1,0:T(8,128)} %get-tuple-element.31), channel_id=1, source_target_pairs={{1,0},{2,1},{3,2},{0,3},{5,4},{6,5},{7,6},{4,7},{9,8},{10,9},{11,1... | collective-permute-start | bytes 589832 | tf_op jit(solution)/shard_map/ppermute | solution.py:265
  60.1 5.3 %collective-permute-start.12 = (f32[240,128]{1,0:T(8,128)}, f32[240,128]{1,0:T(8,128)S(1)}, u32[]{:S(2)}, u32[]{:S(2)}) collective-permute-start(f32[240,128]{1,0:T(8,128)} %get-tuple-element.32), channel_id=1, source_target_pairs={{0,4},{4,0},{1,5},{5,1},{2,6},{6,2},{3,7},{7,3},{8,12},{12,8},{9,1... | collective-permute-start | bytes 368648 | tf_op jit(solution)/shard_map/ppermute | solution.py:345
  70.1 0.7 copy-start.11
  70.8 0.7 copy-start.14
  75.1 0.7 copy-start.3
  75.7 0.7 copy-start.5
  81.2 25.6 %collective-permute-start.13 = (f32[480,128]{1,0:T(8,128)}, f32[480,128]{1,0:T(8,128)S(1)}, u32[]{:S(2)}, u32[]{:S(2)}) collective-permute-start(f32[480,128]{1,0:T(8,128)} %get-tuple-element.34), channel_id=1, source_target_pairs={{0,8},{8,16},{16,24},{1,9},{9,17},{17,25},{2,10},{10,18},{18,26},{... | collective-permute-start | bytes 737288 | tf_op jit(solution)/shard_map/ppermute | solution.py:264
  83.1 23.7 %collective-permute-start.14 = (f32[480,128]{1,0:T(8,128)}, f32[480,128]{1,0:T(8,128)S(1)}, u32[]{:S(2)}, u32[]{:S(2)}) collective-permute-start(f32[480,128]{1,0:T(8,128)} %get-tuple-element.35), channel_id=1, source_target_pairs={{8,0},{16,8},{24,16},{9,1},{17,9},{25,17},{10,2},{18,10},{26,18},{... | collective-permute-start | bytes 737288 | tf_op jit(solution)/shard_map/ppermute | solution.py:265
  88.0 13.9 %collective-permute-start.15 = (f32[384,128]{1,0:T(8,128)}, f32[384,128]{1,0:T(8,128)S(1)}, u32[]{:S(2)}, u32[]{:S(2)}) collective-permute-start(f32[384,128]{1,0:T(8,128)} %get-tuple-element.36), channel_id=1, source_target_pairs={{0,1},{1,2},{2,3},{3,0},{4,5},{5,6},{6,7},{7,4},{8,9},{9,10},{10,1... | collective-permute-start | bytes 589832 | tf_op jit(solution)/shard_map/ppermute | solution.py:264
  88.0 13.8 %collective-permute-start.16 = (f32[384,128]{1,0:T(8,128)}, f32[384,128]{1,0:T(8,128)S(1)}, u32[]{:S(2)}, u32[]{:S(2)}) collective-permute-start(f32[384,128]{1,0:T(8,128)} %get-tuple-element.37), channel_id=1, source_target_pairs={{1,0},{2,1},{3,2},{0,3},{5,4},{6,5},{7,6},{4,7},{9,8},{10,9},{11,1... | collective-permute-start | bytes 589832 | tf_op jit(solution)/shard_map/ppermute | solution.py:265
  91.8 5.3 %collective-permute-start.17 = (f32[240,128]{1,0:T(8,128)}, f32[240,128]{1,0:T(8,128)S(1)}, u32[]{:S(2)}, u32[]{:S(2)}) collective-permute-start(f32[240,128]{1,0:T(8,128)} %get-tuple-element.38), channel_id=1, source_target_pairs={{0,4},{4,0},{1,5},{5,1},{2,6},{6,2},{3,7},{7,3},{8,12},{12,8},{9,1... | collective-permute-start | bytes 368648 | tf_op jit(solution)/shard_map/ppermute | solution.py:345
  101.9 0.7 copy-start.10
  102.6 0.7 copy-start.12
  106.8 0.7 copy-start.4
  107.5 0.7 copy-start.6
  (5 other events, 3.3 us)

commit v2 on v1

--- a/solution.py
+++ b/solution.py
@@ -241,11 +241,13 @@
     pack_faces(u_ref, list(faces), flag_ref, sizes, swap_y)
 
 
+VMEM_LIMIT = 8 * 1024 * 1024
 VM = pl.BlockSpec(memory_space=pltpu.VMEM)
 
 
-def call(kernel, name, ins, outs, flops, scratch=()):
-    shapes = [jax.ShapeDtypeStruct(s, jnp.float32) for s in outs]
+def call(kernel, name, ins, outs, flops, scratch=(), keep=True):
+    shapes = [pltpu.VMEM(s, jnp.float32) if keep else jax.ShapeDtypeStruct(s, jnp.float32) for s in outs]
+    ins = [pltpu.with_memory_space_constraint(x, pltpu.VMEM) for x in ins]
     got = pl.pallas_call(
         kernel,
         out_shape=shapes,
@@ -253,6 +255,7 @@
         out_specs=[VM] * len(outs),
         scratch_shapes=[pltpu.VMEM(s, jnp.float32) for s in scratch],
         name=name,
+        compiler_params=pltpu.CompilerParams(vmem_limit_bytes=VMEM_LIMIT),
         cost_estimate=pl.CostEstimate(flops=flops, transcendentals=0, bytes_accessed=1024),
     )(*ins)
     return got
@@ -376,6 +379,7 @@
             ins,
             [(rows, nv)] + (face_shapes if stage < 3 else []),
             flops,
+            keep=stage < 3,
         )
         u, faces = got[0], got[1:]
     return u.reshape(nx, nh, ny, nv).transpose(0, 2, 1, 3)

time: 114 us -> 77.6 us (0.68)
  Pallas kernels: 54.6 us -> 25.6 us
  local copies, waits for them, and re-layouts: 14.8 us -> 5.22 us
  waiting for transfers between devices: 5.32 us -> 8.51 us
    pallas_call x13, Pallas kernels: 54.6 us -> 25.6 us  [call(): pl.pallas_call(kernel, out_shape=shapes, in_specs=[VM] * len(ins), out_sp...]
    unnamed x38 -> x10, local copies, waits for them, and re-layouts: 8.82 us -> 2.46 us
    ppermute x6, starting transfers between devices: 8.91 us -> 12.1 us  [neighbours(): lax.ppermute(high_face, axis, [(i, (i + 1) % count) for i in range(ends)])]
    ppermute x6, waiting for transfers between devices: 0.02 us -> 2.91 us  [neighbours(): lax.ppermute(low_face, axis, [((i + 1) % count, i) for i in range(ends)])]
    ppermute x6, starting transfers between devices: 22.9 us -> 20.2 us  [neighbours(): lax.ppermute(low_face, axis, [((i + 1) % count, i) for i in range(ends)])]
    reshape x2, local copies, waits for them, and re-layouts: 1.24 us -> 0.01 us  [flow_rows(): jnp.broadcast_to(mine[:, None, :], (nh, SUB, nv)).reshape(nh * SUB, nv)]
  transfers between devices with their start and end apart: 18 -> 18, of which waited for: 1 -> 4; matrix products, arithmetic and copies ran while one was open for 5% -> 3% of each run, Pallas kernels for 37% -> 26%
where the time goes in v2:
time: 77.6 us; the launch traced here: 77 us
  starting transfers between devices  36 us (46%)
  Pallas kernels  25.6 us (33%)
  waiting for transfers between devices  8.51 us (11%)
  local copies, waits for them, and re-layouts  5.22 us (7%)
  between operations  0.93 us (1%)
  other arithmetic  0.79 us (1%)
    pallas_call x13, Pallas kernels, call(): pl.pallas_call(kernel, out_shape=shapes, in_specs=[VM] * len(ins), out_sp...  25.6 us
    ppermute x6, starting transfers between devices, neighbours(): lax.ppermute(low_face, axis, [((i + 1) % count, i) for i in range(ends)])  20.2 us
    ppermute x6, starting transfers between devices, neighbours(): lax.ppermute(high_face, axis, [(i, (i + 1) % count) for i in range(ends)])  12.1 us
    ppermute x3, waiting for transfers between devices, all_max(): lax.ppermute(value, axis, [(i, i ^ reach) for i in range(count)])  5.04 us
    ppermute x3, starting transfers between devices, all_max(): lax.ppermute(value, axis, [(i, i ^ reach) for i in range(count)])  3.19 us
    ppermute x6, waiting for transfers between devices, neighbours(): lax.ppermute(low_face, axis, [((i + 1) % count, i) for i in range(ends)])  2.91 us
    unnamed x10, local copies, waits for them, and re-layouts  2.46 us
  transfers between devices with their start and end apart: 18, of which 4 were waited for; matrix products, arithmetic and copies ran while one was open for 3% of the time, Pallas kernels for 26%

profile of v2, /device:TPU:4, one launch (start us, length us, event | category | flops | bytes accessed | tf_op | source)
XLA Modules:
  0.0 77.0 jit_solution(16492042721601958014)
XLA Ops:
  0.0 0.7 slice_bitcast_fusion.2
  3.1 1.1 %copy-done = f32[8,16,10,128]{3,1,2,0:T(8,128)S(1)} copy-done((f32[8,16,10,128]{3,1,2,0:T(8,128)S(1)}, f32[8,16,10,128]{3,1,2,0:T(8,128)}, u32[]{:S(2)}) %copy-start) | copy-done | bytes 655384
  5.1 1.6 %collective-permute-start.2 = (f32[384,128]{1,0:T(8,128)S(1)}, f32[384,128]{1,0:T(8,128)S(1)}, u32[]{:S(2)}, u32[]{:S(2)}) collective-permute-start(f32[384,128]{1,0:T(8,128)S(1)} %get-tuple-element.24), channel_id=1, source_target_pairs={{0,1},{1,2},{2,3},{3,0},{4,5},{5,6},{6,7},{7,4},{8,9},{9,10},{10,1... | collective-permute-start | bytes 589832 | tf_op jit(solution)/shard_map/ppermute | solution.py:267
  6.6 3.4 %collective-permute-start = (f32[480,128]{1,0:T(8,128)S(1)}, f32[480,128]{1,0:T(8,128)S(1)}, u32[]{:S(2)}, u32[]{:S(2)}) collective-permute-start(f32[480,128]{1,0:T(8,128)S(1)} %get-tuple-element.22), channel_id=1, source_target_pairs={{0,8},{8,16},{16,24},{1,9},{9,17},{17,25},{2,10},{10,18},{18,26},{... | collective-permute-start | bytes 737288 | tf_op jit(solution)/shard_map/ppermute | solution.py:267
  10.0 3.3 %collective-permute-start.1 = (f32[480,128]{1,0:T(8,128)S(1)}, f32[480,128]{1,0:T(8,128)S(1)}, u32[]{:S(2)}, u32[]{:S(2)}) collective-permute-start(f32[480,128]{1,0:T(8,128)S(1)} %get-tuple-element.23), channel_id=1, source_target_pairs={{8,0},{16,8},{24,16},{9,1},{17,9},{25,17},{10,2},{18,10},{26,18},{... | collective-permute-start | bytes 737288 | tf_op jit(solution)/shard_map/ppermute | solution.py:268
  13.4 0.7 constant_dynamic-slice_fusion
  15.5 5.0 %collective-permute-done.6 = f32[8,128]{1,0:T(8,128)S(1)} collective-permute-done((f32[8,128]{1,0:T(8,128)S(1)}, f32[8,128]{1,0:T(8,128)S(1)}, u32[]{:S(2)}, u32[]{:S(2)}) %collective-permute-start.6) | collective-permute-done | bytes 4128 | tf_op jit(solution)/shard_map/ppermute | solution.py:281
  20.5 2.5 %collective-permute-start.7 = (f32[8,128]{1,0:T(8,128)S(1)}, f32[8,128]{1,0:T(8,128)S(1)}, u32[]{:S(2)}, u32[]{:S(2)}) collective-permute-start(f32[8,128]{1,0:T(8,128)S(1)} %fusion), channel_id=1, source_target_pairs={{0,16},{8,24},{16,0},{24,8},{1,17},{9,25},{17,1},{25,9},{2,18},{10... | collective-permute-start | bytes 12296 | tf_op jit(solution)/shard_map/ppermute | solution.py:281
  23.0 0.7 constant_dynamic-slice_fusion.1
  23.9 3.4 %speed1.1.acc_in = f32[1280,128]{1,0:T(8,128)S(1)} custom-call(f32[1280,128]{1,0:T(8,128)S(1)} %bitcast.23), custom_call_target="tpu_custom_call" | custom-call | flops 6553600 | bytes 1024 | tf_op jit(solution)/shard_map/speed1/pallas_call | solution.py:251
  27.4 2.4 %collective-permute-start.3 = (f32[384,128]{1,0:T(8,128)S(1)}, f32[384,128]{1,0:T(8,128)S(1)}, u32[]{:S(2)}, u32[]{:S(2)}) collective-permute-start(f32[384,128]{1,0:T(8,128)S(1)} %get-tuple-element.25), channel_id=1, source_target_pairs={{1,0},{2,1},{3,2},{0,3},{5,4},{6,5},{7,6},{4,7},{9,8},{10,9},{11,1... | collective-permute-start | bytes 589832 | tf_op jit(solution)/shard_map/ppermute | solution.py:268
  29.8 1.8 %y1.1.acc_in = f32[1280,128]{1,0:T(8,128)S(1)} custom-call(f32[1280,128]{1,0:T(8,128)S(1)} %bitcast.24, f32[240,128]{1,0:T(8,128)S(1)} %collective-permute-done.4.low_ref.high_ref, f32[240,128]{1,0:T(8,128)S(1)} %collective-permute-done.4.low_ref.high_ref, f32[32,128]{1,0:T(8,128)S(1)} %broadcast_in_dim.42.flag_ref.refs_3_, ...), custom_call_target="tpu_custom_call" | custom-call | flops 6553600 | bytes 1024 | tf_op jit(solution)/shard_map/y1/pallas_call | solution.py:251
  31.6 1.4 %collective-permute-done.3.high_ref = f32[384,128]{1,0:T(8,128)S(1)} collective-permute-done((f32[384,128]{1,0:T(8,128)S(1)}, f32[384,128]{1,0:T(8,128)S(1)}, u32[]{:S(2)}, u32[]{:S(2)}) %collective-permute-start.3) | collective-permute-done | bytes 196640 | tf_op jit(solution)/shard_map/ppermute | solution.py:268
  33.1 1.3 %head1.1.refs_6_ = f32[1280,128]{1,0:T(8,128)S(1)} custom-call(f32[1280,128]{1,0:T(8,128)S(1)} %bitcast.25, f32[384,128]{1,0:T(8,128)S(1)} %collective-permute-done.2.low_ref, f32[384,128]{1,0:T(8,128)S(1)} %collective-permute-done.3.high_ref, f32[1280,128]{1,0:T(8,128)S(1)} %y1.1.acc_in), custom_call_target="tpu_custom_call" | custom-call | flops 6553600 | bytes 1024 | tf_op jit(solution)/shard_map/head1/pallas_call | solution.py:251
  34.5 1.7 %x1.1 = (f32[1280,128]{1,0:T(8,128)S(1)}, f32[480,128]{1,0:T(8,128)S(1)}, f32[480,128]{1,0:T(8,128)S(1)}, f32[384,128]{1,0:T(8,128)S(1)}, f32[384,128]{1,0:T(8,128)S(1)}, /*index=5*/f32[240,128]{1,0:T(8,128)S(1)}) custom-call(f32[1280,128]{1,0:T(8,128)S(1)} %bitcast.26, f32[480,128]{1,0:T(8,128)S(1)} %collective-permute-done.refs_1_, ...), custom_call_target="tpu_custom_call" | custom-call | flops 6553600 | bytes 1024 | tf_op jit(solution)/shard_map/x1/pallas_call | solution.py:251
  36.2 1.9 %collective-permute-start.8 = (f32[480,128]{1,0:T(8,128)S(1)}, f32[480,128]{1,0:T(8,128)S(1)}, u32[]{:S(2)}, u32[]{:S(2)}) collective-permute-start(f32[480,128]{1,0:T(8,128)S(1)} %get-tuple-element.28), channel_id=1, source_target_pairs={{0,8},{8,16},{16,24},{1,9},{9,17},{17,25},{2,10},{10,18},{18,26},{... | collective-permute-start | bytes 737288 | tf_op jit(solution)/shard_map/ppermute | solution.py:267
  38.1 4.8 %collective-permute-start.9 = (f32[480,128]{1,0:T(8,128)S(1)}, f32[480,128]{1,0:T(8,128)S(1)}, u32[]{:S(2)}, u32[]{:S(2)}) collective-permute-start(f32[480,128]{1,0:T(8,128)S(1)} %get-tuple-element.29), channel_id=1, source_target_pairs={{8,0},{16,8},{24,16},{9,1},{17,9},{25,17},{10,2},{18,10},{26,18},{... | collective-permute-start | bytes 737288 | tf_op jit(solution)/shard_map/ppermute | solution.py:268
  43.0 1.6 %collective-permute-start.10 = (f32[384,128]{1,0:T(8,128)S(1)}, f32[384,128]{1,0:T(8,128)S(1)}, u32[]{:S(2)}, u32[]{:S(2)}) collective-permute-start(f32[384,128]{1,0:T(8,128)S(1)} %get-tuple-element.30), channel_id=1, source_target_pairs={{0,1},{1,2},{2,3},{3,0},{4,5},{5,6},{6,7},{7,4},{8,9},{9,10},{10,1... | collective-permute-start | bytes 589832 | tf_op jit(solution)/shard_map/ppermute | solution.py:267
  44.6 2.6 %collective-permute-start.11 = (f32[384,128]{1,0:T(8,128)S(1)}, f32[384,128]{1,0:T(8,128)S(1)}, u32[]{:S(2)}, u32[]{:S(2)}) collective-permute-start(f32[384,128]{1,0:T(8,128)S(1)} %get-tuple-element.31), channel_id=1, source_target_pairs={{1,0},{2,1},{3,2},{0,3},{5,4},{6,5},{7,6},{4,7},{9,8},{10,9},{11,1... | collective-permute-start | bytes 589832 | tf_op jit(solution)/shard_map/ppermute | solution.py:268
  47.2 3.4 %speed2.1.acc_in = f32[1280,128]{1,0:T(8,128)S(1)} custom-call(f32[1280,128]{1,0:T(8,128)S(1)} %get-tuple-element.27.u_ref.refs_0_), custom_call_target="tpu_custom_call" | custom-call | flops 6553600 | bytes 1024 | tf_op jit(solution)/shard_map/speed2/pallas_call | solution.py:251
  50.6 1.8 %y2.1.acc_in = f32[1280,128]{1,0:T(8,128)S(1)} custom-call(f32[1280,128]{1,0:T(8,128)S(1)} %get-tuple-element.27.u_ref.refs_0_, f32[240,128]{1,0:T(8,128)S(1)} %collective-permute-done.12.low_ref.high_ref, f32[240,128]{1,0:T(8,128)S(1)} %collective-permute-done.12.low_ref.high_ref, f32[32,128]{1,0:T(8,128)S(1)} %broadcast_in_dim.42.flag_ref.refs_3_, ...), custom_call_target="tpu_custom_call" | custom-call | flops 6553600 | bytes 1024 | tf_op jit(solution)/shard_map/y2/pallas_call | solution.py:251
  52.4 1.3 %head2.1.refs_6_ = f32[1280,128]{1,0:T(8,128)S(1)} custom-call(f32[1280,128]{1,0:T(8,128)S(1)} %get-tuple-element.27.u_ref.refs_0_, f32[384,128]{1,0:T(8,128)S(1)} %collective-permute-done.10.low_ref, f32[384,128]{1,0:T(8,128)S(1)} %collective-permute-done.11.high_ref, f32[1280,128]{1,0:T(8,128)S(1)} %y2.1.acc_in), custom_call_target="tpu_custom_call" | custom-call | flops 6553600 | bytes 1024 | tf_op jit(solution)/shard_map/head2/pallas_call | solution.py:251
  53.7 1.8 %x2.1 = (f32[1280,128]{1,0:T(8,128)S(1)}, f32[480,128]{1,0:T(8,128)S(1)}, f32[480,128]{1,0:T(8,128)S(1)}, f32[384,128]{1,0:T(8,128)S(1)}, f32[384,128]{1,0:T(8,128)S(1)}, /*index=5*/f32[240,128]{1,0:T(8,128)S(1)}) custom-call(f32[1280,128]{1,0:T(8,128)S(1)} %get-tuple-element.27.u_ref.refs_0_, f32[480,128]{1,0:T(8,128)S(1)} %collective-permute-done.8.refs_1_, ...), custom_call_target="tpu_custom_call" | custom-call | flops 6553600 | bytes 1024 | tf_op jit(solution)/shard_map/x2/pallas_call | solution.py:251
  55.5 1.9 %collective-permute-start.13 = (f32[480,128]{1,0:T(8,128)S(1)}, f32[480,128]{1,0:T(8,128)S(1)}, u32[]{:S(2)}, u32[]{:S(2)}) collective-permute-start(f32[480,128]{1,0:T(8,128)S(1)} %get-tuple-element.34), channel_id=1, source_target_pairs={{0,8},{8,16},{16,24},{1,9},{9,17},{17,25},{2,10},{10,18},{18,26},{... | collective-permute-start | bytes 737288 | tf_op jit(solution)/shard_map/ppermute | solution.py:267
  57.5 4.8 %collective-permute-start.14 = (f32[480,128]{1,0:T(8,128)S(1)}, f32[480,128]{1,0:T(8,128)S(1)}, u32[]{:S(2)}, u32[]{:S(2)}) collective-permute-start(f32[480,128]{1,0:T(8,128)S(1)} %get-tuple-element.35), channel_id=1, source_target_pairs={{8,0},{16,8},{24,16},{9,1},{17,9},{25,17},{10,2},{18,10},{26,18},{... | collective-permute-start | bytes 737288 | tf_op jit(solution)/shard_map/ppermute | solution.py:268
  62.3 1.6 %collective-permute-start.15 = (f32[384,128]{1,0:T(8,128)S(1)}, f32[384,128]{1,0:T(8,128)S(1)}, u32[]{:S(2)}, u32[]{:S(2)}) collective-permute-start(f32[384,128]{1,0:T(8,128)S(1)} %get-tuple-element.36), channel_id=1, source_target_pairs={{0,1},{1,2},{2,3},{3,0},{4,5},{5,6},{6,7},{7,4},{8,9},{9,10},{10,1... | collective-permute-start | bytes 589832 | tf_op jit(solution)/shard_map/ppermute | solution.py:267
  63.9 2.3 %collective-permute-start.16 = (f32[384,128]{1,0:T(8,128)S(1)}, f32[384,128]{1,0:T(8,128)S(1)}, u32[]{:S(2)}, u32[]{:S(2)}) collective-permute-start(f32[384,128]{1,0:T(8,128)S(1)} %get-tuple-element.37), channel_id=1, source_target_pairs={{1,0},{2,1},{3,2},{0,3},{5,4},{6,5},{7,6},{4,7},{9,8},{10,9},{11,1... | collective-permute-start | bytes 589832 | tf_op jit(solution)/shard_map/ppermute | solution.py:268
  66.2 3.4 %speed3.1.acc_in = f32[1280,128]{1,0:T(8,128)S(1)} custom-call(f32[1280,128]{1,0:T(8,128)S(1)} %get-tuple-element.33.u_ref.refs_0_), custom_call_target="tpu_custom_call" | custom-call | flops 6553600 | bytes 1024 | tf_op jit(solution)/shard_map/speed3/pallas_call | solution.py:251
  69.6 1.8 %y3.1.acc_in = f32[1280,128]{1,0:T(8,128)S(1)} custom-call(f32[1280,128]{1,0:T(8,128)S(1)} %get-tuple-element.33.u_ref.refs_0_, f32[240,128]{1,0:T(8,128)S(1)} %collective-permute-done.17.low_ref.high_ref, f32[240,128]{1,0:T(8,128)S(1)} %collective-permute-done.17.low_ref.high_ref, f32[32,128]{1,0:T(8,128)S(1)} %broadcast_in_dim.42.flag_ref.refs_3_, ...), custom_call_target="tpu_custom_call" | custom-call | flops 6553600 | bytes 1024 | tf_op jit(solution)/shard_map/y3/pallas_call | solution.py:251
  71.9 1.5 %collective-permute-done.16.high_ref = f32[384,128]{1,0:T(8,128)S(1)} collective-permute-done((f32[384,128]{1,0:T(8,128)S(1)}, f32[384,128]{1,0:T(8,128)S(1)}, u32[]{:S(2)}, u32[]{:S(2)}) %collective-permute-start.16) | collective-permute-done | bytes 196640 | tf_op jit(solution)/shard_map/ppermute | solution.py:268
  73.4 1.3 %head3.1.refs_6_ = f32[1280,128]{1,0:T(8,128)S(1)} custom-call(f32[1280,128]{1,0:T(8,128)S(1)} %get-tuple-element.33.u_ref.refs_0_, f32[384,128]{1,0:T(8,128)S(1)} %collective-permute-done.15.low_ref, f32[384,128]{1,0:T(8,128)S(1)} %collective-permute-done.16.high_ref, f32[1280,128]{1,0:T(8,128)S(1)} %y3.1.acc_in), custom_call_target="tpu_custom_call" | custom-call | flops 6553600 | bytes 1024 | tf_op jit(solution)/shard_map/head3/pallas_call | solution.py:251
  74.7 2.4 %x3.1 = f32[1280,128]{1,0:T(8,128)} custom-call(f32[1280,128]{1,0:T(8,128)S(1)} %get-tuple-element.33.u_ref.refs_0_, f32[480,128]{1,0:T(8,128)S(1)} %collective-permute-done.13.refs_1_, f32[480,128]{1,0:T(8,128)S(1)} %collective-permute-done.14.refs_2_, f32[32,128]{1,0:T(8,128)S(1)} %broadcast_in_dim.42.flag_ref.refs_3_, ...), custom_call_target="tpu_custom_call" | custom-call | flops 6553600 | bytes 1024 | tf_op jit(solution)/shard_map/x3/pallas_call | solution.py:251
  (48 shorter events, 4.9 us)
Async XLA Ops:
  0.7 0.7 copy-start.3
  0.7 0.7 copy-start.4
  2.7 12.1 %collective-permute-start.5 = (f32[8,128]{1,0:T(8,128)S(1)}, f32[8,128]{1,0:T(8,128)S(1)}, u32[]{:S(2)}, u32[]{:S(2)}) collective-permute-start(f32[8,128]{1,0:T(8,128)S(1)} %broadcast_in_dim.49), channel_id=1, source_target_pairs={{0,4},{4,0},{1,5},{5,1},{2,6},{6,2},{3,7},{7,3},{8,12},{12,8},{9,1... | collective-permute-start | bytes 12296 | tf_op jit(solution)/shard_map/ppermute | solution.py:281
  3.1 1.1 %copy-start = (f32[8,16,10,128]{3,1,2,0:T(8,128)S(1)}, f32[8,16,10,128]{3,1,2,0:T(8,128)}, u32[]{:S(2)}) copy-start(f32[8,16,10,128]{3,1,2,0:T(8,128)} %param.6) | copy-start | bytes 1966084
  4.2 19.7 %copy-start.1 = (f32[8,16,10,128]{3,1,2,0:T(8,128)S(1)}, f32[8,16,10,128]{3,1,2,0:T(8,128)}, u32[]{:S(2)}) copy-start(f32[8,16,10,128]{3,1,2,0:T(8,128)} %param.6) | copy-start | bytes 1966084
  4.5 25.3 %collective-permute-start.4 = (f32[240,128]{1,0:T(8,128)S(1)}, f32[240,128]{1,0:T(8,128)S(1)}, u32[]{:S(2)}, u32[]{:S(2)}) collective-permute-start(f32[240,128]{1,0:T(8,128)S(1)} %get-tuple-element.26), channel_id=1, source_target_pairs={{0,4},{4,0},{1,5},{5,1},{2,6},{6,2},{3,7},{7,3},{8,12},{12,8},{9,1... | collective-permute-start | bytes 368648 | tf_op jit(solution)/shard_map/ppermute | solution.py:348
  5.1 26.6 %collective-permute-start.2 = (f32[384,128]{1,0:T(8,128)S(1)}, f32[384,128]{1,0:T(8,128)S(1)}, u32[]{:S(2)}, u32[]{:S(2)}) collective-permute-start(f32[384,128]{1,0:T(8,128)S(1)} %get-tuple-element.24), channel_id=1, source_target_pairs={{0,1},{1,2},{2,3},{3,0},{4,5},{5,6},{6,7},{7,4},{8,9},{9,10},{10,1... | collective-permute-start | bytes 589832 | tf_op jit(solution)/shard_map/ppermute | solution.py:267
  6.6 27.7 %collective-permute-start = (f32[480,128]{1,0:T(8,128)S(1)}, f32[480,128]{1,0:T(8,128)S(1)}, u32[]{:S(2)}, u32[]{:S(2)}) collective-permute-start(f32[480,128]{1,0:T(8,128)S(1)} %get-tuple-element.22), channel_id=1, source_target_pairs={{0,8},{8,16},{16,24},{1,9},{9,17},{17,25},{2,10},{10,18},{18,26},{... | collective-permute-start | bytes 737288 | tf_op jit(solution)/shard_map/ppermute | solution.py:267
  10.0 24.4 %collective-permute-start.1 = (f32[480,128]{1,0:T(8,128)S(1)}, f32[480,128]{1,0:T(8,128)S(1)}, u32[]{:S(2)}, u32[]{:S(2)}) collective-permute-start(f32[480,128]{1,0:T(8,128)S(1)} %get-tuple-element.23), channel_id=1, source_target_pairs={{8,0},{16,8},{24,16},{9,1},{17,9},{25,17},{10,2},{18,10},{26,18},{... | collective-permute-start | bytes 737288 | tf_op jit(solution)/shard_map/ppermute | solution.py:268
  14.1 0.7 copy-start.2
  14.8 5.7 %collective-permute-start.6 = (f32[8,128]{1,0:T(8,128)S(1)}, f32[8,128]{1,0:T(8,128)S(1)}, u32[]{:S(2)}, u32[]{:S(2)}) collective-permute-start(f32[8,128]{1,0:T(8,128)S(1)} %broadcast_maximum_fusion), channel_id=1, source_target_pairs={{0,8},{8,0},{16,24},{24,16},{1,9},{9,1},{17,25},{25,17},{2,10},{10... | collective-permute-start | bytes 12296 | tf_op jit(solution)/shard_map/ppermute | solution.py:281
  20.5 6.8 %collective-permute-start.7 = (f32[8,128]{1,0:T(8,128)S(1)}, f32[8,128]{1,0:T(8,128)S(1)}, u32[]{:S(2)}, u32[]{:S(2)}) collective-permute-start(f32[8,128]{1,0:T(8,128)S(1)} %fusion), channel_id=1, source_target_pairs={{0,16},{8,24},{16,0},{24,8},{1,17},{9,25},{17,1},{25,9},{2,18},{10... | collective-permute-start | bytes 12296 | tf_op jit(solution)/shard_map/ppermute | solution.py:281
  27.4 5.7 %collective-permute-start.3 = (f32[384,128]{1,0:T(8,128)S(1)}, f32[384,128]{1,0:T(8,128)S(1)}, u32[]{:S(2)}, u32[]{:S(2)}) collective-permute-start(f32[384,128]{1,0:T(8,128)S(1)} %get-tuple-element.25), channel_id=1, source_target_pairs={{1,0},{2,1},{3,2},{0,3},{5,4},{6,5},{7,6},{4,7},{9,8},{10,9},{11,1... | collective-permute-start | bytes 589832 | tf_op jit(solution)/shard_map/ppermute | solution.py:268
  36.2 17.5 %collective-permute-start.8 = (f32[480,128]{1,0:T(8,128)S(1)}, f32[480,128]{1,0:T(8,128)S(1)}, u32[]{:S(2)}, u32[]{:S(2)}) collective-permute-start(f32[480,128]{1,0:T(8,128)S(1)} %get-tuple-element.28), channel_id=1, source_target_pairs={{0,8},{8,16},{16,24},{1,9},{9,17},{17,25},{2,10},{10,18},{18,26},{... | collective-permute-start | bytes 737288 | tf_op jit(solution)/shard_map/ppermute | solution.py:267
  38.1 15.6 %collective-permute-start.9 = (f32[480,128]{1,0:T(8,128)S(1)}, f32[480,128]{1,0:T(8,128)S(1)}, u32[]{:S(2)}, u32[]{:S(2)}) collective-permute-start(f32[480,128]{1,0:T(8,128)S(1)} %get-tuple-element.29), channel_id=1, source_target_pairs={{8,0},{16,8},{24,16},{9,1},{17,9},{25,17},{10,2},{18,10},{26,18},{... | collective-permute-start | bytes 737288 | tf_op jit(solution)/shard_map/ppermute | solution.py:268
  43.0 9.5 %collective-permute-start.10 = (f32[384,128]{1,0:T(8,128)S(1)}, f32[384,128]{1,0:T(8,128)S(1)}, u32[]{:S(2)}, u32[]{:S(2)}) collective-permute-start(f32[384,128]{1,0:T(8,128)S(1)} %get-tuple-element.30), channel_id=1, source_target_pairs={{0,1},{1,2},{2,3},{3,0},{4,5},{5,6},{6,7},{7,4},{8,9},{9,10},{10,1... | collective-permute-start | bytes 589832 | tf_op jit(solution)/shard_map/ppermute | solution.py:267
  44.6 7.8 %collective-permute-start.11 = (f32[384,128]{1,0:T(8,128)S(1)}, f32[384,128]{1,0:T(8,128)S(1)}, u32[]{:S(2)}, u32[]{:S(2)}) collective-permute-start(f32[384,128]{1,0:T(8,128)S(1)} %get-tuple-element.31), channel_id=1, source_target_pairs={{1,0},{2,1},{3,2},{0,3},{5,4},{6,5},{7,6},{4,7},{9,8},{10,9},{11,1... | collective-permute-start | bytes 589832 | tf_op jit(solution)/shard_map/ppermute | solution.py:268
  47.2 3.4 %collective-permute-start.12 = (f32[240,128]{1,0:T(8,128)S(1)}, f32[240,128]{1,0:T(8,128)S(1)}, u32[]{:S(2)}, u32[]{:S(2)}) collective-permute-start(f32[240,128]{1,0:T(8,128)S(1)} %get-tuple-element.32), channel_id=1, source_target_pairs={{0,4},{4,0},{1,5},{5,1},{2,6},{6,2},{3,7},{7,3},{8,12},{12,8},{9,1... | collective-permute-start | bytes 368648 | tf_op jit(solution)/shard_map/ppermute | solution.py:348
  55.5 19.1 %collective-permute-start.13 = (f32[480,128]{1,0:T(8,128)S(1)}, f32[480,128]{1,0:T(8,128)S(1)}, u32[]{:S(2)}, u32[]{:S(2)}) collective-permute-start(f32[480,128]{1,0:T(8,128)S(1)} %get-tuple-element.34), channel_id=1, source_target_pairs={{0,8},{8,16},{16,24},{1,9},{9,17},{17,25},{2,10},{10,18},{18,26},{... | collective-permute-start | bytes 737288 | tf_op jit(solution)/shard_map/ppermute | solution.py:267
  57.5 17.2 %collective-permute-start.14 = (f32[480,128]{1,0:T(8,128)S(1)}, f32[480,128]{1,0:T(8,128)S(1)}, u32[]{:S(2)}, u32[]{:S(2)}) collective-permute-start(f32[480,128]{1,0:T(8,128)S(1)} %get-tuple-element.35), channel_id=1, source_target_pairs={{8,0},{16,8},{24,16},{9,1},{17,9},{25,17},{10,2},{18,10},{26,18},{... | collective-permute-start | bytes 737288 | tf_op jit(solution)/shard_map/ppermute | solution.py:268
  62.3 9.6 %collective-permute-start.15 = (f32[384,128]{1,0:T(8,128)S(1)}, f32[384,128]{1,0:T(8,128)S(1)}, u32[]{:S(2)}, u32[]{:S(2)}) collective-permute-start(f32[384,128]{1,0:T(8,128)S(1)} %get-tuple-element.36), channel_id=1, source_target_pairs={{0,1},{1,2},{2,3},{3,0},{4,5},{5,6},{6,7},{7,4},{8,9},{9,10},{10,1... | collective-permute-start | bytes 589832 | tf_op jit(solution)/shard_map/ppermute | solution.py:267
  63.9 9.5 %collective-permute-start.16 = (f32[384,128]{1,0:T(8,128)S(1)}, f32[384,128]{1,0:T(8,128)S(1)}, u32[]{:S(2)}, u32[]{:S(2)}) collective-permute-start(f32[384,128]{1,0:T(8,128)S(1)} %get-tuple-element.37), channel_id=1, source_target_pairs={{1,0},{2,1},{3,2},{0,3},{5,4},{6,5},{7,6},{4,7},{9,8},{10,9},{11,1... | collective-permute-start | bytes 589832 | tf_op jit(solution)/shard_map/ppermute | solution.py:268
  66.2 3.4 %collective-permute-start.17 = (f32[240,128]{1,0:T(8,128)S(1)}, f32[240,128]{1,0:T(8,128)S(1)}, u32[]{:S(2)}, u32[]{:S(2)}) collective-permute-start(f32[240,128]{1,0:T(8,128)S(1)} %get-tuple-element.38), channel_id=1, source_target_pairs={{0,4},{4,0},{1,5},{5,1},{2,6},{6,2},{3,7},{7,3},{8,12},{12,8},{9,1... | collective-permute-start | bytes 368648 | tf_op jit(solution)/shard_map/ppermute | solution.py:348

commit v3 on v2

--- a/solution.py
+++ b/solution.py
@@ -98,6 +98,17 @@
     return low, high
 
 
+def axis_flags(flag_ref, which):
+    return [flag_ref[pl.ds((3 * which + k) * SUB, SUB), :] > 0.0 for k in range(3)]
+
+
+def sided(even, load, a_ref, b_ref):
+    from_a, from_b = load(a_ref), load(b_ref)
+    low = [jnp.where(even, b, a) for a, b in zip(from_a, from_b)]
+    high = [jnp.where(even, a, b) for a, b in zip(from_a, from_b)]
+    return low, high
+
+
 def speed_kernel(u_ref, acc_ref, line_ref, out_ref, *, eps, scale):
     rows = u_ref.shape[0]
     count = LANES // SUB
@@ -121,10 +132,9 @@
     lax.fori_loop(0, rows // LANES, group, 0)
 
 
-def y_kernel(u_ref, low_ref, high_ref, flag_ref, wind_ref, speed_ref, acc_in, acc_ref, *, sizes, eps):
+def y_kernel(u_ref, a_ref, b_ref, flag_ref, wind_ref, speed_ref, acc_in, acc_ref, *, sizes, eps):
     nx, nh, ny = sizes
-    first = flag_ref[0:SUB] > 0.0
-    last = flag_ref[SUB : 2 * SUB] > 0.0
+    first, last, even = axis_flags(flag_ref, 0)
     for xg in range(nx // SUB):
 
         def column(h, carry):
@@ -136,8 +146,7 @@
             def halo(ref, k):
                 return ref[pl.ds(pl.multiple_of((k * nh + h) * nx + xg * SUB, SUB), SUB), :]
 
-            low = [halo(low_ref, k) for k in range(3)]
-            high = [halo(high_ref, k) for k in range(3)]
+            low, high = sided(even, lambda ref: [halo(ref, k) for k in range(3)], a_ref, b_ref)
             low, high = edge_fix(low, center[:2], center[-2:], high, (first, last))
             speed = speed_ref[pl.ds(pl.multiple_of(h * SUB, SUB), SUB), :]
             flows = lambda y: speed + wind_ref[pl.ds(y * nx + xg * SUB, SUB), :]
@@ -148,8 +157,9 @@
         lax.fori_loop(0, nh, column, 0)
 
 
-def head_kernel(u_ref, low_ref, high_ref, acc_in, acc_ref, *, sizes, eps, scale):
+def head_kernel(u_ref, a_ref, b_ref, flag_ref, acc_in, acc_ref, *, sizes, eps, scale):
     nx, nh, ny = sizes
+    even = axis_flags(flag_ref, 2)[2]
 
     def line(x, carry):
         for yg in range(ny // SUB):
@@ -157,9 +167,8 @@
             def rows(h, height=nh):
                 return pl.ds(pl.multiple_of((x * height + h) * ny + yg * SUB, SUB), SUB)
 
-            us = [low_ref[rows(k, 3), :] for k in range(3)]
-            us += [u_ref[rows(h), :] for h in range(nh)]
-            us += [high_ref[rows(k, 3), :] for k in range(3)]
+            low, high = sided(even, lambda ref: [ref[rows(k, 3), :] for k in range(3)], a_ref, b_ref)
+            us = low + [u_ref[rows(h), :] for h in range(nh)] + high
             for h, value in enumerate(line_max(us, eps, scale)):
                 acc_ref[rows(h), :] = acc_in[rows(h), :] + value
         return carry
@@ -167,14 +176,13 @@
     lax.fori_loop(0, nx, line, 0)
 
 
-def x_kernel(*refs, sizes, eps, stage, swap_y):
+def x_kernel(*refs, sizes, eps, stage):
     nx, nh, ny = sizes
     it = iter(refs)
-    u_ref, low_ref, high_ref, flag_ref, wind_ref, speed_ref, acc_in, rate_ref = (next(it) for _ in range(8))
+    u_ref, a_ref, b_ref, flag_ref, wind_ref, speed_ref, acc_in, rate_ref = (next(it) for _ in range(8))
     first_ref = next(it) if stage > 1 else u_ref
     next_ref = next(it)
-    first = flag_ref[2 * SUB : 3 * SUB] > 0.0
-    last = flag_ref[3 * SUB : 4 * SUB] > 0.0
+    first, last, even = axis_flags(flag_ref, 1)
     step = CFL_NUMBER / rate_ref[...]
 
     def line(h, carry):
@@ -184,8 +192,7 @@
                 return pl.ds(pl.multiple_of((x * nh + h) * ny + yg * SUB, SUB), SUB)
 
             center = [u_ref[rows(x), :] for x in range(nx)]
-            low = [low_ref[rows(k), :] for k in range(3)]
-            high = [high_ref[rows(k), :] for k in range(3)]
+            low, high = sided(even, lambda ref: [ref[rows(k), :] for k in range(3)], a_ref, b_ref)
             low, high = edge_fix(low, center[:2], center[-2:], high, (first, last))
             speed = speed_ref[pl.ds(pl.multiple_of(h * SUB, SUB), SUB), :]
             flows = lambda x: speed + wind_ref[pl.ds(x * ny + yg * SUB, SUB), :]
@@ -203,19 +210,36 @@
 
     lax.fori_loop(0, nh, line, 0)
     if stage < 3:
-        pack_faces(next_ref, list(it), flag_ref, sizes, swap_y)
-
-
-def pack_faces(u_ref, faces, flag_ref, sizes, swap_y):
+        pack_faces(next_ref, list(it), flag_ref, sizes)
+
+
+def pack_faces(u_ref, faces, flag_ref, sizes):
     nx, nh, ny = sizes
     plane = nh * ny
-    xlo, xhi, hlo, hhi = faces[:4]
-    xlo[...] = u_ref[pl.ds(0, 3 * plane), :]
-    xhi[...] = u_ref[pl.ds((nx - 3) * plane, 3 * plane), :]
+    xa, xb, ha, hb, ya = faces[:5]
+    yb = faces[5] if len(faces) > 5 else None
+    even = axis_flags(flag_ref, 1)[2]
+
+    def both(a_ref, b_ref, at, low, high, even):
+        a_ref[at, :] = jnp.where(even, high, low)
+        if b_ref is not None:
+            b_ref[at, :] = jnp.where(even, low, high)
+
+    def x_rows(i, carry):
+        at = pl.multiple_of(i * SUB, SUB)
+        low = u_ref[pl.ds(at, SUB), :]
+        high = u_ref[pl.ds(at + (nx - 3) * plane, SUB), :]
+        both(xa, xb, pl.ds(at, SUB), low, high, even)
+        return carry
+
+    lax.fori_loop(0, 3 * plane // SUB, x_rows, 0, unroll=6)
+    even_h = axis_flags(flag_ref, 2)[2]
     for x in range(nx):
-        hlo[pl.ds(x * 3 * ny, 3 * ny), :] = u_ref[pl.ds(x * plane, 3 * ny), :]
-        hhi[pl.ds(x * 3 * ny, 3 * ny), :] = u_ref[pl.ds(x * plane + (nh - 3) * ny, 3 * ny), :]
-    first = flag_ref[0:SUB] > 0.0
+        for k in range(3 * ny // SUB):
+            low = u_ref[pl.ds(x * plane + k * SUB, SUB), :]
+            high = u_ref[pl.ds(x * plane + (nh - 3) * ny + k * SUB, SUB), :]
+            both(ha, hb, pl.ds(x * 3 * ny + k * SUB, SUB), low, high, even_h)
+    even_y = axis_flags(flag_ref, 0)[2]
     for xg in range(nx // SUB):
 
         def column(h, carry):
@@ -225,20 +249,14 @@
                     return pl.ds((xg * SUB * nh + h) * ny + y, SUB, stride=plane)
 
                 at = pl.ds(pl.multiple_of((k * nh + h) * nx + xg * SUB, SUB), SUB)
-                low = u_ref[rows(k), :]
-                high = u_ref[rows(ny - 3 + k), :]
-                if swap_y:
-                    faces[4][at, :] = jnp.where(first, high, low)
-                else:
-                    faces[4][at, :] = low
-                    faces[5][at, :] = high
+                both(ya, yb, at, u_ref[rows(k), :], u_ref[rows(ny - 3 + k), :], even_y)
             return carry
 
         lax.fori_loop(0, nh, column, 0)
 
 
-def pack_kernel(u_ref, flag_ref, *faces, sizes, swap_y):
-    pack_faces(u_ref, list(faces), flag_ref, sizes, swap_y)
+def pack_kernel(u_ref, flag_ref, *faces, sizes):
+    pack_faces(u_ref, list(faces), flag_ref, sizes)
 
 
 VMEM_LIMIT = 8 * 1024 * 1024
@@ -261,12 +279,27 @@
     return got
 
 
-def neighbours(low_face, high_face, axis, closed):
+def paired(axis):
+    return lax.axis_size(axis) % 2 == 0
+
+
+def neighbours(face_a, face_b, axis, closed):
     count = lax.axis_size(axis)
     ends = count if closed else count - 1
-    from_low = lax.ppermute(high_face, axis, [(i, (i + 1) % count) for i in range(ends)])
-    from_high = lax.ppermute(low_face, axis, [((i + 1) % count, i) for i in range(ends)])
-    return from_low, from_high
+    if not paired(axis):
+        got_b = lax.ppermute(face_a, axis, [(i, (i + 1) % count) for i in range(ends)])
+        got_a = lax.ppermute(face_b, axis, [((i + 1) % count, i) for i in range(ends)])
+        return got_a, got_b
+
+    def swap(face, start):
+        pairs = []
+        for i in range(start, ends, 2):
+            pairs += [(i, (i + 1) % count), ((i + 1) % count, i)]
+        return lax.ppermute(face, axis, pairs) if pairs else None
+
+    got_b = swap(face_b, 1) if face_b is not None else None
+    got_a = swap(face_a, 0)
+    return got_a, got_a if got_b is None else got_b
 
 
 def all_max(value, axes):
@@ -291,8 +324,6 @@
     n_head = nh * lax.axis_size("ha")
     d_theta = 2.0 * math.pi / n_head
     d_speed = SPEED_SPAN / nv
-    count_y = lax.axis_size("gy")
-    swap_y = count_y == 2
 
     angles = np.arange(n_head) * d_theta
     cosines, sines = np.cos(angles), np.sin(angles)
@@ -301,10 +332,12 @@
     def edge(axis, at):
         return (lax.axis_index(axis) == at).astype(jnp.float32)
 
-    flags = jnp.stack(
-        [edge("gy", 0), edge("gy", count_y - 1), edge("gx", 0), edge("gx", lax.axis_size("gx") - 1)]
-    )
-    flags = jnp.broadcast_to(flags[:, None, None], (4, SUB, nv)).reshape(4 * SUB, nv)
+    flags = []
+    for axis in ("gy", "gx", "ha"):
+        even = (lax.axis_index(axis) % 2 == 0) | (not paired(axis))
+        flags += [edge(axis, 0), edge(axis, lax.axis_size(axis) - 1), even.astype(jnp.float32)]
+    flags = jnp.stack(flags)
+    flags = jnp.broadcast_to(flags[:, None, None], (9, SUB, nv)).reshape(9 * SUB, nv)
 
     ends = np.array([speeds[0], speeds[-1]])
     cos_ends = jnp.asarray((ends[:, None] * cosines).reshape(-1, 1, 1), jnp.float32)
@@ -328,7 +361,7 @@
 
     start = level_set.transpose(0, 2, 1, 3).reshape(rows, nv)
     x_face, h_face, y_face = (3 * nh * ny, nv), (nx * 3 * ny, nv), (3 * nh * nx, nv)
-    face_shapes = [x_face, x_face, h_face, h_face] + [y_face] * (1 if swap_y else 2)
+    face_shapes = [x_face, x_face, h_face, h_face] + [y_face] * (1 if lax.axis_size("gy") == 2 else 2)
     vregs = rows // SUB
     flops = vregs * 40 * SUB * LANES
 
@@ -337,17 +370,14 @@
     eps_v = 0.75 * WENO_EPS * d_speed**2
 
     faces = call(
-        functools.partial(pack_kernel, sizes=sizes, swap_y=swap_y), "pack", [start, flags], face_shapes, 1000
+        functools.partial(pack_kernel, sizes=sizes), "pack", [start, flags], face_shapes, 1000
     )
     rate = all_max(top, ("gy", "gx"))
     u = start
     for stage in (1, 2, 3):
-        from_xl, from_xh = neighbours(faces[0], faces[1], "gx", False)
-        from_hl, from_hh = neighbours(faces[2], faces[3], "ha", True)
-        if swap_y:
-            from_yl = from_yh = lax.ppermute(faces[4], "gy", [(0, 1), (1, 0)])
-        else:
-            from_yl, from_yh = neighbours(faces[4], faces[5], "gy", False)
+        got_x = neighbours(faces[0], faces[1], "gx", False)
+        got_h = neighbours(faces[2], faces[3], "ha", True)
+        got_y = neighbours(faces[4], faces[5] if len(faces) > 5 else None, "gy", False)
         (acc,) = call(
             functools.partial(speed_kernel, eps=eps_v, scale=ACCEL_MAX / (6.0 * d_speed)),
             f"speed{stage}",
@@ -359,22 +389,22 @@
         (acc,) = call(
             functools.partial(y_kernel, sizes=sizes, eps=eps_g),
             f"y{stage}",
-            [u, from_yl, from_yh, flags, wind_y, speed_y, acc],
+            [u, *got_y, flags, wind_y, speed_y, acc],
             [(rows, nv)],
             flops,
         )
         (acc,) = call(
             functools.partial(head_kernel, sizes=sizes, eps=eps_h, scale=TURN_MAX / (6.0 * d_theta)),
             f"head{stage}",
-            [u, from_hl, from_hh, acc],
+            [u, *got_h, flags, acc],
             [(rows, nv)],
             flops,
         )
-        ins = [u, from_xl, from_xh, flags, wind_x, speed_x, acc, rate]
+        ins = [u, *got_x, flags, wind_x, speed_x, acc, rate]
         if stage > 1:
             ins.append(start)
         got = call(
-            functools.partial(x_kernel, sizes=sizes, eps=eps_g, stage=stage, swap_y=swap_y),
+            functools.partial(x_kernel, sizes=sizes, eps=eps_g, stage=stage),
             f"x{stage}",
             ins,
             [(rows, nv)] + (face_shapes if stage < 3 else []),

time: 77.6 us -> 73.7 us (0.950)
  starting transfers between devices: 36 us -> 26.2 us
  waiting for transfers between devices: 8.51 us -> 14 us
    ppermute x15, starting transfers between devices: 32.8 us -> 24.6 us  [swap(): return lax.ppermute(face, axis, pairs) if pairs else None]
    ppermute x15, waiting for transfers between devices: 3.47 us -> 7.34 us  [swap(): return lax.ppermute(face, axis, pairs) if pairs else None]
    ppermute x3, waiting for transfers between devices: 5.04 us -> 6.63 us  [all_max(): lax.ppermute(value, axis, [(i, i ^ reach) for i in range(count)])]
    ppermute x3, starting transfers between devices: 3.19 us -> 1.64 us  [all_max(): lax.ppermute(value, axis, [(i, i ^ reach) for i in range(count)])]
  transfers between devices with their start and end apart: 18 -> 18, of which waited for: 4 -> 4; matrix products, arithmetic and copies ran while one was open for 3% -> 3% of each run, Pallas kernels for 26% -> 27%
where the time goes in v3:
time: 73.7 us; the launch traced here: 72.9 us
  starting transfers between devices  26.2 us (36%)
  Pallas kernels  25.7 us (35%)
  waiting for transfers between devices  14 us (19%)
  local copies, waits for them, and re-layouts  5.34 us (7%)
  between operations  0.96 us (1%)
    pallas_call x13, Pallas kernels, call(): pl.pallas_call(kernel, out_shape=shapes, in_specs=[VM] * len(ins), out_sp...  25.7 us
    ppermute x15, starting transfers between devices, swap(): return lax.ppermute(face, axis, pairs) if pairs else None  24.6 us
    ppermute x15, waiting for transfers between devices, swap(): return lax.ppermute(face, axis, pairs) if pairs else None  7.34 us
    ppermute x3, waiting for transfers between devices, all_max(): lax.ppermute(value, axis, [(i, i ^ reach) for i in range(count)])  6.63 us
    unnamed x10, local copies, waits for them, and re-layouts  2.47 us
    ppermute x3, starting transfers between devices, all_max(): lax.ppermute(value, axis, [(i, i ^ reach) for i in range(count)])  1.64 us
  transfers between devices with their start and end apart: 18, of which 4 were waited for; matrix products, arithmetic and copies ran while one was open for 3% of the time, Pallas kernels for 27%

profile of v3, /device:TPU:4, one launch (start us, length us, event | category | flops | bytes accessed | tf_op | source)
XLA Modules:
  0.0 72.9 jit_solution(13237279373978879265)
XLA Ops:
  0.0 0.7 slice_bitcast_fusion.2
  1.4 0.7 multiply_reduce_fusion
  3.2 1.1 %copy-done = f32[8,16,10,128]{3,1,2,0:T(8,128)S(1)} copy-done((f32[8,16,10,128]{3,1,2,0:T(8,128)S(1)}, f32[8,16,10,128]{3,1,2,0:T(8,128)}, u32[]{:S(2)}) %copy-start) | copy-done | bytes 655384
  5.1 1.6 %collective-permute-start.2 = (f32[384,128]{1,0:T(8,128)S(1)}, f32[384,128]{1,0:T(8,128)S(1)}, u32[]{:S(2)}, u32[]{:S(2)}) collective-permute-start(f32[384,128]{1,0:T(8,128)S(1)} %get-tuple-element.24), channel_id=1, source_target_pairs={{0,1},{1,0},{2,3},{3,2},{4,5},{5,4},{6,7},{7,6},{8,9},{9,8},{10,11... | collective-permute-start | bytes 589832 | tf_op jit(solution)/shard_map/ppermute | solution.py:298
  6.7 1.5 %collective-permute-start = (f32[480,128]{1,0:T(8,128)S(1)}, f32[480,128]{1,0:T(8,128)S(1)}, u32[]{:S(2)}, u32[]{:S(2)}) collective-permute-start(f32[480,128]{1,0:T(8,128)S(1)} %get-tuple-element.22), channel_id=1, source_target_pairs={{0,8},{8,0},{16,24},{24,16},{1,9},{9,1},{17,25},{25,17},{2,10},{10... | collective-permute-start | bytes 737288 | tf_op jit(solution)/shard_map/ppermute | solution.py:298
  8.2 2.4 %collective-permute-start.1 = (f32[480,128]{1,0:T(8,128)S(1)}, f32[480,128]{1,0:T(8,128)S(1)}, u32[]{:S(2)}, u32[]{:S(2)}) collective-permute-start(f32[480,128]{1,0:T(8,128)S(1)} %get-tuple-element.23), channel_id=1, source_target_pairs={{8,16},{16,8},{9,17},{17,9},{10,18},{18,10},{11,19},{19,11},{12,20... | collective-permute-start | bytes 737288 | tf_op jit(solution)/shard_map/ppermute | solution.py:298
  10.6 0.7 constant_dynamic-slice_fusion
  12.1 6.6 %collective-permute-done.6 = f32[8,128]{1,0:T(8,128)S(1)} collective-permute-done((f32[8,128]{1,0:T(8,128)S(1)}, f32[8,128]{1,0:T(8,128)S(1)}, u32[]{:S(2)}, u32[]{:S(2)}) %collective-permute-start.6) | collective-permute-done | bytes 4128 | tf_op jit(solution)/shard_map/ppermute | solution.py:314
  18.7 1.5 %collective-permute-start.7 = (f32[8,128]{1,0:T(8,128)S(1)}, f32[8,128]{1,0:T(8,128)S(1)}, u32[]{:S(2)}, u32[]{:S(2)}) collective-permute-start(f32[8,128]{1,0:T(8,128)S(1)} %fusion), channel_id=1, source_target_pairs={{0,16},{8,24},{16,0},{24,8},{1,17},{9,25},{17,1},{25,9},{2,18},{10... | collective-permute-start | bytes 12296 | tf_op jit(solution)/shard_map/ppermute | solution.py:314
  20.2 0.7 constant_dynamic-slice_fusion.1
  21.2 3.4 %speed1.1.acc_in = f32[1280,128]{1,0:T(8,128)S(1)} custom-call(f32[1280,128]{1,0:T(8,128)S(1)} %bitcast.28), custom_call_target="tpu_custom_call" | custom-call | flops 6553600 | bytes 1024 | tf_op jit(solution)/shard_map/speed1/pallas_call | solution.py:269
  24.6 2.5 %collective-permute-start.3 = (f32[384,128]{1,0:T(8,128)S(1)}, f32[384,128]{1,0:T(8,128)S(1)}, u32[]{:S(2)}, u32[]{:S(2)}) collective-permute-start(f32[384,128]{1,0:T(8,128)S(1)} %get-tuple-element.25), channel_id=1, source_target_pairs={{1,2},{2,1},{3,0},{0,3},{5,6},{6,5},{7,4},{4,7},{9,10},{10,9},{11,... | collective-permute-start | bytes 589832 | tf_op jit(solution)/shard_map/ppermute | solution.py:298
  27.2 1.8 %y1.1.acc_in = f32[1280,128]{1,0:T(8,128)S(1)} custom-call(f32[1280,128]{1,0:T(8,128)S(1)} %bitcast.29, f32[240,128]{1,0:T(8,128)S(1)} %collective-permute-done.4.a_ref.b_ref, f32[240,128]{1,0:T(8,128)S(1)} %collective-permute-done.4.a_ref.b_ref, f32[72,128]{1,0:T(8,128)S(1)} %broadcast_in_dim.42.flag_ref.refs_3_, f32[128,128]{1,0:T(8,128)S(1)} %broadcast_in_dim.47.wind_ref, ...), custom_call_target="tpu_custom_call" | custom-call | flops 6553600 | bytes 1024 | tf_op jit(solution)/shard_map/y1/pallas_call | solution.py:269
  29.0 3.1 %collective-permute-done.3.b_ref = f32[384,128]{1,0:T(8,128)S(1)} collective-permute-done((f32[384,128]{1,0:T(8,128)S(1)}, f32[384,128]{1,0:T(8,128)S(1)}, u32[]{:S(2)}, u32[]{:S(2)}) %collective-permute-start.3) | collective-permute-done | bytes 196640 | tf_op jit(solution)/shard_map/ppermute | solution.py:298
  32.2 1.3 %head1.1.refs_6_ = f32[1280,128]{1,0:T(8,128)S(1)} custom-call(f32[1280,128]{1,0:T(8,128)S(1)} %bitcast.30, f32[384,128]{1,0:T(8,128)S(1)} %collective-permute-done.2.a_ref, f32[384,128]{1,0:T(8,128)S(1)} %collective-permute-done.3.b_ref, f32[72,128]{1,0:T(8,128)S(1)} %broadcast_in_dim.42.flag_ref.refs_3_, f32[1280,128]{1,0:T(8,128)S(1)} %y1.1.acc_in), custom_call_target="tpu_custom_call" | custom-call | flops 6553600 | bytes 1024 | tf_op jit(solution)/shard_map/head1/pallas_call | solution.py:269
  33.6 1.8 %x1.1 = (f32[1280,128]{1,0:T(8,128)S(1)}, f32[480,128]{1,0:T(8,128)S(1)}, f32[480,128]{1,0:T(8,128)S(1)}, f32[384,128]{1,0:T(8,128)S(1)}, f32[384,128]{1,0:T(8,128)S(1)}, /*index=5*/f32[240,128]{1,0:T(8,128)S(1)}) custom-call(f32[1280,128]{1,0:T(8,128)S(1)} %bitcast.31, f32[480,128]{1,0:T(8,128)S(1)} %collective-permute-done.refs_1_, ...), custom_call_target="tpu_custom_call" | custom-call | flops 6553600 | bytes 1024 | tf_op jit(solution)/shard_map/x1/pallas_call | solution.py:269
  35.3 1.1 %collective-permute-start.8 = (f32[480,128]{1,0:T(8,128)S(1)}, f32[480,128]{1,0:T(8,128)S(1)}, u32[]{:S(2)}, u32[]{:S(2)}) collective-permute-start(f32[480,128]{1,0:T(8,128)S(1)} %get-tuple-element.28), channel_id=1, source_target_pairs={{0,8},{8,0},{16,24},{24,16},{1,9},{9,1},{17,25},{25,17},{2,10},{10... | collective-permute-start | bytes 737288 | tf_op jit(solution)/shard_map/ppermute | solution.py:298
  36.4 3.4 %collective-permute-start.9 = (f32[480,128]{1,0:T(8,128)S(1)}, f32[480,128]{1,0:T(8,128)S(1)}, u32[]{:S(2)}, u32[]{:S(2)}) collective-permute-start(f32[480,128]{1,0:T(8,128)S(1)} %get-tuple-element.29), channel_id=1, source_target_pairs={{8,16},{16,8},{9,17},{17,9},{10,18},{18,10},{11,19},{19,11},{12,20... | collective-permute-start | bytes 737288 | tf_op jit(solution)/shard_map/ppermute | solution.py:298
  39.8 3.4 %collective-permute-start.10 = (f32[384,128]{1,0:T(8,128)S(1)}, f32[384,128]{1,0:T(8,128)S(1)}, u32[]{:S(2)}, u32[]{:S(2)}) collective-permute-start(f32[384,128]{1,0:T(8,128)S(1)} %get-tuple-element.30), channel_id=1, source_target_pairs={{0,1},{1,0},{2,3},{3,2},{4,5},{5,4},{6,7},{7,6},{8,9},{9,8},{10,11... | collective-permute-start | bytes 589832 | tf_op jit(solution)/shard_map/ppermute | solution.py:298
  43.2 2.6 %collective-permute-start.11 = (f32[384,128]{1,0:T(8,128)S(1)}, f32[384,128]{1,0:T(8,128)S(1)}, u32[]{:S(2)}, u32[]{:S(2)}) collective-permute-start(f32[384,128]{1,0:T(8,128)S(1)} %get-tuple-element.31), channel_id=1, source_target_pairs={{1,2},{2,1},{3,0},{0,3},{5,6},{6,5},{7,4},{4,7},{9,10},{10,9},{11,... | collective-permute-start | bytes 589832 | tf_op jit(solution)/shard_map/ppermute | solution.py:298
  45.8 3.4 %speed2.1.acc_in = f32[1280,128]{1,0:T(8,128)S(1)} custom-call(f32[1280,128]{1,0:T(8,128)S(1)} %get-tuple-element.27.u_ref.refs_0_), custom_call_target="tpu_custom_call" | custom-call | flops 6553600 | bytes 1024 | tf_op jit(solution)/shard_map/speed2/pallas_call | solution.py:269
  49.2 1.8 %y2.1.acc_in = f32[1280,128]{1,0:T(8,128)S(1)} custom-call(f32[1280,128]{1,0:T(8,128)S(1)} %get-tuple-element.27.u_ref.refs_0_, f32[240,128]{1,0:T(8,128)S(1)} %collective-permute-done.12.a_ref.b_ref, f32[240,128]{1,0:T(8,128)S(1)} %collective-permute-done.12.a_ref.b_ref, f32[72,128]{1,0:T(8,128)S(1)} %broadcast_in_dim.42.flag_ref.refs_3_, ...), custom_call_target="tpu_custom_call" | custom-call | flops 6553600 | bytes 1024 | tf_op jit(solution)/shard_map/y2/pallas_call | solution.py:269
  51.0 2.7 %collective-permute-done.11.b_ref = f32[384,128]{1,0:T(8,128)S(1)} collective-permute-done((f32[384,128]{1,0:T(8,128)S(1)}, f32[384,128]{1,0:T(8,128)S(1)}, u32[]{:S(2)}, u32[]{:S(2)}) %collective-permute-start.11) | collective-permute-done | bytes 196640 | tf_op jit(solution)/shard_map/ppermute | solution.py:298
  53.8 1.3 %head2.1.refs_6_ = f32[1280,128]{1,0:T(8,128)S(1)} custom-call(f32[1280,128]{1,0:T(8,128)S(1)} %get-tuple-element.27.u_ref.refs_0_, f32[384,128]{1,0:T(8,128)S(1)} %collective-permute-done.10.a_ref, f32[384,128]{1,0:T(8,128)S(1)} %collective-permute-done.11.b_ref, f32[72,128]{1,0:T(8,128)S(1)} %broadcast_in_dim.42.flag_ref.refs_3_, f32[1280,128]{1,0:T(8,128)S(1)} %y2.1.acc_in), custom_call_target="tpu_custom_call" | custom-call | flops 6553600 | bytes 1024 | tf_op jit(solution)/shard_map/head2/pallas_call | solution.py:269
  55.1 1.8 %x2.1 = (f32[1280,128]{1,0:T(8,128)S(1)}, f32[480,128]{1,0:T(8,128)S(1)}, f32[480,128]{1,0:T(8,128)S(1)}, f32[384,128]{1,0:T(8,128)S(1)}, f32[384,128]{1,0:T(8,128)S(1)}, /*index=5*/f32[240,128]{1,0:T(8,128)S(1)}) custom-call(f32[1280,128]{1,0:T(8,128)S(1)} %get-tuple-element.27.u_ref.refs_0_, f32[480,128]{1,0:T(8,128)S(1)} %collective-permute-done.8.refs_1_, ...), custom_call_target="tpu_custom_call" | custom-call | flops 6553600 | bytes 1024 | tf_op jit(solution)/shard_map/x2/pallas_call | solution.py:269
  57.0 3.3 %collective-permute-start.14 = (f32[480,128]{1,0:T(8,128)S(1)}, f32[480,128]{1,0:T(8,128)S(1)}, u32[]{:S(2)}, u32[]{:S(2)}) collective-permute-start(f32[480,128]{1,0:T(8,128)S(1)} %get-tuple-element.35), channel_id=1, source_target_pairs={{8,16},{16,8},{9,17},{17,9},{10,18},{18,10},{11,19},{19,11},{12,20... | collective-permute-start | bytes 737288 | tf_op jit(solution)/shard_map/ppermute | solution.py:298
  60.4 2.1 %collective-permute-start.16 = (f32[384,128]{1,0:T(8,128)S(1)}, f32[384,128]{1,0:T(8,128)S(1)}, u32[]{:S(2)}, u32[]{:S(2)}) collective-permute-start(f32[384,128]{1,0:T(8,128)S(1)} %get-tuple-element.37), channel_id=1, source_target_pairs={{1,2},{2,1},{3,0},{0,3},{5,6},{6,5},{7,4},{4,7},{9,10},{10,9},{11,... | collective-permute-start | bytes 589832 | tf_op jit(solution)/shard_map/ppermute | solution.py:298
  62.6 3.4 %speed3.1.acc_in = f32[1280,128]{1,0:T(8,128)S(1)} custom-call(f32[1280,128]{1,0:T(8,128)S(1)} %get-tuple-element.33.u_ref.refs_0_), custom_call_target="tpu_custom_call" | custom-call | flops 6553600 | bytes 1024 | tf_op jit(solution)/shard_map/speed3/pallas_call | solution.py:269
  66.0 1.8 %y3.1.acc_in = f32[1280,128]{1,0:T(8,128)S(1)} custom-call(f32[1280,128]{1,0:T(8,128)S(1)} %get-tuple-element.33.u_ref.refs_0_, f32[240,128]{1,0:T(8,128)S(1)} %collective-permute-done.17.a_ref.b_ref, f32[240,128]{1,0:T(8,128)S(1)} %collective-permute-done.17.a_ref.b_ref, f32[72,128]{1,0:T(8,128)S(1)} %broadcast_in_dim.42.flag_ref.refs_3_, ...), custom_call_target="tpu_custom_call" | custom-call | flops 6553600 | bytes 1024 | tf_op jit(solution)/shard_map/y3/pallas_call | solution.py:269
  67.8 1.5 %collective-permute-done.15.a_ref = f32[384,128]{1,0:T(8,128)S(1)} collective-permute-done((f32[384,128]{1,0:T(8,128)S(1)}, f32[384,128]{1,0:T(8,128)S(1)}, u32[]{:S(2)}, u32[]{:S(2)}) %collective-permute-start.15) | collective-permute-done | bytes 196640 | tf_op jit(solution)/shard_map/ppermute | solution.py:298
  69.2 1.3 %head3.1.refs_6_ = f32[1280,128]{1,0:T(8,128)S(1)} custom-call(f32[1280,128]{1,0:T(8,128)S(1)} %get-tuple-element.33.u_ref.refs_0_, f32[384,128]{1,0:T(8,128)S(1)} %collective-permute-done.15.a_ref, f32[384,128]{1,0:T(8,128)S(1)} %collective-permute-done.16.b_ref, f32[72,128]{1,0:T(8,128)S(1)} %broadcast_in_dim.42.flag_ref.refs_3_, f32[1280,128]{1,0:T(8,128)S(1)} %y3.1.acc_in), custom_call_target="tpu_custom_call" | custom-call | flops 6553600 | bytes 1024 | tf_op jit(solution)/shard_map/head3/pallas_call | solution.py:269
  70.6 2.3 %x3.1 = f32[1280,128]{1,0:T(8,128)} custom-call(f32[1280,128]{1,0:T(8,128)S(1)} %get-tuple-element.33.u_ref.refs_0_, f32[480,128]{1,0:T(8,128)S(1)} %collective-permute-done.13.refs_1_, f32[480,128]{1,0:T(8,128)S(1)} %collective-permute-done.14.refs_2_, f32[72,128]{1,0:T(8,128)S(1)} %broadcast_in_dim.42.flag_ref.refs_3_, ...), custom_call_target="tpu_custom_call" | custom-call | flops 6553600 | bytes 1024 | tf_op jit(solution)/shard_map/x3/pallas_call | solution.py:269
  (49 shorter events, 3.3 us)
Async XLA Ops:
  0.7 0.7 copy-start.3
  0.7 0.7 copy-start.4
  2.7 9.3 %collective-permute-start.5 = (f32[8,128]{1,0:T(8,128)S(1)}, f32[8,128]{1,0:T(8,128)S(1)}, u32[]{:S(2)}, u32[]{:S(2)}) collective-permute-start(f32[8,128]{1,0:T(8,128)S(1)} %broadcast_in_dim.49), channel_id=1, source_target_pairs={{0,4},{4,0},{1,5},{5,1},{2,6},{6,2},{3,7},{7,3},{8,12},{12,8},{9,1... | collective-permute-start | bytes 12296 | tf_op jit(solution)/shard_map/ppermute | solution.py:314
  3.2 1.1 %copy-start = (f32[8,16,10,128]{3,1,2,0:T(8,128)S(1)}, f32[8,16,10,128]{3,1,2,0:T(8,128)}, u32[]{:S(2)}) copy-start(f32[8,16,10,128]{3,1,2,0:T(8,128)} %param.6) | copy-start | bytes 1966084
  4.3 16.9 %copy-start.1 = (f32[8,16,10,128]{3,1,2,0:T(8,128)S(1)}, f32[8,16,10,128]{3,1,2,0:T(8,128)}, u32[]{:S(2)}) copy-start(f32[8,16,10,128]{3,1,2,0:T(8,128)} %param.6) | copy-start | bytes 1966084
  4.6 22.6 %collective-permute-start.4 = (f32[240,128]{1,0:T(8,128)S(1)}, f32[240,128]{1,0:T(8,128)S(1)}, u32[]{:S(2)}, u32[]{:S(2)}) collective-permute-start(f32[240,128]{1,0:T(8,128)S(1)} %get-tuple-element.26), channel_id=1, source_target_pairs={{0,4},{4,0},{1,5},{5,1},{2,6},{6,2},{3,7},{7,3},{8,12},{12,8},{9,1... | collective-permute-start | bytes 368648 | tf_op jit(solution)/shard_map/ppermute | solution.py:298
  5.1 23.9 %collective-permute-start.2 = (f32[384,128]{1,0:T(8,128)S(1)}, f32[384,128]{1,0:T(8,128)S(1)}, u32[]{:S(2)}, u32[]{:S(2)}) collective-permute-start(f32[384,128]{1,0:T(8,128)S(1)} %get-tuple-element.24), channel_id=1, source_target_pairs={{0,1},{1,0},{2,3},{3,2},{4,5},{5,4},{6,7},{7,6},{8,9},{9,8},{10,11... | collective-permute-start | bytes 589832 | tf_op jit(solution)/shard_map/ppermute | solution.py:298
  6.7 26.8 %collective-permute-start = (f32[480,128]{1,0:T(8,128)S(1)}, f32[480,128]{1,0:T(8,128)S(1)}, u32[]{:S(2)}, u32[]{:S(2)}) collective-permute-start(f32[480,128]{1,0:T(8,128)S(1)} %get-tuple-element.22), channel_id=1, source_target_pairs={{0,8},{8,0},{16,24},{24,16},{1,9},{9,1},{17,25},{25,17},{2,10},{10... | collective-permute-start | bytes 737288 | tf_op jit(solution)/shard_map/ppermute | solution.py:298
  8.2 25.3 %collective-permute-start.1 = (f32[480,128]{1,0:T(8,128)S(1)}, f32[480,128]{1,0:T(8,128)S(1)}, u32[]{:S(2)}, u32[]{:S(2)}) collective-permute-start(f32[480,128]{1,0:T(8,128)S(1)} %get-tuple-element.23), channel_id=1, source_target_pairs={{8,16},{16,8},{9,17},{17,9},{10,18},{18,10},{11,19},{19,11},{12,20... | collective-permute-start | bytes 737288 | tf_op jit(solution)/shard_map/ppermute | solution.py:298
  11.3 0.7 copy-start.2
  12.0 6.7 %collective-permute-start.6 = (f32[8,128]{1,0:T(8,128)S(1)}, f32[8,128]{1,0:T(8,128)S(1)}, u32[]{:S(2)}, u32[]{:S(2)}) collective-permute-start(f32[8,128]{1,0:T(8,128)S(1)} %broadcast_maximum_fusion), channel_id=1, source_target_pairs={{0,8},{8,0},{16,24},{24,16},{1,9},{9,1},{17,25},{25,17},{2,10},{10... | collective-permute-start | bytes 12296 | tf_op jit(solution)/shard_map/ppermute | solution.py:314
  18.7 5.9 %collective-permute-start.7 = (f32[8,128]{1,0:T(8,128)S(1)}, f32[8,128]{1,0:T(8,128)S(1)}, u32[]{:S(2)}, u32[]{:S(2)}) collective-permute-start(f32[8,128]{1,0:T(8,128)S(1)} %fusion), channel_id=1, source_target_pairs={{0,16},{8,24},{16,0},{24,8},{1,17},{9,25},{17,1},{25,9},{2,18},{10... | collective-permute-start | bytes 12296 | tf_op jit(solution)/shard_map/ppermute | solution.py:314
  24.6 7.5 %collective-permute-start.3 = (f32[384,128]{1,0:T(8,128)S(1)}, f32[384,128]{1,0:T(8,128)S(1)}, u32[]{:S(2)}, u32[]{:S(2)}) collective-permute-start(f32[384,128]{1,0:T(8,128)S(1)} %get-tuple-element.25), channel_id=1, source_target_pairs={{1,2},{2,1},{3,0},{0,3},{5,6},{6,5},{7,4},{4,7},{9,10},{10,9},{11,... | collective-permute-start | bytes 589832 | tf_op jit(solution)/shard_map/ppermute | solution.py:298
  35.3 19.7 %collective-permute-start.8 = (f32[480,128]{1,0:T(8,128)S(1)}, f32[480,128]{1,0:T(8,128)S(1)}, u32[]{:S(2)}, u32[]{:S(2)}) collective-permute-start(f32[480,128]{1,0:T(8,128)S(1)} %get-tuple-element.28), channel_id=1, source_target_pairs={{0,8},{8,0},{16,24},{24,16},{1,9},{9,1},{17,25},{25,17},{2,10},{10... | collective-permute-start | bytes 737288 | tf_op jit(solution)/shard_map/ppermute | solution.py:298
  36.4 18.7 %collective-permute-start.9 = (f32[480,128]{1,0:T(8,128)S(1)}, f32[480,128]{1,0:T(8,128)S(1)}, u32[]{:S(2)}, u32[]{:S(2)}) collective-permute-start(f32[480,128]{1,0:T(8,128)S(1)} %get-tuple-element.29), channel_id=1, source_target_pairs={{8,16},{16,8},{9,17},{17,9},{10,18},{18,10},{11,19},{19,11},{12,20... | collective-permute-start | bytes 737288 | tf_op jit(solution)/shard_map/ppermute | solution.py:298
  39.8 11.2 %collective-permute-start.10 = (f32[384,128]{1,0:T(8,128)S(1)}, f32[384,128]{1,0:T(8,128)S(1)}, u32[]{:S(2)}, u32[]{:S(2)}) collective-permute-start(f32[384,128]{1,0:T(8,128)S(1)} %get-tuple-element.30), channel_id=1, source_target_pairs={{0,1},{1,0},{2,3},{3,2},{4,5},{5,4},{6,7},{7,6},{8,9},{9,8},{10,11... | collective-permute-start | bytes 589832 | tf_op jit(solution)/shard_map/ppermute | solution.py:298
  43.2 10.6 %collective-permute-start.11 = (f32[384,128]{1,0:T(8,128)S(1)}, f32[384,128]{1,0:T(8,128)S(1)}, u32[]{:S(2)}, u32[]{:S(2)}) collective-permute-start(f32[384,128]{1,0:T(8,128)S(1)} %get-tuple-element.31), channel_id=1, source_target_pairs={{1,2},{2,1},{3,0},{0,3},{5,6},{6,5},{7,4},{4,7},{9,10},{10,9},{11,... | collective-permute-start | bytes 589832 | tf_op jit(solution)/shard_map/ppermute | solution.py:298
  45.8 3.4 %collective-permute-start.12 = (f32[240,128]{1,0:T(8,128)S(1)}, f32[240,128]{1,0:T(8,128)S(1)}, u32[]{:S(2)}, u32[]{:S(2)}) collective-permute-start(f32[240,128]{1,0:T(8,128)S(1)} %get-tuple-element.32), channel_id=1, source_target_pairs={{0,4},{4,0},{1,5},{5,1},{2,6},{6,2},{3,7},{7,3},{8,12},{12,8},{9,1... | collective-permute-start | bytes 368648 | tf_op jit(solution)/shard_map/ppermute | solution.py:298
  56.9 13.6 %collective-permute-start.13 = (f32[480,128]{1,0:T(8,128)S(1)}, f32[480,128]{1,0:T(8,128)S(1)}, u32[]{:S(2)}, u32[]{:S(2)}) collective-permute-start(f32[480,128]{1,0:T(8,128)S(1)} %get-tuple-element.34), channel_id=1, source_target_pairs={{0,8},{8,0},{16,24},{24,16},{1,9},{9,1},{17,25},{25,17},{2,10},{10... | collective-permute-start | bytes 737288 | tf_op jit(solution)/shard_map/ppermute | solution.py:298
  57.0 13.6 %collective-permute-start.14 = (f32[480,128]{1,0:T(8,128)S(1)}, f32[480,128]{1,0:T(8,128)S(1)}, u32[]{:S(2)}, u32[]{:S(2)}) collective-permute-start(f32[480,128]{1,0:T(8,128)S(1)} %get-tuple-element.35), channel_id=1, source_target_pairs={{8,16},{16,8},{9,17},{17,9},{10,18},{18,10},{11,19},{19,11},{12,20... | collective-permute-start | bytes 737288 | tf_op jit(solution)/shard_map/ppermute | solution.py:298
  60.4 8.9 %collective-permute-start.15 = (f32[384,128]{1,0:T(8,128)S(1)}, f32[384,128]{1,0:T(8,128)S(1)}, u32[]{:S(2)}, u32[]{:S(2)}) collective-permute-start(f32[384,128]{1,0:T(8,128)S(1)} %get-tuple-element.36), channel_id=1, source_target_pairs={{0,1},{1,0},{2,3},{3,2},{4,5},{5,4},{6,7},{7,6},{8,9},{9,8},{10,11... | collective-permute-start | bytes 589832 | tf_op jit(solution)/shard_map/ppermute | solution.py:298
  60.4 8.8 %collective-permute-start.16 = (f32[384,128]{1,0:T(8,128)S(1)}, f32[384,128]{1,0:T(8,128)S(1)}, u32[]{:S(2)}, u32[]{:S(2)}) collective-permute-start(f32[384,128]{1,0:T(8,128)S(1)} %get-tuple-element.37), channel_id=1, source_target_pairs={{1,2},{2,1},{3,0},{0,3},{5,6},{6,5},{7,4},{4,7},{9,10},{10,9},{11,... | collective-permute-start | bytes 589832 | tf_op jit(solution)/shard_map/ppermute | solution.py:298
  62.6 3.4 %collective-permute-start.17 = (f32[240,128]{1,0:T(8,128)S(1)}, f32[240,128]{1,0:T(8,128)S(1)}, u32[]{:S(2)}, u32[]{:S(2)}) collective-permute-start(f32[240,128]{1,0:T(8,128)S(1)} %get-tuple-element.38), channel_id=1, source_target_pairs={{0,4},{4,0},{1,5},{5,1},{2,6},{6,2},{3,7},{7,3},{8,12},{12,8},{9,1... | collective-permute-start | bytes 368648 | tf_op jit(solution)/shard_map/ppermute | solution.py:298

commit v4 on v3

v4 whole, which is shorter than its diff:
```python
import functools
import math

import jax
import jax.numpy as jnp
import numpy as np
from jax import lax
from jax.experimental import pallas as pl
from jax.experimental.pallas import tpu as pltpu
from jax.sharding import PartitionSpec as P


CELL_SIZE = 0.05
SPEED_LOW = 0.1
SPEED_SPAN = 0.4
TURN_MAX = 1.0
ACCEL_MAX = 0.05
CFL_NUMBER = 0.5
WENO_EPS = 1e-06
SUB = 8
LANES = 128


def weno_terms(us, eps):
    n = len(us) - 6
    u = {i - 3: v for i, v in enumerate(us)}
    q = {r: u[r] - u[r - 1] for r in range(-2, n + 3)}
    p = {m: q[m + 1] - q[m] for m in range(-2, n + 2)}
    t, alpha, beta, gamma, a3, g3 = {}, {}, {}, {}, {}, {}
    for r in range(-1, n + 2):
        t[r] = p[r] - p[r - 1]
        z = 1.5 * t[r]
        base = t[r] * t[r] + ((0.75 * p[r - 1]) * p[r] + eps)
        if r <= n - 1:
            s = base + p[r] * z
            alpha[r] = pl.reciprocal(s * s, approx=APPROX)
            a3[r] = (1.0 / 3.0) * alpha[r]
        if r >= 1:
            s = base - p[r - 1] * z
            gamma[r] = pl.reciprocal(s * s, approx=APPROX)
            g3[r] = (1.0 / 3.0) * gamma[r]
        if 0 <= r <= n:
            beta[r] = pl.reciprocal(0.5 * (base * base), approx=APPROX)
    f = {m: t[m] - t[m + 1] for m in range(-1, n + 1)}
    f2 = {m: f[m] + f[m] for m in range(-1, n + 1)}
    return n, q, p, alpha, beta, gamma, a3, g3, f, f2


APPROX = True


def line_max(us, eps):
    n, q, p, alpha, beta, gamma, a3, g3, f, f2 = weno_terms(us, eps)
    q6 = {r: 6.0 * q[r] for r in range(0, n + 1)}
    outs = []
    for i in range(n):
        er = (g3[i + 2] * f2[i + 1] + alpha[i] * f[i]) * pl.reciprocal(
            g3[i + 2] + beta[i + 1] + alpha[i], approx=APPROX
        )
        el = (a3[i - 1] * f2[i - 1] + gamma[i + 1] * f[i]) * pl.reciprocal(
            a3[i - 1] + beta[i] + gamma[i + 1], approx=APPROX
        )
        p2 = p[i] + p[i]
        outs.append(jnp.minimum((p2 - q6[i + 1]) + (p[i + 1] + er), (p2 + q6[i]) + (p[i - 1] + el)))
    return outs


def line_upwind(us, eps, flows):
    n, q, p, alpha, beta, gamma, a3, g3, f, f2 = weno_terms(us, eps)
    outs = []
    for i in range(n):
        flow = flows(i)
        right = flow > 0.0
        w1 = jnp.where(right, g3[i + 2], a3[i - 1])
        w2 = jnp.where(right, beta[i + 1], beta[i])
        w3 = jnp.where(right, alpha[i], gamma[i + 1])
        f1 = jnp.where(right, f2[i + 1], f2[i - 1])
        pn = jnp.where(right, p[i + 1], p[i - 1])
        qn = jnp.where(right, q[i + 1], q[i])
        e = (w1 * f1 + w3 * f[i]) * pl.reciprocal(w1 + w2 + w3, approx=APPROX)
        x = pn + (p[i] + p[i]) + e
        outs.append(flow * qn - jnp.abs((1.0 / 6.0) * flow) * x)
    return outs


def edge_fix(low, center_low, center_high, high, flags):
    first, last = flags
    slope = center_low[0] - center_low[1]
    low = [
        jnp.where(first, center_low[0] + reach * slope, got)
        for reach, got in zip((3.0, 2.0, 1.0), low)
    ]
    slope = center_high[1] - center_high[0]
    high = [
        jnp.where(last, center_high[1] + reach * slope, got)
        for reach, got in zip((1.0, 2.0, 3.0), high)
    ]
    return low, high


def axis_flags(axis):
    count = lax.axis_size(axis)
    at = jnp.full((SUB, LANES), lax.axis_index(axis), jnp.int32)
    even = at % 2 == 0 if paired(axis) else at >= 0
    return at == 0, at == count - 1, even


def sided(even, load, a_ref, b_ref):
    from_a, from_b = load(a_ref), load(b_ref)
    low = [jnp.where(even, b, a) for a, b in zip(from_a, from_b)]
    high = [jnp.where(even, a, b) for a, b in zip(from_a, from_b)]
    return low, high


def pitch(sizes):
    _, nh, ny = sizes
    rows = nh * ny
    while rows % 8 != 4:
        rows += 1
    return rows


BLOCK = LANES // SUB
TURNED = BLOCK + 2 * SUB + 4
TERMS = BLOCK + 4


def turn(u_ref, turned_ref, h, sizes):
    nx, _, ny = sizes
    p = pitch(sizes)
    planes = nx * ny // LANES
    per = LANES // ny
    for g in range(planes):
        mat = jnp.concatenate([u_ref[pl.ds((g * per + x) * p + h * ny, ny), :] for x in range(per)], axis=0)
        mat = mat.T
        tiles = [mat[SUB * i : SUB * (i + 1)] for i in range(LANES // SUB)]
        row = lax.broadcasted_iota(jnp.int32, (SUB, LANES), 0).astype(jnp.float32)
        edge, inner = mat[0:1], mat[1:2]
        below = edge + (float(SUB) - row) * (edge - inner)
        edge, inner = mat[LANES - 1 :], mat[LANES - 2 : LANES - 1]
        above = edge + (row + 1.0) * (edge - inner)
        tiles = [below] + tiles + [above]
        base = (h * planes + g) * SUB * TURNED
        for s in range(SUB):
            for k in range(BLOCK // SUB + 2):
                turned_ref[pl.ds(base + s * TURNED + k * SUB, SUB), :] = tiles[s * (BLOCK // SUB) + k]


def speed_kernel(turned_ref, out_ref, *, eps, scale):
    groups = turned_ref.shape[0] // (SUB * TURNED)

    def group(g, carry):
        start = g * SUB * TURNED + SUB - 3
        us = [turned_ref[pl.ds(start + j, SUB, stride=TURNED), :] for j in range(BLOCK + 6)]
        for j, value in enumerate(line_max(us, eps)):
            out_ref[pl.ds(g * SUB * TERMS + j, SUB, stride=TERMS), :] = -scale * value
        return carry

    lax.fori_loop(0, groups, group, 0)


def y_kernel(u_ref, a_ref, b_ref, wind_ref, speed_ref, acc_ref, *, sizes, eps):
    nx, nh, ny = sizes
    p = pitch(sizes)
    first, last, even = axis_flags("gy")
    head = lax.axis_index("ha") * nh
    for xg in range(nx // SUB):

        def column(h, carry):
            def rows(y):
                return pl.ds(xg * SUB * p + h * ny + y, SUB, stride=p)

            center = [u_ref[rows(y), :] for y in range(ny)]

            def halo(ref, k):
                return ref[pl.ds(pl.multiple_of((k * nh + h) * nx + xg * SUB, SUB), SUB), :]

            low, high = sided(even, lambda ref: [halo(ref, k) for k in range(3)], a_ref, b_ref)
            low, high = edge_fix(low, center[:2], center[-2:], high, (first, last))
            speed = speed_ref[pl.ds(head + h, 1), :]
            flows = lambda y: speed + wind_ref[pl.ds(y * nx + xg * SUB, SUB), :]
            for y, value in enumerate(line_upwind(low + center + high, eps, flows)):
                acc_ref[rows(y), :] = value
            return carry

        lax.fori_loop(0, nh, column, 0)


def head_kernel(u_ref, a_ref, b_ref, acc_in, acc_ref, *, sizes, eps, scale):
    nx, nh, ny = sizes
    p = pitch(sizes)
    even = axis_flags("ha")[2]

    def line(x, carry):
        for yg in range(ny // SUB):

            def face(k):
                return pl.ds(pl.multiple_of((x * 3 + k) * ny + yg * SUB, SUB), SUB)

            def rows(h):
                return pl.ds(x * p + h * ny + yg * SUB, SUB)

            low, high = sided(even, lambda ref: [ref[face(k), :] for k in range(3)], a_ref, b_ref)
            us = low + [u_ref[rows(h), :] for h in range(nh)] + high
            for h, value in enumerate(line_max(us, eps)):
                acc_ref[rows(h), :] = acc_in[rows(h), :] - scale * value
        return carry

    lax.fori_loop(0, nx, line, 0)


def x_kernel(*refs, sizes, eps, stage):
    nx, nh, ny = sizes
    p = pitch(sizes)
    it = iter(refs)
    u_ref, a_ref, b_ref, wind_ref, speed_ref, acc_in, terms_ref, rate_ref = (next(it) for _ in range(8))
    first_ref = next(it) if stage > 1 else u_ref
    next_ref = next(it)
    turned_ref = next(it) if stage < 3 else None
    first, last, even = axis_flags("gx")
    head = lax.axis_index("ha") * nh
    step = CFL_NUMBER / rate_ref[...]
    planes = nx * ny // LANES
    per = LANES // ny

    def line(h, carry):
        if stage < 3:
            turn(next_ref, turned_ref, jnp.maximum(h - 1, 0), sizes)
        terms = []
        for g in range(planes):
            base = (h * planes + g) * SUB * TERMS
            mat = jnp.concatenate([terms_ref[pl.ds(base + s * TERMS, BLOCK), :] for s in range(SUB)], axis=0)
            terms.append(mat.T)
        speed = speed_ref[pl.ds(head + h, 1), :]
        for yg in range(ny // SUB):

            def rows(x):
                return pl.ds(x * p + h * ny + yg * SUB, SUB)

            def face(k):
                return pl.ds(pl.multiple_of((k * nh + h) * ny + yg * SUB, SUB), SUB)

            center = [u_ref[rows(x), :] for x in range(nx)]
            low, high = sided(even, lambda ref: [ref[face(k), :] for k in range(3)], a_ref, b_ref)
            low, high = edge_fix(low, center[:2], center[-2:], high, (first, last))
            flows = lambda x: speed + wind_ref[pl.ds(x * ny + yg * SUB, SUB), :]
            for x, value in enumerate(line_upwind(low + center + high, eps, flows)):
                at = (x % per) * ny + yg * SUB
                total = (acc_in[rows(x), :] + terms[x // per][at : at + SUB]) + value
                change = step * jnp.minimum(total, 0.0)
                if stage == 1:
                    new = center[x] + change
                elif stage == 2:
                    new = 0.75 * first_ref[rows(x), :] + 0.25 * (center[x] + change)
                else:
                    start = first_ref[rows(x), :]
                    new = (2.0 / 3.0) * ((center[x] - start) + change)
                if stage < 3:
                    next_ref[rows(x), :] = new
                else:
                    out = pl.ds(pl.multiple_of((x * nh + h) * ny + yg * SUB, SUB), SUB)
                    next_ref[out, :] = new
        return carry

    lax.fori_loop(0, nh, line, 0)
    if stage < 3:
        turn(next_ref, turned_ref, nh - 1, sizes)
        pack_faces(next_ref, list(it), sizes)


def pack_faces(u_ref, faces, sizes):
    nx, nh, ny = sizes
    p = pitch(sizes)
    xa, xb, ha, hb, ya = faces[:5]
    yb = faces[5] if len(faces) > 5 else None
    even = axis_flags("gx")[2]

    def both(a_ref, b_ref, at, low, high, even):
        a_ref[at, :] = jnp.where(even, high, low)
        if b_ref is not None:
            b_ref[at, :] = jnp.where(even, low, high)

    for k in range(3):
        for i in range(nh * ny // SUB):
            low = u_ref[pl.ds(k * p + i * SUB, SUB), :]
            high = u_ref[pl.ds((nx - 3 + k) * p + i * SUB, SUB), :]
            both(xa, xb, pl.ds(k * nh * ny + i * SUB, SUB), low, high, even)
    even_h = axis_flags("ha")[2]
    for x in range(nx):
        for k in range(3 * ny // SUB):
            low = u_ref[pl.ds(x * p + k * SUB, SUB), :]
            high = u_ref[pl.ds(x * p + (nh - 3) * ny + k * SUB, SUB), :]
            both(ha, hb, pl.ds(x * 3 * ny + k * SUB, SUB), low, high, even_h)
    even_y = axis_flags("gy")[2]
    for xg in range(nx // SUB):
        for h in range(nh):
            for k in range(3):

                def rows(y):
                    return pl.ds(xg * SUB * p + h * ny + y, SUB, stride=p)

                at = pl.ds((k * nh + h) * nx + xg * SUB, SUB)
                both(ya, yb, at, u_ref[rows(k), :], u_ref[rows(ny - 3 + k), :], even_y)


def pack_kernel(start_ref, u_ref, *rest, sizes):
    nx, nh, ny = sizes
    p = pitch(sizes)
    faces, sems = list(rest[:-1]), rest[-1]
    copies = [
        pltpu.make_async_copy(
            start_ref.at[pl.ds(x * nh * ny, nh * ny), :], u_ref.at[pl.ds(x * p, nh * ny), :], sems.at[x]
        )
        for x in range(nx)
    ]
    for copy in copies:
        copy.start()
    for copy in copies:
        copy.wait()
    pack_faces(u_ref, faces, sizes)


def turn_kernel(u_ref, turned_ref, *, sizes):
    for h in range(sizes[1]):
        turn(u_ref, turned_ref, h, sizes)


VMEM_LIMIT = 8 * 1024 * 1024
VM = pl.BlockSpec(memory_space=pltpu.VMEM)


def call(kernel, ins, outs, flops, keep=True, hbm=0, scratch=()):
    shapes = [pltpu.VMEM(s, jnp.float32) if keep else jax.ShapeDtypeStruct(s, jnp.float32) for s in outs]
    ins = [pltpu.with_memory_space_constraint(x, pltpu.HBM) for x in ins[:hbm]] + [pltpu.with_memory_space_constraint(x, pltpu.VMEM) for x in ins[hbm:]]
    return pl.pallas_call(
        kernel,
        out_shape=shapes,
        in_specs=[pl.BlockSpec(memory_space=pltpu.HBM)] * hbm + [VM] * (len(ins) - hbm),
        out_specs=[VM] * len(outs),
        scratch_shapes=list(scratch),
        compiler_params=pltpu.CompilerParams(vmem_limit_bytes=VMEM_LIMIT),
        cost_estimate=pl.CostEstimate(flops=flops, transcendentals=0, bytes_accessed=1024),
    )(*ins)


def paired(axis):
    return lax.axis_size(axis) % 2 == 0


def neighbours(face_a, face_b, axis, closed):
    count = lax.axis_size(axis)
    ends = count if closed else count - 1

    def send(face, pairs):
        return lax.ppermute(face, axis, pairs)

    if not paired(axis):
        got_b = send(face_a, [(i, (i + 1) % count) for i in range(ends)])
        got_a = send(face_b, [((i + 1) % count, i) for i in range(ends)])
        return got_a, got_b

    def swap(face, start):
        pairs = []
        for i in range(start, ends, 2):
            pairs += [(i, (i + 1) % count), ((i + 1) % count, i)]
        return send(face, pairs) if pairs else None

    got_b = swap(face_b, 1) if face_b is not None else None
    got_a = swap(face_a, 0)
    return got_a, got_a if got_b is None else got_b


def all_max(value, axes):
    for axis in axes:
        count = lax.axis_size(axis)
        if count & (count - 1):
            value = lax.pmax(value, axis)
            continue
        reach = 1
        while reach < count:
            other = lax.ppermute(value, axis, [(i, i ^ reach) for i in range(count)])
            value = jnp.maximum(value, other)
            reach *= 2
    return value


def body(level_set, wind_field):
    nx, ny, nh, nv = level_set.shape
    sizes = (nx, nh, ny)
    rows = nx * nh * ny
    n_head = nh * lax.axis_size("ha")
    d_theta = 2.0 * math.pi / n_head
    d_speed = SPEED_SPAN / nv

    angles = np.arange(n_head) * d_theta
    cosines, sines = np.cos(angles), np.sin(angles)
    speeds = SPEED_LOW + SPEED_SPAN * (np.arange(nv) + 0.5) / nv
    speed_x = jnp.asarray(cosines[:, None] * speeds / CELL_SIZE, jnp.float32)
    speed_y = jnp.asarray(sines[:, None] * speeds / CELL_SIZE, jnp.float32)

    start = level_set.transpose(0, 2, 1, 3).reshape(rows, nv)
    x_face, h_face, y_face = (3 * nh * ny, nv), (nx * 3 * ny, nv), (3 * nh * nx, nv)
    face_shapes = [x_face, x_face, h_face, h_face] + [y_face] * (1 if lax.axis_size("gy") == 2 else 2)
    padded = (nx * pitch(sizes), nv)
    groups = rows // LANES
    turned_shape, terms_shape = (groups * SUB * TURNED, LANES), (groups * SUB * TERMS, LANES)
    flops = rows * LANES * 40

    eps_g = 0.75 * WENO_EPS * CELL_SIZE**2
    eps_h = 0.75 * WENO_EPS * d_theta**2
    eps_v = 0.75 * WENO_EPS * d_speed**2

    got = call(
        functools.partial(pack_kernel, sizes=sizes),
        [start],
        [padded] + face_shapes,
        1000,
        hbm=1,
        scratch=[pltpu.SemaphoreType.DMA((nx,))],
    )
    u, faces = got[0], got[1:]
    first = u

    wind_field, *faces = lax.optimization_barrier((wind_field, *faces))
    ends = np.array([speeds[0], speeds[-1]])
    cos_ends = jnp.asarray((ends[:, None] * cosines).reshape(-1, 1, 1), jnp.float32)
    sin_ends = jnp.asarray((ends[:, None] * sines).reshape(-1, 1, 1), jnp.float32)
    top = jnp.max(
        jnp.abs(cos_ends + wind_field[0]) / CELL_SIZE + jnp.abs(sin_ends + wind_field[1]) / CELL_SIZE
    )
    top = jnp.broadcast_to(top + (TURN_MAX / d_theta + ACCEL_MAX / d_speed), (SUB, nv))
    wind = wind_field * (1.0 / CELL_SIZE)
    wind_x = jnp.broadcast_to(wind[0][:, :, None], (nx, ny, nv)).reshape(nx * ny, nv)
    wind_y = jnp.broadcast_to(wind[1].T[:, :, None], (ny, nx, nv)).reshape(ny * nx, nv)

    rate = all_max(top, ("gy", "gx"))
    for stage in (1, 2, 3):
        got_x = neighbours(faces[0], faces[1], "gx", False)
        got_h = neighbours(faces[2], faces[3], "ha", True)
        got_y = neighbours(faces[4], faces[5] if len(faces) > 5 else None, "gy", False)
        if stage == 1:
            (turned,) = call(functools.partial(turn_kernel, sizes=sizes), [u], [turned_shape], 1000)
        (terms,) = call(
            functools.partial(speed_kernel, eps=eps_v, scale=ACCEL_MAX / (6.0 * d_speed)),
            [turned],
            [terms_shape],
            flops,
        )
        (acc,) = call(
            functools.partial(y_kernel, sizes=sizes, eps=eps_g), [u, *got_y, wind_y, speed_y], [padded], flops
        )
        (acc,) = call(
            functools.partial(head_kernel, sizes=sizes, eps=eps_h, scale=TURN_MAX / (6.0 * d_theta)),
            [u, *got_h, acc],
            [padded],
            flops,
        )
        ins = [u, *got_x, wind_x, speed_x, acc, terms, rate]
        if stage > 1:
            ins.append(first)
        got = call(
            functools.partial(x_kernel, sizes=sizes, eps=eps_g, stage=stage),
            ins,
            [padded, turned_shape] + face_shapes if stage < 3 else [(rows, nv)],
            flops,
            keep=stage < 3,
        )
        if stage < 3:
            u, turned, faces = got[0], got[1], got[2:]
    return got[0].reshape(nx, nh, ny, nv).transpose(0, 2, 1, 3)


def solution(mesh):
    return jax.shard_map(
        body,
        mesh=mesh,
        in_specs=(P("gx", "gy", "ha", None), P(None, "gx", "gy")),
        out_specs=P("gx", "gy", "ha", None),
        check_vma=False,
    )
```

time: 73.7 us -> 65.6 us (0.89)
  Pallas kernels: 25.7 us -> 19.5 us
  other arithmetic: 0.72 us -> 2.16 us
  local copies, waits for them, and re-layouts: 5.34 us -> 4.06 us
  waiting for transfers between devices: 14 us -> 13.1 us
  starting transfers between devices: 26.2 us -> 25.3 us
    pallas_call x13 -> x14, Pallas kernels: 25.7 us -> 19.5 us  [call(): pl.pallas_call(kernel, out_shape=shapes, in_specs=[pl.BlockSpec(memory_sp...]
    unnamed x10 -> x12, local copies, waits for them, and re-layouts: 2.47 us -> 0.61 us
    dynamic_slice x2 -> x0, local copies, waits for them, and re-layouts: 1.43 us -> none  [flow_rows(): mine = lax.dynamic_slice_in_dim(full, head, nh, 0)]
    transpose x2, local copies, waits for them, and re-layouts: 0.07 us -> 1.33 us  [body(): wind[1].T[:, :, None]]
    ppermute x18, starting transfers between devices: 26.2 us -> 25.3 us  [the longest x15 23.7 us: send(): return lax.ppermute(face, axis, pairs)]
    ppermute x18, waiting for transfers between devices: 14 us -> 13.1 us  [the longest x15 9.27 us: send(): return lax.ppermute(face, axis, pairs)]
    reduce_max x1, other arithmetic: 0.7 us -> 1.44 us  [body(): jnp.max(jnp.abs(cos_ends + wind_field[0]) / CELL_SIZE + jnp.abs(sin_ends...]
  transfers between devices with their start and end apart: 18 -> 18, of which waited for: 4 -> 7; matrix products, arithmetic and copies ran while one was open for 3% -> 5% of each run, Pallas kernels for 27% -> 18%
where the time goes in v4:
time: 65.6 us; the launch traced here: 65 us
  starting transfers between devices  25.3 us (39%)
  Pallas kernels  19.5 us (30%)
  waiting for transfers between devices  13.1 us (20%)
  local copies, waits for them, and re-layouts  4.06 us (6%)
  other arithmetic  2.16 us (3%)
  between operations  0.9 us (1%)
    ppermute x15, starting transfers between devices, send(): return lax.ppermute(face, axis, pairs)  23.7 us
    pallas_call x14, Pallas kernels, call(): pl.pallas_call(kernel, out_shape=shapes, in_specs=[pl.BlockSpec(memory_sp...  19.5 us
    ppermute x15, waiting for transfers between devices, send(): return lax.ppermute(face, axis, pairs)  9.27 us
    ppermute x3, waiting for transfers between devices, all_max(): other = lax.ppermute(value, axis, [(i, i ^ reach) for i in range(count)])  3.84 us
    ppermute x3, starting transfers between devices, all_max(): other = lax.ppermute(value, axis, [(i, i ^ reach) for i in range(count)])  1.63 us
    reduce_max x1, other arithmetic, body(): jnp.max(jnp.abs(cos_ends + wind_field[0]) / CELL_SIZE + jnp.abs(sin_ends...  1.44 us
    transpose x2, local copies, waits for them, and re-layouts, body(): wind[1].T[:, :, None]  1.33 us
  transfers between devices with their start and end apart: 18, of which 7 were waited for; matrix products, arithmetic and copies ran while one was open for 5% of the time, Pallas kernels for 18%

profile of v4, /device:TPU:4, one launch (start us, length us, event | category | flops | bytes accessed | tf_op | source)
XLA Modules:
  0.0 65.0 jit_solution(17980421343065640224)
XLA Ops:
  0.0 2.1 %shard_map.64 = (f32[1312,128]{1,0:T(8,128)S(1)}, f32[480,128]{1,0:T(8,128)}, f32[480,128]{1,0:T(8,128)S(1)}, f32[384,128]{1,0:T(8,128)}, f32[384,128]{1,0:T(8,128)}, /*index=5*/f32[240,128]{1,0:T(8,128)S(1)}) custom-call(f32[1280,128]{1,0:T(8,128)} %bitcast.14), custom_call_target="tpu_custom_call" | custom-call | flops 1000 | bytes 1024 | tf_op jit(solution)/shard_map/pallas_call | solution.py:335
  2.1 0.7 %slice_bitcast_fusion.2 = (f32[8,16]{1,0:T(8,128)S(1)}, f32[8,16]{1,0:T(8,128)S(1)}) fusion(f32[2,8,16]{2,1,0:T(8,128)} %param.7), kind=kLoop, calls=%fused_computation.3 | loop fusion | bytes 2048 | tf_op jit(solution)/shard_map/add | solution.py:429
  2.8 1.4 %multiply_reduce_fusion = f32[]{:T(128)} fusion(f32[8,16]{1,0:T(8,128)S(1)} %get-tuple-element.58, f32[80]{0:T(128)} %constant.23, f32[8,16]{1,0:T(8,128)S(1)} %get-tuple-element.57, f32[80]{0:T(128)} %constant.22), kind=kLoop, calls=%fused_computation | loop fusion | flops 71679 | bytes 1668 | tf_op jit(solution)/shard_map/reduce_max | solution.py:428
  5.0 1.2 %collective-permute-done.5 = f32[8,128]{1,0:T(8,128)S(1)} collective-permute-done((f32[8,128]{1,0:T(8,128)S(1)}, f32[8,128]{1,0:T(8,128)S(1)}, u32[]{:S(2)}, u32[]{:S(2)}) %collective-permute-start.5) | collective-permute-done | bytes 4128 | tf_op jit(solution)/shard_map/ppermute | solution.py:381
  6.1 1.5 %collective-permute-start.6 = (f32[8,128]{1,0:T(8,128)S(1)}, f32[8,128]{1,0:T(8,128)S(1)}, u32[]{:S(2)}, u32[]{:S(2)}) collective-permute-start(f32[8,128]{1,0:T(8,128)S(1)} %broadcast_maximum_fusion), channel_id=1, source_target_pairs={{0,8},{8,0},{16,24},{24,16},{1,9},{9,1},{17,25},{25,17},{2,10},{10... | collective-permute-start | bytes 12296 | tf_op jit(solution)/shard_map/ppermute | solution.py:381
  7.6 1.6 %collective-permute-start.2 = (f32[384,128]{1,0:T(8,128)}, f32[384,128]{1,0:T(8,128)S(1)}, u32[]{:S(2)}, u32[]{:S(2)}) collective-permute-start(f32[384,128]{1,0:T(8,128)} %get-tuple-element.40), channel_id=1, source_target_pairs={{0,1},{1,0},{2,3},{3,2},{4,5},{5,4},{6,7},{7,6},{8,9},{9,8},{10,11... | collective-permute-start | bytes 589832 | tf_op jit(solution)/shard_map/ppermute | solution.py:355
  9.7 3.3 %collective-permute-start.1 = (f32[480,128]{1,0:T(8,128)S(1)}, f32[480,128]{1,0:T(8,128)S(1)}, u32[]{:S(2)}, u32[]{:S(2)}) collective-permute-start(f32[480,128]{1,0:T(8,128)S(1)} %get-tuple-element.38), channel_id=1, source_target_pairs={{8,16},{16,8},{9,17},{17,9},{10,18},{18,10},{11,19},{19,11},{12,20... | collective-permute-start | bytes 737288 | tf_op jit(solution)/shard_map/ppermute | solution.py:355
  13.2 0.7 %broadcast_multiply_fusion = f32[2,8,16]{2,1,0:T(8,128)S(1)} fusion(f32[2,8,16]{2,1,0:T(8,128)} %param.7), kind=kLoop, calls=%fused_computation.4 | loop fusion | flops 256 | bytes 2048 | tf_op jit(solution)/shard_map/mul | solution.py:432
  14.1 2.7 %collective-permute-done.7 = f32[8,128]{1,0:T(8,128)S(1)} collective-permute-done((f32[8,128]{1,0:T(8,128)S(1)}, f32[8,128]{1,0:T(8,128)S(1)}, u32[]{:S(2)}, u32[]{:S(2)}) %collective-permute-start.7) | collective-permute-done | bytes 4128 | tf_op jit(solution)/shard_map/ppermute | solution.py:381
  17.4 2.5 %collective-permute-start.3 = (f32[384,128]{1,0:T(8,128)}, f32[384,128]{1,0:T(8,128)S(1)}, u32[]{:S(2)}, u32[]{:S(2)}) collective-permute-start(f32[384,128]{1,0:T(8,128)} %get-tuple-element.41), channel_id=1, source_target_pairs={{1,2},{2,1},{3,0},{0,3},{5,6},{6,5},{7,4},{4,7},{9,10},{10,9},{11,... | collective-permute-start | bytes 589832 | tf_op jit(solution)/shard_map/ppermute | solution.py:355
  20.5 0.6 broadcast_in_dim.18
  21.1 0.7 %copy.9 = f32[16,8]{1,0:T(8,128)S(1)} copy(f32[16,8]{0,1:T(8,128)} %get-tuple-element.59) | data formatting | bytes 1024 | tf_op jit(solution)/shard_map/transpose | solution.py:434
  22.5 1.2 %shard_map.68.refs_6_ = f32[1600,128]{1,0:T(8,128)S(1)} custom-call(f32[2880,128]{1,0:T(8,128)S(1)} %shard_map.67.turned_ref), custom_call_target="tpu_custom_call" | custom-call | flops 6553600 | bytes 1024 | tf_op jit(solution)/shard_map/pallas_call | solution.py:335
  23.8 1.2 %shard_map.65.acc_in = f32[1312,128]{1,0:T(8,128)S(1)} custom-call(f32[1312,128]{1,0:T(8,128)S(1)} %get-tuple-element.31.u_ref.refs_0_.refs_8_, f32[240,128]{1,0:T(8,128)S(1)} %collective-permute-done.4.a_ref.b_ref, f32[240,128]{1,0:T(8,128)S(1)} %collective-permute-done.4.a_ref.b_ref, f32[128,128]{1,0:T(8,128)S(1)} %broadcast_in_dim.21.wind_ref, ...), custom_call_target="tpu_custom_call" | custom-call | flops 6553600 | bytes 1024 | tf_op jit(solution)/shard_map/pallas_call | solution.py:335
  25.1 1.3 %shard_map.66.refs_5_ = f32[1312,128]{1,0:T(8,128)S(1)} custom-call(f32[1312,128]{1,0:T(8,128)S(1)} %get-tuple-element.31.u_ref.refs_0_.refs_8_, f32[384,128]{1,0:T(8,128)S(1)} %collective-permute-done.2.a_ref, f32[384,128]{1,0:T(8,128)S(1)} %collective-permute-done.3.b_ref, f32[1312,128]{1,0:T(8,128)S(1)} %shard_map.65.acc_in), custom_call_target="tpu_custom_call" | custom-call | flops 6553600 | bytes 1024 | tf_op jit(solution)/shard_map/pallas_call | solution.py:335
  26.5 1.7 %shard_map.69 = (f32[1312,128]{1,0:T(8,128)S(1)}, f32[2880,128]{1,0:T(8,128)S(1)}, f32[480,128]{1,0:T(8,128)S(1)}, f32[480,128]{1,0:T(8,128)S(1)}, f32[384,128]{...) custom-call(f32[1312,128]{1,0:T(8,128)S(1)} %get-tuple-element.31.u_ref.refs_0_.refs_8_, ...), custom_call_target="tpu_custom_call" | custom-call | flops 6553600 | bytes 1024 | tf_op jit(solution)/shard_map/pallas_call | solution.py:335
  28.6 3.3 %collective-permute-start.9 = (f32[480,128]{1,0:T(8,128)S(1)}, f32[480,128]{1,0:T(8,128)S(1)}, u32[]{:S(2)}, u32[]{:S(2)}) collective-permute-start(f32[480,128]{1,0:T(8,128)S(1)} %get-tuple-element.45), channel_id=1, source_target_pairs={{8,16},{16,8},{9,17},{17,9},{10,18},{18,10},{11,19},{19,11},{12,20... | collective-permute-start | bytes 737288 | tf_op jit(solution)/shard_map/ppermute | solution.py:355
  31.9 3.8 %collective-permute-start.10 = (f32[384,128]{1,0:T(8,128)S(1)}, f32[384,128]{1,0:T(8,128)S(1)}, u32[]{:S(2)}, u32[]{:S(2)}) collective-permute-start(f32[384,128]{1,0:T(8,128)S(1)} %get-tuple-element.46), channel_id=1, source_target_pairs={{0,1},{1,0},{2,3},{3,2},{4,5},{5,4},{6,7},{7,6},{8,9},{9,8},{10,11... | collective-permute-start | bytes 589832 | tf_op jit(solution)/shard_map/ppermute | solution.py:355
  35.7 2.6 %collective-permute-start.11 = (f32[384,128]{1,0:T(8,128)S(1)}, f32[384,128]{1,0:T(8,128)S(1)}, u32[]{:S(2)}, u32[]{:S(2)}) collective-permute-start(f32[384,128]{1,0:T(8,128)S(1)} %get-tuple-element.47), channel_id=1, source_target_pairs={{1,2},{2,1},{3,0},{0,3},{5,6},{6,5},{7,4},{4,7},{9,10},{10,9},{11,... | collective-permute-start | bytes 589832 | tf_op jit(solution)/shard_map/ppermute | solution.py:355
  38.4 1.2 %shard_map.72.refs_6_ = f32[1600,128]{1,0:T(8,128)S(1)} custom-call(f32[2880,128]{1,0:T(8,128)S(1)} %get-tuple-element.49.turned_ref), custom_call_target="tpu_custom_call" | custom-call | flops 6553600 | bytes 1024 | tf_op jit(solution)/shard_map/pallas_call | solution.py:335
  39.7 1.2 %shard_map.70.acc_in = f32[1312,128]{1,0:T(8,128)S(1)} custom-call(f32[1312,128]{1,0:T(8,128)S(1)} %get-tuple-element.43.u_ref.refs_0_, f32[240,128]{1,0:T(8,128)S(1)} %collective-permute-done.12.a_ref.b_ref, f32[240,128]{1,0:T(8,128)S(1)} %collective-permute-done.12.a_ref.b_ref, f32[128,128]{1,0:T(8,128)S(1)} %broadcast_in_dim.21.wind_ref, ...), custom_call_target="tpu_custom_call" | custom-call | flops 6553600 | bytes 1024 | tf_op jit(solution)/shard_map/pallas_call | solution.py:335
  40.9 5.2 %collective-permute-done.11.b_ref = f32[384,128]{1,0:T(8,128)S(1)} collective-permute-done((f32[384,128]{1,0:T(8,128)S(1)}, f32[384,128]{1,0:T(8,128)S(1)}, u32[]{:S(2)}, u32[]{:S(2)}) %collective-permute-start.11) | collective-permute-done | bytes 196640 | tf_op jit(solution)/shard_map/ppermute | solution.py:355
  46.1 1.3 %shard_map.71.refs_5_ = f32[1312,128]{1,0:T(8,128)S(1)} custom-call(f32[1312,128]{1,0:T(8,128)S(1)} %get-tuple-element.43.u_ref.refs_0_, f32[384,128]{1,0:T(8,128)S(1)} %collective-permute-done.10.a_ref, f32[384,128]{1,0:T(8,128)S(1)} %collective-permute-done.11.b_ref, f32[1312,128]{1,0:T(8,128)S(1)} %shard_map.70.acc_in), custom_call_target="tpu_custom_call" | custom-call | flops 6553600 | bytes 1024 | tf_op jit(solution)/shard_map/pallas_call | solution.py:335
  47.4 1.8 %shard_map.73 = (f32[1312,128]{1,0:T(8,128)S(1)}, f32[2880,128]{1,0:T(8,128)S(1)}, f32[480,128]{1,0:T(8,128)S(1)}, f32[480,128]{1,0:T(8,128)S(1)}, f32[384,128]{...) custom-call(f32[1312,128]{1,0:T(8,128)S(1)} %get-tuple-element.43.u_ref.refs_0_, ...), custom_call_target="tpu_custom_call" | custom-call | flops 6553600 | bytes 1024 | tf_op jit(solution)/shard_map/pallas_call | solution.py:335
  49.2 3.4 %collective-permute-start.14 = (f32[480,128]{1,0:T(8,128)S(1)}, f32[480,128]{1,0:T(8,128)S(1)}, u32[]{:S(2)}, u32[]{:S(2)}) collective-permute-start(f32[480,128]{1,0:T(8,128)S(1)} %get-tuple-element.52), channel_id=1, source_target_pairs={{8,16},{16,8},{9,17},{17,9},{10,18},{18,10},{11,19},{19,11},{12,20... | collective-permute-start | bytes 737288 | tf_op jit(solution)/shard_map/ppermute | solution.py:355
  52.7 2.1 %collective-permute-start.16 = (f32[384,128]{1,0:T(8,128)S(1)}, f32[384,128]{1,0:T(8,128)S(1)}, u32[]{:S(2)}, u32[]{:S(2)}) collective-permute-start(f32[384,128]{1,0:T(8,128)S(1)} %get-tuple-element.54), channel_id=1, source_target_pairs={{1,2},{2,1},{3,0},{0,3},{5,6},{6,5},{7,4},{4,7},{9,10},{10,9},{11,... | collective-permute-start | bytes 589832 | tf_op jit(solution)/shard_map/ppermute | solution.py:355
  54.8 1.2 %shard_map.76.refs_6_ = f32[1600,128]{1,0:T(8,128)S(1)} custom-call(f32[2880,128]{1,0:T(8,128)S(1)} %get-tuple-element.56.turned_ref), custom_call_target="tpu_custom_call" | custom-call | flops 6553600 | bytes 1024 | tf_op jit(solution)/shard_map/pallas_call | solution.py:335
  56.2 1.2 %shard_map.74.acc_in = f32[1312,128]{1,0:T(8,128)S(1)} custom-call(f32[1312,128]{1,0:T(8,128)S(1)} %get-tuple-element.50.u_ref.refs_0_, f32[240,128]{1,0:T(8,128)S(1)} %collective-permute-done.17.a_ref.b_ref, f32[240,128]{1,0:T(8,128)S(1)} %collective-permute-done.17.a_ref.b_ref, f32[128,128]{1,0:T(8,128)S(1)} %broadcast_in_dim.21.wind_ref, ...), custom_call_target="tpu_custom_call" | custom-call | flops 6553600 | bytes 1024 | tf_op jit(solution)/shard_map/pallas_call | solution.py:335
  57.4 1.8 %collective-permute-done.15.a_ref = f32[384,128]{1,0:T(8,128)S(1)} collective-permute-done((f32[384,128]{1,0:T(8,128)S(1)}, f32[384,128]{1,0:T(8,128)S(1)}, u32[]{:S(2)}, u32[]{:S(2)}) %collective-permute-start.15) | collective-permute-done | bytes 196640 | tf_op jit(solution)/shard_map/ppermute | solution.py:355
  59.1 2.1 %collective-permute-done.16.b_ref = f32[384,128]{1,0:T(8,128)S(1)} collective-permute-done((f32[384,128]{1,0:T(8,128)S(1)}, f32[384,128]{1,0:T(8,128)S(1)}, u32[]{:S(2)}, u32[]{:S(2)}) %collective-permute-start.16) | collective-permute-done | bytes 196640 | tf_op jit(solution)/shard_map/ppermute | solution.py:355
  61.2 1.3 %shard_map.75.refs_5_ = f32[1312,128]{1,0:T(8,128)S(1)} custom-call(f32[1312,128]{1,0:T(8,128)S(1)} %get-tuple-element.50.u_ref.refs_0_, f32[384,128]{1,0:T(8,128)S(1)} %collective-permute-done.15.a_ref, f32[384,128]{1,0:T(8,128)S(1)} %collective-permute-done.16.b_ref, f32[1312,128]{1,0:T(8,128)S(1)} %shard_map.74.acc_in), custom_call_target="tpu_custom_call" | custom-call | flops 6553600 | bytes 1024 | tf_op jit(solution)/shard_map/pallas_call | solution.py:335
  62.6 2.4 %shard_map.77 = f32[1280,128]{1,0:T(8,128)} custom-call(f32[1312,128]{1,0:T(8,128)S(1)} %get-tuple-element.50.u_ref.refs_0_, f32[480,128]{1,0:T(8,128)S(1)} %collective-permute-done.13.refs_1_, f32[480,128]{1,0:T(8,128)S(1)} %collective-permute-done.14.refs_2_, f32[128,128]{1,0:T(8,128)S(1)} %broadcast_in_dim.19.refs_3_, f32[40,128]{1,0:T(8,128)S(1)} %copy-done.1, ...), custom_call_target="tpu_custom_call" | custom-call | flops 6553600 | bytes 1024 | tf_op jit(solution)/shard_map/pallas_call | solution.py:335
  (43 shorter events, 3.6 us)
Async XLA Ops:
  4.9 1.2 %collective-permute-start.5 = (f32[8,128]{1,0:T(8,128)S(1)}, f32[8,128]{1,0:T(8,128)S(1)}, u32[]{:S(2)}, u32[]{:S(2)}) collective-permute-start(f32[8,128]{1,0:T(8,128)S(1)} %broadcast_in_dim.22), channel_id=1, source_target_pairs={{0,4},{4,0},{1,5},{5,1},{2,6},{6,2},{3,7},{7,3},{8,12},{12,8},{9,1... | collective-permute-start | bytes 12296 | tf_op jit(solution)/shard_map/ppermute | solution.py:381
  6.1 6.9 %collective-permute-start.6 = (f32[8,128]{1,0:T(8,128)S(1)}, f32[8,128]{1,0:T(8,128)S(1)}, u32[]{:S(2)}, u32[]{:S(2)}) collective-permute-start(f32[8,128]{1,0:T(8,128)S(1)} %broadcast_maximum_fusion), channel_id=1, source_target_pairs={{0,8},{8,0},{16,24},{24,16},{1,9},{9,1},{17,25},{25,17},{2,10},{10... | collective-permute-start | bytes 12296 | tf_op jit(solution)/shard_map/ppermute | solution.py:381
  7.6 16.1 %collective-permute-start.4 = (f32[240,128]{1,0:T(8,128)S(1)}, f32[240,128]{1,0:T(8,128)S(1)}, u32[]{:S(2)}, u32[]{:S(2)}) collective-permute-start(f32[240,128]{1,0:T(8,128)S(1)} %get-tuple-element.42), channel_id=1, source_target_pairs={{0,4},{4,0},{1,5},{5,1},{2,6},{6,2},{3,7},{7,3},{8,12},{12,8},{9,1... | collective-permute-start | bytes 368648 | tf_op jit(solution)/shard_map/ppermute | solution.py:355
  7.6 17.4 %collective-permute-start.2 = (f32[384,128]{1,0:T(8,128)}, f32[384,128]{1,0:T(8,128)S(1)}, u32[]{:S(2)}, u32[]{:S(2)}) collective-permute-start(f32[384,128]{1,0:T(8,128)} %get-tuple-element.40), channel_id=1, source_target_pairs={{0,1},{1,0},{2,3},{3,2},{4,5},{5,4},{6,7},{7,6},{8,9},{9,8},{10,11... | collective-permute-start | bytes 589832 | tf_op jit(solution)/shard_map/ppermute | solution.py:355
  9.2 17.2 %collective-permute-start = (f32[480,128]{1,0:T(8,128)}, f32[480,128]{1,0:T(8,128)S(1)}, u32[]{:S(2)}, u32[]{:S(2)}) collective-permute-start(f32[480,128]{1,0:T(8,128)} %get-tuple-element.37), channel_id=1, source_target_pairs={{0,8},{8,0},{16,24},{24,16},{1,9},{9,1},{17,25},{25,17},{2,10},{10... | collective-permute-start | bytes 737288 | tf_op jit(solution)/shard_map/ppermute | solution.py:355
  9.7 16.7 %collective-permute-start.1 = (f32[480,128]{1,0:T(8,128)S(1)}, f32[480,128]{1,0:T(8,128)S(1)}, u32[]{:S(2)}, u32[]{:S(2)}) collective-permute-start(f32[480,128]{1,0:T(8,128)S(1)} %get-tuple-element.38), channel_id=1, source_target_pairs={{8,16},{16,8},{9,17},{17,9},{10,18},{18,10},{11,19},{19,11},{12,20... | collective-permute-start | bytes 737288 | tf_op jit(solution)/shard_map/ppermute | solution.py:355
  13.1 3.7 %collective-permute-start.7 = (f32[8,128]{1,0:T(8,128)S(1)}, f32[8,128]{1,0:T(8,128)S(1)}, u32[]{:S(2)}, u32[]{:S(2)}) collective-permute-start(f32[8,128]{1,0:T(8,128)S(1)} %fusion), channel_id=1, source_target_pairs={{0,16},{8,24},{16,0},{24,8},{1,17},{9,25},{17,1},{25,9},{2,18},{10... | collective-permute-start | bytes 12296 | tf_op jit(solution)/shard_map/ppermute | solution.py:381
  14.1 9.7 %copy-start = (f32[40,128]{1,0:T(8,128)S(1)}, f32[40,128]{1,0:T(8,128)}, u32[]{:S(2)}) copy-start(f32[40,128]{1,0:T(8,128)} %constant.18.clone.speed_ref) | copy-start | bytes 61444
  16.8 0.6 copy-start.2
  17.4 7.7 %collective-permute-start.3 = (f32[384,128]{1,0:T(8,128)}, f32[384,128]{1,0:T(8,128)S(1)}, u32[]{:S(2)}, u32[]{:S(2)}) collective-permute-start(f32[384,128]{1,0:T(8,128)} %get-tuple-element.41), channel_id=1, source_target_pairs={{1,2},{2,1},{3,0},{0,3},{5,6},{6,5},{7,4},{4,7},{9,10},{10,9},{11,... | collective-permute-start | bytes 589832 | tf_op jit(solution)/shard_map/ppermute | solution.py:355
  22.5 1.2 %copy-start.3 = (f32[8,128]{1,0:T(8,128)S(1)}, f32[8,128]{1,0:T(8,128)}, u32[]{:S(2)}) copy-start(f32[8,128]{1,0:T(8,128)} %copy-done.2) | copy-start | bytes 12292
  22.5 1.3 %copy-start.5 = (f32[128]{0:T(128)S(1)}, f32[128]{0:T(128)}, u32[]{:S(2)}) copy-start(f32[128]{0:T(128)} %broadcast_in_dim.20) | copy-start | bytes 1540
  25.0 1.4 %copy-start.4 = (f32[128]{0:T(128)S(1)}, f32[128]{0:T(128)}, u32[]{:S(2)}) copy-start(f32[128]{0:T(128)} %broadcast_in_dim.18) | copy-start | bytes 1540
  25.1 1.5 %copy-start.1 = (f32[40,128]{1,0:T(8,128)S(1)}, f32[40,128]{1,0:T(8,128)}, u32[]{:S(2)}) copy-start(f32[40,128]{1,0:T(8,128)} %constant.17.clone.refs_4_) | copy-start | bytes 61444
  28.2 19.1 %collective-permute-start.8 = (f32[480,128]{1,0:T(8,128)S(1)}, f32[480,128]{1,0:T(8,128)S(1)}, u32[]{:S(2)}, u32[]{:S(2)}) collective-permute-start(f32[480,128]{1,0:T(8,128)S(1)} %get-tuple-element.44), channel_id=1, source_target_pairs={{0,8},{8,0},{16,24},{24,16},{1,9},{9,1},{17,25},{25,17},{2,10},{10... | collective-permute-start | bytes 737288 | tf_op jit(solution)/shard_map/ppermute | solution.py:355
  28.6 18.8 %collective-permute-start.9 = (f32[480,128]{1,0:T(8,128)S(1)}, f32[480,128]{1,0:T(8,128)S(1)}, u32[]{:S(2)}, u32[]{:S(2)}) collective-permute-start(f32[480,128]{1,0:T(8,128)S(1)} %get-tuple-element.45), channel_id=1, source_target_pairs={{8,16},{16,8},{9,17},{17,9},{10,18},{18,10},{11,19},{19,11},{12,20... | collective-permute-start | bytes 737288 | tf_op jit(solution)/shard_map/ppermute | solution.py:355
  31.9 9.0 %collective-permute-start.10 = (f32[384,128]{1,0:T(8,128)S(1)}, f32[384,128]{1,0:T(8,128)S(1)}, u32[]{:S(2)}, u32[]{:S(2)}) collective-permute-start(f32[384,128]{1,0:T(8,128)S(1)} %get-tuple-element.46), channel_id=1, source_target_pairs={{0,1},{1,0},{2,3},{3,2},{4,5},{5,4},{6,7},{7,6},{8,9},{9,8},{10,11... | collective-permute-start | bytes 589832 | tf_op jit(solution)/shard_map/ppermute | solution.py:355
  35.7 10.3 %collective-permute-start.11 = (f32[384,128]{1,0:T(8,128)S(1)}, f32[384,128]{1,0:T(8,128)S(1)}, u32[]{:S(2)}, u32[]{:S(2)}) collective-permute-start(f32[384,128]{1,0:T(8,128)S(1)} %get-tuple-element.47), channel_id=1, source_target_pairs={{1,2},{2,1},{3,0},{0,3},{5,6},{6,5},{7,4},{4,7},{9,10},{10,9},{11,... | collective-permute-start | bytes 589832 | tf_op jit(solution)/shard_map/ppermute | solution.py:355
  38.3 1.3 %collective-permute-start.12 = (f32[240,128]{1,0:T(8,128)S(1)}, f32[240,128]{1,0:T(8,128)S(1)}, u32[]{:S(2)}, u32[]{:S(2)}) collective-permute-start(f32[240,128]{1,0:T(8,128)S(1)} %get-tuple-element.48), channel_id=1, source_target_pairs={{0,4},{4,0},{1,5},{5,1},{2,6},{6,2},{3,7},{7,3},{8,12},{12,8},{9,1... | collective-permute-start | bytes 368648 | tf_op jit(solution)/shard_map/ppermute | solution.py:355
  49.2 13.4 %collective-permute-start.13 = (f32[480,128]{1,0:T(8,128)S(1)}, f32[480,128]{1,0:T(8,128)S(1)}, u32[]{:S(2)}, u32[]{:S(2)}) collective-permute-start(f32[480,128]{1,0:T(8,128)S(1)} %get-tuple-element.51), channel_id=1, source_target_pairs={{0,8},{8,0},{16,24},{24,16},{1,9},{9,1},{17,25},{25,17},{2,10},{10... | collective-permute-start | bytes 737288 | tf_op jit(solution)/shard_map/ppermute | solution.py:355
  49.2 13.3 %collective-permute-start.14 = (f32[480,128]{1,0:T(8,128)S(1)}, f32[480,128]{1,0:T(8,128)S(1)}, u32[]{:S(2)}, u32[]{:S(2)}) collective-permute-start(f32[480,128]{1,0:T(8,128)S(1)} %get-tuple-element.52), channel_id=1, source_target_pairs={{8,16},{16,8},{9,17},{17,9},{10,18},{18,10},{11,19},{19,11},{12,20... | collective-permute-start | bytes 737288 | tf_op jit(solution)/shard_map/ppermute | solution.py:355
  52.6 6.5 %collective-permute-start.15 = (f32[384,128]{1,0:T(8,128)S(1)}, f32[384,128]{1,0:T(8,128)S(1)}, u32[]{:S(2)}, u32[]{:S(2)}) collective-permute-start(f32[384,128]{1,0:T(8,128)S(1)} %get-tuple-element.53), channel_id=1, source_target_pairs={{0,1},{1,0},{2,3},{3,2},{4,5},{5,4},{6,7},{7,6},{8,9},{9,8},{10,11... | collective-permute-start | bytes 589832 | tf_op jit(solution)/shard_map/ppermute | solution.py:355
  52.7 8.6 %collective-permute-start.16 = (f32[384,128]{1,0:T(8,128)S(1)}, f32[384,128]{1,0:T(8,128)S(1)}, u32[]{:S(2)}, u32[]{:S(2)}) collective-permute-start(f32[384,128]{1,0:T(8,128)S(1)} %get-tuple-element.54), channel_id=1, source_target_pairs={{1,2},{2,1},{3,0},{0,3},{5,6},{6,5},{7,4},{4,7},{9,10},{10,9},{11,... | collective-permute-start | bytes 589832 | tf_op jit(solution)/shard_map/ppermute | solution.py:355
  54.8 1.3 %collective-permute-start.17 = (f32[240,128]{1,0:T(8,128)S(1)}, f32[240,128]{1,0:T(8,128)S(1)}, u32[]{:S(2)}, u32[]{:S(2)}) collective-permute-start(f32[240,128]{1,0:T(8,128)S(1)} %get-tuple-element.55), channel_id=1, source_target_pairs={{0,4},{4,0},{1,5},{5,1},{2,6},{6,2},{3,7},{7,3},{8,12},{12,8},{9,1... | collective-permute-start | bytes 368648 | tf_op jit(solution)/shard_map/ppermute | solution.py:355

commit v5 on v4

--- a/solution.py
+++ b/solution.py
@@ -217,6 +217,13 @@
     first_ref = next(it) if stage > 1 else u_ref
     next_ref = next(it)
     turned_ref = next(it) if stage < 3 else None
+    if stage == 3:
+        done_ref, sems = next(it), next(it)
+
+        def out_copy(h):
+            at = pl.ds(pl.multiple_of(h * ny, SUB), ny)
+            return pltpu.make_async_copy(done_ref.at[:, at, :], next_ref.at[:, at, :], sems.at[h])
+
     first, last, even = axis_flags("gx")
     head = lax.axis_index("ha") * nh
     step = CFL_NUMBER / rate_ref[...]
@@ -258,28 +265,25 @@
                 if stage < 3:
                     next_ref[rows(x), :] = new
                 else:
-                    out = pl.ds(pl.multiple_of((x * nh + h) * ny + yg * SUB, SUB), SUB)
-                    next_ref[out, :] = new
+                    done_ref[x, pl.ds(pl.multiple_of(h * ny + yg * SUB, SUB), SUB), :] = new
+        if stage == 3:
+            out_copy(h).start()
         return carry
 
     lax.fori_loop(0, nh, line, 0)
-    if stage < 3:
-        turn(next_ref, turned_ref, nh - 1, sizes)
-        pack_faces(next_ref, list(it), sizes)
+    if stage == 3:
+        for h in range(nh):
+            out_copy(h).wait()
+        return
+    turn(next_ref, turned_ref, nh - 1, sizes)
+    pack_faces(next_ref, list(it), sizes)
 
 
 def pack_faces(u_ref, faces, sizes):
     nx, nh, ny = sizes
     p = pitch(sizes)
-    xa, xb, ha, hb, ya = faces[:5]
-    yb = faces[5] if len(faces) > 5 else None
+    xa, xb, ha, hb = faces[:4]
     even = axis_flags("gx")[2]
-
-    def both(a_ref, b_ref, at, low, high, even):
-        a_ref[at, :] = jnp.where(even, high, low)
-        if b_ref is not None:
-            b_ref[at, :] = jnp.where(even, low, high)
-
     for k in range(3):
         for i in range(nh * ny // SUB):
             low = u_ref[pl.ds(k * p + i * SUB, SUB), :]
@@ -291,6 +295,19 @@
             low = u_ref[pl.ds(x * p + k * SUB, SUB), :]
             high = u_ref[pl.ds(x * p + (nh - 3) * ny + k * SUB, SUB), :]
             both(ha, hb, pl.ds(x * 3 * ny + k * SUB, SUB), low, high, even_h)
+    y_faces(u_ref, faces[4:], sizes)
+
+
+def both(a_ref, b_ref, at, low, high, even):
+    a_ref[at, :] = jnp.where(even, high, low)
+    if b_ref is not None:
+        b_ref[at, :] = jnp.where(even, low, high)
+
+
+def y_faces(u_ref, faces, sizes):
+    nx, nh, ny = sizes
+    p = pitch(sizes)
+    ya, yb = faces[0], faces[1] if len(faces) > 1 else None
     even_y = axis_flags("gy")[2]
     for xg in range(nx // SUB):
         for h in range(nh):
@@ -303,25 +320,62 @@
                 both(ya, yb, at, u_ref[rows(k), :], u_ref[rows(ny - 3 + k), :], even_y)
 
 
-def pack_kernel(start_ref, u_ref, *rest, sizes):
-    nx, nh, ny = sizes
-    p = pitch(sizes)
-    faces, sems = list(rest[:-1]), rest[-1]
+def pack_kernel(start_ref, wind_ref, rate_ref, xa, xb, ha, hb, wind, sems, *, sizes, ends, rest):
+    nx, nh, ny = sizes
+    plane, count = nh * ny, iter(range(2 * nx + 3))
+
+    def copy(source, target):
+        got = pltpu.make_async_copy(source, target, sems.at[next(count)])
+        got.start()
+        return got
+
+    def side(axis, high, flip):
+        even = lax.axis_index(axis) % 2 == 0 if paired(axis) else True
+        return pl.multiple_of(jnp.where(jnp.logical_xor(even, flip), high, 0), SUB)
+
+    copies = []
+    for face, flip in ((hb, True), (ha, False)):
+        at = side("ha", (nh - 3) * ny, flip)
+        for x in range(nx):
+            source = start_ref.at[pl.ds(x * plane + at, 3 * ny), :]
+            copies.append(copy(source, face.at[pl.ds(x * 3 * ny, 3 * ny), :]))
+    for face, flip in ((xa, False), (xb, True)):
+        copies.append(copy(start_ref.at[pl.ds(side("gx", (nx - 3) * plane, flip), 3 * plane), :], face))
+    copy(wind_ref, wind).wait()
+    top = None
+    for along_x, along_y in ends:
+        rate = jnp.abs(wind[0] * (1.0 / CELL_SIZE) + along_x) + jnp.abs(wind[1] * (1.0 / CELL_SIZE) + along_y)
+        top = rate if top is None else jnp.maximum(top, rate)
+    rate_ref[...] = jnp.full(rate_ref.shape, jnp.max(top) + rest, jnp.float32)
+    for got in copies:
+        got.wait()
+
+
+def prep_kernel(start_ref, wind_ref, u_ref, turned_ref, wind_x, wind_y, *refs, sizes):
+    nx, nh, ny = sizes
+    p = pitch(sizes)
+    faces, (wind, columns, sems) = refs[:-3], refs[-3:]
     copies = [
         pltpu.make_async_copy(
             start_ref.at[pl.ds(x * nh * ny, nh * ny), :], u_ref.at[pl.ds(x * p, nh * ny), :], sems.at[x]
         )
         for x in range(nx)
     ]
+    copies.append(pltpu.make_async_copy(wind_ref, wind, sems.at[nx]))
     for copy in copies:
         copy.start()
-    for copy in copies:
+    copies[-1].wait()
+    for y in range(ny):
+        for k, table in enumerate((columns, wind_y)):
+            column = wind[k][:, y : y + 1] * (1.0 / CELL_SIZE)
+            table[pl.ds(y * nx, nx), :] = jnp.broadcast_to(column, (nx, LANES))
+    for x in range(nx):
+        for yg in range(ny // SUB):
+            wind_x[pl.ds(x * ny + yg * SUB, SUB), :] = columns[pl.ds(yg * SUB * nx + x, SUB, stride=nx), :]
+    for copy in copies[:-1]:
         copy.wait()
-    pack_faces(u_ref, faces, sizes)
-
-
-def turn_kernel(u_ref, turned_ref, *, sizes):
-    for h in range(sizes[1]):
+    y_faces(u_ref, list(faces), sizes)
+    for h in range(nh):
         turn(u_ref, turned_ref, h, sizes)
 
 
@@ -336,7 +390,7 @@
         kernel,
         out_shape=shapes,
         in_specs=[pl.BlockSpec(memory_space=pltpu.HBM)] * hbm + [VM] * (len(ins) - hbm),
-        out_specs=[VM] * len(outs),
+        out_specs=[VM if keep else pl.BlockSpec(memory_space=pltpu.HBM)] * len(outs),
         scratch_shapes=list(scratch),
         compiler_params=pltpu.CompilerParams(vmem_limit_bytes=VMEM_LIMIT),
         cost_estimate=pl.CostEstimate(flops=flops, transcendentals=0, bytes_accessed=1024),
@@ -370,17 +424,18 @@
     return got_a, got_a if got_b is None else got_b
 
 
-def all_max(value, axes):
-    for axis in axes:
+def all_max(value):
+    rounds = []
+    for axis in ("gx", "gy"):
         count = lax.axis_size(axis)
         if count & (count - 1):
             value = lax.pmax(value, axis)
-            continue
-        reach = 1
-        while reach < count:
-            other = lax.ppermute(value, axis, [(i, i ^ reach) for i in range(count)])
-            value = jnp.maximum(value, other)
-            reach *= 2
+        else:
+            rounds += [(axis, 1 << k) for k in range(count.bit_length() - 1)]
+    rounds.sort(key=lambda step: step not in (("gx", 1), ("gy", 1)))
+    for axis, reach in rounds:
+        other = lax.ppermute(value, axis, [(i, i ^ reach) for i in range(lax.axis_size(axis))])
+        value = jnp.maximum(value, other)
     return value
 
 
@@ -410,36 +465,42 @@
     eps_h = 0.75 * WENO_EPS * d_theta**2
     eps_v = 0.75 * WENO_EPS * d_speed**2
 
-    got = call(
-        functools.partial(pack_kernel, sizes=sizes),
-        [start],
-        [padded] + face_shapes,
+    ends = [
+        (float(v * c / CELL_SIZE), float(v * s / CELL_SIZE))
+        for v in (speeds[0], speeds[-1])
+        for c, s in zip(cosines, sines)
+    ]
+    copies = pltpu.SemaphoreType.DMA
+    wind_shape = wind_field.shape
+    rate, *faces = call(
+        functools.partial(
+            pack_kernel, sizes=sizes, ends=ends, rest=TURN_MAX / d_theta + ACCEL_MAX / d_speed
+        ),
+        [start, wind_field],
+        [(SUB, nv)] + face_shapes[:4],
         1000,
-        hbm=1,
-        scratch=[pltpu.SemaphoreType.DMA((nx,))],
+        hbm=2,
+        scratch=[pltpu.VMEM(wind_shape, jnp.float32), copies((2 * nx + 3,))],
     )
-    u, faces = got[0], got[1:]
+    u, turned, wind_x, wind_y, *y_face = call(
+        functools.partial(prep_kernel, sizes=sizes),
+        [start, wind_field],
+        [padded, turned_shape, (nx * ny, nv), (ny * nx, nv)] + face_shapes[4:],
+        1000,
+        hbm=2,
+        scratch=[
+            pltpu.VMEM(wind_shape, jnp.float32),
+            pltpu.VMEM((ny * nx, nv), jnp.float32),
+            copies((nx + 1,)),
+        ],
+    )
+    faces += y_face
+    rate = all_max(rate)
     first = u
-
-    wind_field, *faces = lax.optimization_barrier((wind_field, *faces))
-    ends = np.array([speeds[0], speeds[-1]])
-    cos_ends = jnp.asarray((ends[:, None] * cosines).reshape(-1, 1, 1), jnp.float32)
-    sin_ends = jnp.asarray((ends[:, None] * sines).reshape(-1, 1, 1), jnp.float32)
-    top = jnp.max(
-        jnp.abs(cos_ends + wind_field[0]) / CELL_SIZE + jnp.abs(sin_ends + wind_field[1]) / CELL_SIZE
-    )
-    top = jnp.broadcast_to(top + (TURN_MAX / d_theta + ACCEL_MAX / d_speed), (SUB, nv))
-    wind = wind_field * (1.0 / CELL_SIZE)
-    wind_x = jnp.broadcast_to(wind[0][:, :, None], (nx, ny, nv)).reshape(nx * ny, nv)
-    wind_y = jnp.broadcast_to(wind[1].T[:, :, None], (ny, nx, nv)).reshape(ny * nx, nv)
-
-    rate = all_max(top, ("gy", "gx"))
     for stage in (1, 2, 3):
         got_x = neighbours(faces[0], faces[1], "gx", False)
         got_h = neighbours(faces[2], faces[3], "ha", True)
         got_y = neighbours(faces[4], faces[5] if len(faces) > 5 else None, "gy", False)
-        if stage == 1:
-            (turned,) = call(functools.partial(turn_kernel, sizes=sizes), [u], [turned_shape], 1000)
         (terms,) = call(
             functools.partial(speed_kernel, eps=eps_v, scale=ACCEL_MAX / (6.0 * d_speed)),
             [turned],
@@ -461,9 +522,10 @@
         got = call(
             functools.partial(x_kernel, sizes=sizes, eps=eps_g, stage=stage),
             ins,
-            [padded, turned_shape] + face_shapes if stage < 3 else [(rows, nv)],
+            [padded, turned_shape] + face_shapes if stage < 3 else [(nx, nh * ny, nv)],
             flops,
             keep=stage < 3,
+            scratch=[] if stage < 3 else [pltpu.VMEM((nx, nh * ny, nv), jnp.float32), copies((nh,))],
         )
         if stage < 3:
             u, turned, faces = got[0], got[1], got[2:]

time: 65.6 us -> 63.6 us (0.970)
  local copies, waits for them, and re-layouts: 4.06 us -> 0.01 us
  waiting for transfers between devices: 13.1 us -> 16.8 us
  other arithmetic: 2.16 us -> 0.01 us
  starting transfers between devices: 25.3 us -> 26.1 us
  between operations: 0.9 us -> 0.16 us
    ppermute x3, waiting for transfers between devices: 3.84 us -> 6.09 us  [all_max(): lax.ppermute(value, axis, [(i, i ^ reach) for i in range(lax.axis_size(ax...]
    reduce_max x1 -> x0, other arithmetic: 1.44 us -> none  [body(): jnp.max(jnp.abs(cos_ends + wind_field[0]) / CELL_SIZE + jnp.abs(sin_ends...]
    ppermute x15, waiting for transfers between devices: 9.27 us -> 10.7 us  [send(): return lax.ppermute(face, axis, pairs)]
    broadcast_in_dim x5 -> x0, local copies, waits for them, and re-layouts: 1.42 us -> none  [the longest x2 0.72 us: body(): jnp.broadcast_to(wind[0][:, :, None], (nx, ny, nv)).reshape(nx * ny, nv)]
    transpose x2 -> x0, local copies, waits for them, and re-layouts: 1.33 us -> none  [body(): wind[1].T[:, :, None]]
    ppermute x15, starting transfers between devices: 23.7 us -> 24.8 us  [send(): return lax.ppermute(face, axis, pairs)]
    add x1 -> x0, local copies, waits for them, and re-layouts: 0.71 us -> none  [body(): cos_ends + wind_field[0]]
    mul x1 -> x0, other arithmetic: 0.7 us -> none  [body(): wind = wind_field * (1.0 / CELL_SIZE)]
  transfers between devices with their start and end apart: 18 -> 18, of which waited for: 7 -> 9; matrix products, arithmetic and copies ran while one was open for 5% -> 0% of each run, Pallas kernels for 18% -> 20%
where the time goes in v5:
time: 63.6 us; the launch traced here: 63 us
  starting transfers between devices  26.1 us (41%)
  Pallas kernels  20 us (31%)
  waiting for transfers between devices  16.8 us (26%)
    ppermute x15, starting transfers between devices, send(): return lax.ppermute(face, axis, pairs)  24.8 us
    pallas_call x14, Pallas kernels, call(): pl.pallas_call(kernel, out_shape=shapes, in_specs=[pl.BlockSpec(memory_sp...  20 us
    ppermute x15, waiting for transfers between devices, send(): return lax.ppermute(face, axis, pairs)  10.7 us
    ppermute x3, waiting for transfers between devices, all_max(): lax.ppermute(value, axis, [(i, i ^ reach) for i in range(lax.axis_size(ax...  6.09 us
  transfers between devices with their start and end apart: 18, of which 9 were waited for; matrix products, arithmetic and copies ran while one was open for 0% of the time, Pallas kernels for 20%

profile of v5, /device:TPU:4, one launch (start us, length us, event | category | flops | bytes accessed | tf_op | source)
XLA Modules:
  0.0 63.0 jit_solution(9384989927977288400)
XLA Ops:
  0.0 1.5 %shard_map.47 = (f32[8,128]{1,0:T(8,128)S(1)}, f32[480,128]{1,0:T(8,128)S(1)}, f32[480,128]{1,0:T(8,128)S(1)}, f32[384,128]{1,0:T(8,128)S(1)}, f32[384,128]{1,0:T(8,128)S(1)}) custom-call(f32[1280,128]{1,0:T(8,128)} %bitcast.6, f32[2,8,16]{2,1,0:T(8,128)} %wind_ref.3), custom_call_target="tpu_custom_call" | custom-call | flops 1000 | bytes 1024 | tf_op jit(solution)/shard_map/pallas_call | solution.py:389
  1.5 1.6 %collective-permute-start = (f32[480,128]{1,0:T(8,128)S(1)}, f32[480,128]{1,0:T(8,128)S(1)}, u32[]{:S(2)}, u32[]{:S(2)}) collective-permute-start(f32[480,128]{1,0:T(8,128)S(1)} %get-tuple-element.30), channel_id=1, source_target_pairs={{0,8},{8,0},{16,24},{24,16},{1,9},{9,1},{17,25},{25,17},{2,10},{10... | collective-permute-start | bytes 737288 | tf_op jit(solution)/shard_map/ppermute | solution.py:409
  3.1 1.9 %collective-permute-start.1 = (f32[480,128]{1,0:T(8,128)S(1)}, f32[480,128]{1,0:T(8,128)S(1)}, u32[]{:S(2)}, u32[]{:S(2)}) collective-permute-start(f32[480,128]{1,0:T(8,128)S(1)} %get-tuple-element.31), channel_id=1, source_target_pairs={{8,16},{16,8},{9,17},{17,9},{10,18},{18,10},{11,19},{19,11},{12,20... | collective-permute-start | bytes 737288 | tf_op jit(solution)/shard_map/ppermute | solution.py:409
  5.0 2.1 %collective-permute-start.2 = (f32[384,128]{1,0:T(8,128)S(1)}, f32[384,128]{1,0:T(8,128)S(1)}, u32[]{:S(2)}, u32[]{:S(2)}) collective-permute-start(f32[384,128]{1,0:T(8,128)S(1)} %get-tuple-element.33), channel_id=1, source_target_pairs={{0,1},{1,0},{2,3},{3,2},{4,5},{5,4},{6,7},{7,6},{8,9},{9,8},{10,11... | collective-permute-start | bytes 589832 | tf_op jit(solution)/shard_map/ppermute | solution.py:409
  7.1 2.5 %collective-permute-start.3 = (f32[384,128]{1,0:T(8,128)S(1)}, f32[384,128]{1,0:T(8,128)S(1)}, u32[]{:S(2)}, u32[]{:S(2)}) collective-permute-start(f32[384,128]{1,0:T(8,128)S(1)} %get-tuple-element.34), channel_id=1, source_target_pairs={{1,2},{2,1},{3,0},{0,3},{5,6},{6,5},{7,4},{4,7},{9,10},{10,9},{11,... | collective-permute-start | bytes 589832 | tf_op jit(solution)/shard_map/ppermute | solution.py:409
  9.6 4.1 %collective-permute-done.5 = f32[8,128]{1,0:T(8,128)S(1)} collective-permute-done((f32[8,128]{1,0:T(8,128)S(1)}, f32[8,128]{1,0:T(8,128)S(1)}, u32[]{:S(2)}, u32[]{:S(2)}) %collective-permute-start.5) | collective-permute-done | bytes 4128 | tf_op jit(solution)/shard_map/ppermute | solution.py:437
  13.6 1.2 %collective-permute-done.6 = f32[8,128]{1,0:T(8,128)S(1)} collective-permute-done((f32[8,128]{1,0:T(8,128)S(1)}, f32[8,128]{1,0:T(8,128)S(1)}, u32[]{:S(2)}, u32[]{:S(2)}) %collective-permute-start.6) | collective-permute-done | bytes 4128 | tf_op jit(solution)/shard_map/ppermute | solution.py:437
  14.8 1.2 %collective-permute-start.7 = (f32[8,128]{1,0:T(8,128)S(1)}, f32[8,128]{1,0:T(8,128)S(1)}, u32[]{:S(2)}, u32[]{:S(2)}) collective-permute-start(f32[8,128]{1,0:T(8,128)S(1)} %max.10), channel_id=1, source_target_pairs={{0,16},{8,24},{16,0},{24,8},{1,17},{9,25},{17,1},{25,9},{2,18},{10... | collective-permute-start | bytes 12296 | tf_op jit(solution)/shard_map/ppermute | solution.py:437
  16.1 1.5 %shard_map.46 = (f32[1312,128]{1,0:T(8,128)S(1)}, f32[2880,128]{1,0:T(8,128)S(1)}, f32[128,128]{1,0:T(8,128)S(1)}, f32[128,128]{1,0:T(8,128)S(1)}, f32[240,128]{1,0:T(8,128)S(1)}) custom-call(f32[1280,128]{1,0:T(8,128)} %bitcast.7, f32[2,8,16]{2,1,0:T(8,128)} %wind_ref.3), custom_call_target="tpu_custom_call" | custom-call | flops 1000 | bytes 1024 | tf_op jit(solution)/shard_map/pallas_call | solution.py:389
  17.6 0.9 %collective-permute-done.7 = f32[8,128]{1,0:T(8,128)S(1)} collective-permute-done((f32[8,128]{1,0:T(8,128)S(1)}, f32[8,128]{1,0:T(8,128)S(1)}, u32[]{:S(2)}, u32[]{:S(2)}) %collective-permute-start.7) | collective-permute-done | bytes 4128 | tf_op jit(solution)/shard_map/ppermute | solution.py:437
  18.4 1.2 %shard_map.50.refs_6_ = f32[1600,128]{1,0:T(8,128)S(1)} custom-call(f32[2880,128]{1,0:T(8,128)S(1)} %get-tuple-element.37.turned_ref), custom_call_target="tpu_custom_call" | custom-call | flops 6553600 | bytes 1024 | tf_op jit(solution)/shard_map/pallas_call | solution.py:389
  19.8 1.2 %shard_map.48.acc_in = f32[1312,128]{1,0:T(8,128)S(1)} custom-call(f32[1312,128]{1,0:T(8,128)S(1)} %get-tuple-element.29.u_ref.refs_0_.refs_8_, f32[240,128]{1,0:T(8,128)S(1)} %collective-permute-done.4.a_ref.b_ref, f32[240,128]{1,0:T(8,128)S(1)} %collective-permute-done.4.a_ref.b_ref, f32[128,128]{1,0:T(8,128)S(1)} %get-tuple-element.36.wind_ref, ...), custom_call_target="tpu_custom_call" | custom-call | flops 6553600 | bytes 1024 | tf_op jit(solution)/shard_map/pallas_call | solution.py:389
  21.0 1.3 %shard_map.49.refs_5_ = f32[1312,128]{1,0:T(8,128)S(1)} custom-call(f32[1312,128]{1,0:T(8,128)S(1)} %get-tuple-element.29.u_ref.refs_0_.refs_8_, f32[384,128]{1,0:T(8,128)S(1)} %collective-permute-done.2.a_ref, f32[384,128]{1,0:T(8,128)S(1)} %collective-permute-done.3.b_ref, f32[1312,128]{1,0:T(8,128)S(1)} %shard_map.48.acc_in), custom_call_target="tpu_custom_call" | custom-call | flops 6553600 | bytes 1024 | tf_op jit(solution)/shard_map/pallas_call | solution.py:389
  22.3 1.7 %shard_map.51 = (f32[1312,128]{1,0:T(8,128)S(1)}, f32[2880,128]{1,0:T(8,128)S(1)}, f32[480,128]{1,0:T(8,128)S(1)}, f32[480,128]{1,0:T(8,128)S(1)}, f32[384,128]{...) custom-call(f32[1312,128]{1,0:T(8,128)S(1)} %get-tuple-element.29.u_ref.refs_0_.refs_8_, ...), custom_call_target="tpu_custom_call" | custom-call | flops 6553600 | bytes 1024 | tf_op jit(solution)/shard_map/pallas_call | solution.py:389
  24.1 2.5 %collective-permute-start.8 = (f32[480,128]{1,0:T(8,128)S(1)}, f32[480,128]{1,0:T(8,128)S(1)}, u32[]{:S(2)}, u32[]{:S(2)}) collective-permute-start(f32[480,128]{1,0:T(8,128)S(1)} %get-tuple-element.40), channel_id=1, source_target_pairs={{0,8},{8,0},{16,24},{24,16},{1,9},{9,1},{17,25},{25,17},{2,10},{10... | collective-permute-start | bytes 737288 | tf_op jit(solution)/shard_map/ppermute | solution.py:409
  26.6 2.1 %collective-permute-start.9 = (f32[480,128]{1,0:T(8,128)S(1)}, f32[480,128]{1,0:T(8,128)S(1)}, u32[]{:S(2)}, u32[]{:S(2)}) collective-permute-start(f32[480,128]{1,0:T(8,128)S(1)} %get-tuple-element.41), channel_id=1, source_target_pairs={{8,16},{16,8},{9,17},{17,9},{10,18},{18,10},{11,19},{19,11},{12,20... | collective-permute-start | bytes 737288 | tf_op jit(solution)/shard_map/ppermute | solution.py:409
  28.7 1.9 %collective-permute-start.10 = (f32[384,128]{1,0:T(8,128)S(1)}, f32[384,128]{1,0:T(8,128)S(1)}, u32[]{:S(2)}, u32[]{:S(2)}) collective-permute-start(f32[384,128]{1,0:T(8,128)S(1)} %get-tuple-element.42), channel_id=1, source_target_pairs={{0,1},{1,0},{2,3},{3,2},{4,5},{5,4},{6,7},{7,6},{8,9},{9,8},{10,11... | collective-permute-start | bytes 589832 | tf_op jit(solution)/shard_map/ppermute | solution.py:409
  30.6 2.5 %collective-permute-start.11 = (f32[384,128]{1,0:T(8,128)S(1)}, f32[384,128]{1,0:T(8,128)S(1)}, u32[]{:S(2)}, u32[]{:S(2)}) collective-permute-start(f32[384,128]{1,0:T(8,128)S(1)} %get-tuple-element.43), channel_id=1, source_target_pairs={{1,2},{2,1},{3,0},{0,3},{5,6},{6,5},{7,4},{4,7},{9,10},{10,9},{11,... | collective-permute-start | bytes 589832 | tf_op jit(solution)/shard_map/ppermute | solution.py:409
  33.1 1.2 %shard_map.54.refs_6_ = f32[1600,128]{1,0:T(8,128)S(1)} custom-call(f32[2880,128]{1,0:T(8,128)S(1)} %get-tuple-element.45.turned_ref), custom_call_target="tpu_custom_call" | custom-call | flops 6553600 | bytes 1024 | tf_op jit(solution)/shard_map/pallas_call | solution.py:389
  34.4 1.2 %shard_map.52.acc_in = f32[1312,128]{1,0:T(8,128)S(1)} custom-call(f32[1312,128]{1,0:T(8,128)S(1)} %get-tuple-element.39.u_ref.refs_0_, f32[240,128]{1,0:T(8,128)S(1)} %collective-permute-done.12.a_ref.b_ref, f32[240,128]{1,0:T(8,128)S(1)} %collective-permute-done.12.a_ref.b_ref, f32[128,128]{1,0:T(8,128)S(1)} %get-tuple-element.36.wind_ref, ...), custom_call_target="tpu_custom_call" | custom-call | flops 6553600 | bytes 1024 | tf_op jit(solution)/shard_map/pallas_call | solution.py:389
  35.6 0.3 collective-permute-done.10.a_ref
  35.9 6.2 %collective-permute-done.11.b_ref = f32[384,128]{1,0:T(8,128)S(1)} collective-permute-done((f32[384,128]{1,0:T(8,128)S(1)}, f32[384,128]{1,0:T(8,128)S(1)}, u32[]{:S(2)}, u32[]{:S(2)}) %collective-permute-start.11) | collective-permute-done | bytes 196640 | tf_op jit(solution)/shard_map/ppermute | solution.py:409
  42.1 1.3 %shard_map.53.refs_5_ = f32[1312,128]{1,0:T(8,128)S(1)} custom-call(f32[1312,128]{1,0:T(8,128)S(1)} %get-tuple-element.39.u_ref.refs_0_, f32[384,128]{1,0:T(8,128)S(1)} %collective-permute-done.10.a_ref, f32[384,128]{1,0:T(8,128)S(1)} %collective-permute-done.11.b_ref, f32[1312,128]{1,0:T(8,128)S(1)} %shard_map.52.acc_in), custom_call_target="tpu_custom_call" | custom-call | flops 6553600 | bytes 1024 | tf_op jit(solution)/shard_map/pallas_call | solution.py:389
  43.4 1.8 %shard_map.55 = (f32[1312,128]{1,0:T(8,128)S(1)}, f32[2880,128]{1,0:T(8,128)S(1)}, f32[480,128]{1,0:T(8,128)S(1)}, f32[480,128]{1,0:T(8,128)S(1)}, f32[384,128]{...) custom-call(f32[1312,128]{1,0:T(8,128)S(1)} %get-tuple-element.39.u_ref.refs_0_, ...), custom_call_target="tpu_custom_call" | custom-call | flops 6553600 | bytes 1024 | tf_op jit(solution)/shard_map/pallas_call | solution.py:389
  45.3 4.4 %collective-permute-start.14 = (f32[480,128]{1,0:T(8,128)S(1)}, f32[480,128]{1,0:T(8,128)S(1)}, u32[]{:S(2)}, u32[]{:S(2)}) collective-permute-start(f32[480,128]{1,0:T(8,128)S(1)} %get-tuple-element.48), channel_id=1, source_target_pairs={{8,16},{16,8},{9,17},{17,9},{10,18},{18,10},{11,19},{19,11},{12,20... | collective-permute-start | bytes 737288 | tf_op jit(solution)/shard_map/ppermute | solution.py:409
  49.6 0.6 %collective-permute-start.15 = (f32[384,128]{1,0:T(8,128)S(1)}, f32[384,128]{1,0:T(8,128)S(1)}, u32[]{:S(2)}, u32[]{:S(2)}) collective-permute-start(f32[384,128]{1,0:T(8,128)S(1)} %get-tuple-element.49), channel_id=1, source_target_pairs={{0,1},{1,0},{2,3},{3,2},{4,5},{5,4},{6,7},{7,6},{8,9},{9,8},{10,11... | collective-permute-start | bytes 589832 | tf_op jit(solution)/shard_map/ppermute | solution.py:409
  50.3 2.6 %collective-permute-start.16 = (f32[384,128]{1,0:T(8,128)S(1)}, f32[384,128]{1,0:T(8,128)S(1)}, u32[]{:S(2)}, u32[]{:S(2)}) collective-permute-start(f32[384,128]{1,0:T(8,128)S(1)} %get-tuple-element.50), channel_id=1, source_target_pairs={{1,2},{2,1},{3,0},{0,3},{5,6},{6,5},{7,4},{4,7},{9,10},{10,9},{11,... | collective-permute-start | bytes 589832 | tf_op jit(solution)/shard_map/ppermute | solution.py:409
  52.9 1.2 %shard_map.58.refs_6_ = f32[1600,128]{1,0:T(8,128)S(1)} custom-call(f32[2880,128]{1,0:T(8,128)S(1)} %get-tuple-element.52.turned_ref), custom_call_target="tpu_custom_call" | custom-call | flops 6553600 | bytes 1024 | tf_op jit(solution)/shard_map/pallas_call | solution.py:389
  54.2 1.2 %shard_map.56.acc_in = f32[1312,128]{1,0:T(8,128)S(1)} custom-call(f32[1312,128]{1,0:T(8,128)S(1)} %get-tuple-element.46.u_ref.refs_0_, f32[240,128]{1,0:T(8,128)S(1)} %collective-permute-done.17.a_ref.b_ref, f32[240,128]{1,0:T(8,128)S(1)} %collective-permute-done.17.a_ref.b_ref, f32[128,128]{1,0:T(8,128)S(1)} %get-tuple-element.36.wind_ref, ...), custom_call_target="tpu_custom_call" | custom-call | flops 6553600 | bytes 1024 | tf_op jit(solution)/shard_map/pallas_call | solution.py:389
  55.4 4.0 %collective-permute-done.15.a_ref = f32[384,128]{1,0:T(8,128)S(1)} collective-permute-done((f32[384,128]{1,0:T(8,128)S(1)}, f32[384,128]{1,0:T(8,128)S(1)}, u32[]{:S(2)}, u32[]{:S(2)}) %collective-permute-start.15) | collective-permute-done | bytes 196640 | tf_op jit(solution)/shard_map/ppermute | solution.py:409
  59.4 1.3 %shard_map.57.refs_5_ = f32[1312,128]{1,0:T(8,128)S(1)} custom-call(f32[1312,128]{1,0:T(8,128)S(1)} %get-tuple-element.46.u_ref.refs_0_, f32[384,128]{1,0:T(8,128)S(1)} %collective-permute-done.15.a_ref, f32[384,128]{1,0:T(8,128)S(1)} %collective-permute-done.16.b_ref, f32[1312,128]{1,0:T(8,128)S(1)} %shard_map.56.acc_in), custom_call_target="tpu_custom_call" | custom-call | flops 6553600 | bytes 1024 | tf_op jit(solution)/shard_map/pallas_call | solution.py:389
  60.7 2.3 %shard_map.59 = f32[8,160,128]{2,1,0:T(8,128)} custom-call(f32[1312,128]{1,0:T(8,128)S(1)} %get-tuple-element.46.u_ref.refs_0_, f32[480,128]{1,0:T(8,128)S(1)} %collective-permute-done.13.refs_1_, f32[480,128]{1,0:T(8,128)S(1)} %collective-permute-done.14.refs_2_, f32[128,128]{1,0:T(8,128)S(1)} %get-tuple-element.32.refs_3_, f32[40,128]{1,0:T(8,128)S(1)} %copy-done.1, ...), custom_call_target="tpu_custom_call" | custom-call | flops 6553600 | bytes 1024 | tf_op jit(solution)/shard_map/pallas_call | solution.py:389
  (25 shorter events, 0.4 us)
Async XLA Ops:
  1.5 20.8 %collective-permute-start = (f32[480,128]{1,0:T(8,128)S(1)}, f32[480,128]{1,0:T(8,128)S(1)}, u32[]{:S(2)}, u32[]{:S(2)}) collective-permute-start(f32[480,128]{1,0:T(8,128)S(1)} %get-tuple-element.30), channel_id=1, source_target_pairs={{0,8},{8,0},{16,24},{24,16},{1,9},{9,1},{17,25},{25,17},{2,10},{10... | collective-permute-start | bytes 737288 | tf_op jit(solution)/shard_map/ppermute | solution.py:409
  3.1 19.3 %collective-permute-start.1 = (f32[480,128]{1,0:T(8,128)S(1)}, f32[480,128]{1,0:T(8,128)S(1)}, u32[]{:S(2)}, u32[]{:S(2)}) collective-permute-start(f32[480,128]{1,0:T(8,128)S(1)} %get-tuple-element.31), channel_id=1, source_target_pairs={{8,16},{16,8},{9,17},{17,9},{10,18},{18,10},{11,19},{19,11},{12,20... | collective-permute-start | bytes 737288 | tf_op jit(solution)/shard_map/ppermute | solution.py:409
  5.0 16.0 %collective-permute-start.2 = (f32[384,128]{1,0:T(8,128)S(1)}, f32[384,128]{1,0:T(8,128)S(1)}, u32[]{:S(2)}, u32[]{:S(2)}) collective-permute-start(f32[384,128]{1,0:T(8,128)S(1)} %get-tuple-element.33), channel_id=1, source_target_pairs={{0,1},{1,0},{2,3},{3,2},{4,5},{5,4},{6,7},{7,6},{8,9},{9,8},{10,11... | collective-permute-start | bytes 589832 | tf_op jit(solution)/shard_map/ppermute | solution.py:409
  7.1 13.9 %collective-permute-start.3 = (f32[384,128]{1,0:T(8,128)S(1)}, f32[384,128]{1,0:T(8,128)S(1)}, u32[]{:S(2)}, u32[]{:S(2)}) collective-permute-start(f32[384,128]{1,0:T(8,128)S(1)} %get-tuple-element.34), channel_id=1, source_target_pairs={{1,2},{2,1},{3,0},{0,3},{5,6},{6,5},{7,4},{4,7},{9,10},{10,9},{11,... | collective-permute-start | bytes 589832 | tf_op jit(solution)/shard_map/ppermute | solution.py:409
  9.6 4.1 %collective-permute-start.5 = (f32[8,128]{1,0:T(8,128)S(1)}, f32[8,128]{1,0:T(8,128)S(1)}, u32[]{:S(2)}, u32[]{:S(2)}) collective-permute-start(f32[8,128]{1,0:T(8,128)S(1)} %get-tuple-element.38), channel_id=1, source_target_pairs={{0,8},{8,0},{16,24},{24,16},{1,9},{9,1},{17,25},{25,17},{2,10},{10... | collective-permute-start | bytes 12296 | tf_op jit(solution)/shard_map/ppermute | solution.py:437
  13.6 1.2 %collective-permute-start.6 = (f32[8,128]{1,0:T(8,128)S(1)}, f32[8,128]{1,0:T(8,128)S(1)}, u32[]{:S(2)}, u32[]{:S(2)}) collective-permute-start(f32[8,128]{1,0:T(8,128)S(1)} %max.9), channel_id=1, source_target_pairs={{0,4},{4,0},{1,5},{5,1},{2,6},{6,2},{3,7},{7,3},{8,12},{12,8},{9,1... | collective-permute-start | bytes 12296 | tf_op jit(solution)/shard_map/ppermute | solution.py:437
  14.8 4.9 %copy-start = (f32[40,128]{1,0:T(8,128)S(1)}, f32[40,128]{1,0:T(8,128)}, u32[]{:S(2)}) copy-start(f32[40,128]{1,0:T(8,128)} %constant.5.clone.speed_ref) | copy-start | bytes 61444
  14.8 3.6 %collective-permute-start.7 = (f32[8,128]{1,0:T(8,128)S(1)}, f32[8,128]{1,0:T(8,128)S(1)}, u32[]{:S(2)}, u32[]{:S(2)}) collective-permute-start(f32[8,128]{1,0:T(8,128)S(1)} %max.10), channel_id=1, source_target_pairs={{0,16},{8,24},{16,0},{24,8},{1,17},{9,25},{17,1},{25,9},{2,18},{10... | collective-permute-start | bytes 12296 | tf_op jit(solution)/shard_map/ppermute | solution.py:437
  18.4 1.3 %collective-permute-start.4 = (f32[240,128]{1,0:T(8,128)S(1)}, f32[240,128]{1,0:T(8,128)S(1)}, u32[]{:S(2)}, u32[]{:S(2)}) collective-permute-start(f32[240,128]{1,0:T(8,128)S(1)} %get-tuple-element.35), channel_id=1, source_target_pairs={{0,4},{4,0},{1,5},{5,1},{2,6},{6,2},{3,7},{7,3},{8,12},{12,8},{9,1... | collective-permute-start | bytes 368648 | tf_op jit(solution)/shard_map/ppermute | solution.py:409
  21.0 1.4 %copy-start.1 = (f32[40,128]{1,0:T(8,128)S(1)}, f32[40,128]{1,0:T(8,128)}, u32[]{:S(2)}) copy-start(f32[40,128]{1,0:T(8,128)} %constant.4.clone.refs_4_) | copy-start | bytes 61444
  24.1 19.3 %collective-permute-start.8 = (f32[480,128]{1,0:T(8,128)S(1)}, f32[480,128]{1,0:T(8,128)S(1)}, u32[]{:S(2)}, u32[]{:S(2)}) collective-permute-start(f32[480,128]{1,0:T(8,128)S(1)} %get-tuple-element.40), channel_id=1, source_target_pairs={{0,8},{8,0},{16,24},{24,16},{1,9},{9,1},{17,25},{25,17},{2,10},{10... | collective-permute-start | bytes 737288 | tf_op jit(solution)/shard_map/ppermute | solution.py:409
  26.6 16.8 %collective-permute-start.9 = (f32[480,128]{1,0:T(8,128)S(1)}, f32[480,128]{1,0:T(8,128)S(1)}, u32[]{:S(2)}, u32[]{:S(2)}) collective-permute-start(f32[480,128]{1,0:T(8,128)S(1)} %get-tuple-element.41), channel_id=1, source_target_pairs={{8,16},{16,8},{9,17},{17,9},{10,18},{18,10},{11,19},{19,11},{12,20... | collective-permute-start | bytes 737288 | tf_op jit(solution)/shard_map/ppermute | solution.py:409
  28.7 7.2 %collective-permute-start.10 = (f32[384,128]{1,0:T(8,128)S(1)}, f32[384,128]{1,0:T(8,128)S(1)}, u32[]{:S(2)}, u32[]{:S(2)}) collective-permute-start(f32[384,128]{1,0:T(8,128)S(1)} %get-tuple-element.42), channel_id=1, source_target_pairs={{0,1},{1,0},{2,3},{3,2},{4,5},{5,4},{6,7},{7,6},{8,9},{9,8},{10,11... | collective-permute-start | bytes 589832 | tf_op jit(solution)/shard_map/ppermute | solution.py:409
  30.6 11.5 %collective-permute-start.11 = (f32[384,128]{1,0:T(8,128)S(1)}, f32[384,128]{1,0:T(8,128)S(1)}, u32[]{:S(2)}, u32[]{:S(2)}) collective-permute-start(f32[384,128]{1,0:T(8,128)S(1)} %get-tuple-element.43), channel_id=1, source_target_pairs={{1,2},{2,1},{3,0},{0,3},{5,6},{6,5},{7,4},{4,7},{9,10},{10,9},{11,... | collective-permute-start | bytes 589832 | tf_op jit(solution)/shard_map/ppermute | solution.py:409
  33.1 1.3 %collective-permute-start.12 = (f32[240,128]{1,0:T(8,128)S(1)}, f32[240,128]{1,0:T(8,128)S(1)}, u32[]{:S(2)}, u32[]{:S(2)}) collective-permute-start(f32[240,128]{1,0:T(8,128)S(1)} %get-tuple-element.44), channel_id=1, source_target_pairs={{0,4},{4,0},{1,5},{5,1},{2,6},{6,2},{3,7},{7,3},{8,12},{12,8},{9,1... | collective-permute-start | bytes 368648 | tf_op jit(solution)/shard_map/ppermute | solution.py:409
  45.2 15.5 %collective-permute-start.13 = (f32[480,128]{1,0:T(8,128)S(1)}, f32[480,128]{1,0:T(8,128)S(1)}, u32[]{:S(2)}, u32[]{:S(2)}) collective-permute-start(f32[480,128]{1,0:T(8,128)S(1)} %get-tuple-element.47), channel_id=1, source_target_pairs={{0,8},{8,0},{16,24},{24,16},{1,9},{9,1},{17,25},{25,17},{2,10},{10... | collective-permute-start | bytes 737288 | tf_op jit(solution)/shard_map/ppermute | solution.py:409
  45.3 15.5 %collective-permute-start.14 = (f32[480,128]{1,0:T(8,128)S(1)}, f32[480,128]{1,0:T(8,128)S(1)}, u32[]{:S(2)}, u32[]{:S(2)}) collective-permute-start(f32[480,128]{1,0:T(8,128)S(1)} %get-tuple-element.48), channel_id=1, source_target_pairs={{8,16},{16,8},{9,17},{17,9},{10,18},{18,10},{11,19},{19,11},{12,20... | collective-permute-start | bytes 737288 | tf_op jit(solution)/shard_map/ppermute | solution.py:409
  49.6 9.8 %collective-permute-start.15 = (f32[384,128]{1,0:T(8,128)S(1)}, f32[384,128]{1,0:T(8,128)S(1)}, u32[]{:S(2)}, u32[]{:S(2)}) collective-permute-start(f32[384,128]{1,0:T(8,128)S(1)} %get-tuple-element.49), channel_id=1, source_target_pairs={{0,1},{1,0},{2,3},{3,2},{4,5},{5,4},{6,7},{7,6},{8,9},{9,8},{10,11... | collective-permute-start | bytes 589832 | tf_op jit(solution)/shard_map/ppermute | solution.py:409
  50.3 9.1 %collective-permute-start.16 = (f32[384,128]{1,0:T(8,128)S(1)}, f32[384,128]{1,0:T(8,128)S(1)}, u32[]{:S(2)}, u32[]{:S(2)}) collective-permute-start(f32[384,128]{1,0:T(8,128)S(1)} %get-tuple-element.50), channel_id=1, source_target_pairs={{1,2},{2,1},{3,0},{0,3},{5,6},{6,5},{7,4},{4,7},{9,10},{10,9},{11,... | collective-permute-start | bytes 589832 | tf_op jit(solution)/shard_map/ppermute | solution.py:409
  52.9 1.3 %collective-permute-start.17 = (f32[240,128]{1,0:T(8,128)S(1)}, f32[240,128]{1,0:T(8,128)S(1)}, u32[]{:S(2)}, u32[]{:S(2)}) collective-permute-start(f32[240,128]{1,0:T(8,128)S(1)} %get-tuple-element.51), channel_id=1, source_target_pairs={{0,4},{4,0},{1,5},{5,1},{2,6},{6,2},{3,7},{7,3},{8,12},{12,8},{9,1... | collective-permute-start | bytes 368648 | tf_op jit(solution)/shard_map/ppermute | solution.py:409

commit v6 on v5

--- a/solution.py
+++ b/solution.py
@@ -186,34 +186,105 @@
         lax.fori_loop(0, nh, column, 0)
 
 
-def head_kernel(u_ref, a_ref, b_ref, acc_in, acc_ref, *, sizes, eps, scale):
-    nx, nh, ny = sizes
-    p = pitch(sizes)
-    even = axis_flags("ha")[2]
-
-    def line(x, carry):
-        for yg in range(ny // SUB):
-
-            def face(k):
-                return pl.ds(pl.multiple_of((x * 3 + k) * ny + yg * SUB, SUB), SUB)
-
-            def rows(h):
-                return pl.ds(x * p + h * ny + yg * SUB, SUB)
-
-            low, high = sided(even, lambda ref: [ref[face(k), :] for k in range(3)], a_ref, b_ref)
-            us = low + [u_ref[rows(h), :] for h in range(nh)] + high
-            for h, value in enumerate(line_max(us, eps)):
-                acc_ref[rows(h), :] = acc_in[rows(h), :] - scale * value
-        return carry
-
-    lax.fori_loop(0, nx, line, 0)
+def is_even(axis):
+    return lax.axis_index(axis) % 2 == 0 if paired(axis) else None
+
+
+def by_parity(even, up_when_even, run):
+    if even is None:
+        run(up_when_even)
+        return
+    pl.when(even)(lambda: run(up_when_even))
+    pl.when(jnp.logical_not(even))(lambda: run(not up_when_even))
+
+
+def end_line(center, face, up, edge=None):
+    inside = list(center) if up else list(center)[::-1]
+    beyond = list(face) if up else list(face)[::-1]
+    if edge is not None:
+        slope = inside[-1] - inside[-2]
+        beyond = [jnp.where(edge, inside[-1] + reach * slope, got) for reach, got in zip((1.0, 2.0, 3.0), beyond)]
+    return inside + beyond
+
+
+def head_kernel(u_ref, face_ref, acc_in, acc_ref, *, sizes, eps, scale, face_a):
+    nx, nh, ny = sizes
+    p = pitch(sizes)
+    half = nh // 2
+
+    def run(up):
+        cells = range(half, nh) if up else range(half - 1, -1, -1)
+
+        def line(x, carry):
+            for yg in range(ny // SUB):
+
+                def face(k):
+                    return pl.ds(pl.multiple_of((x * 3 + k) * ny + yg * SUB, SUB), SUB)
+
+                def rows(h):
+                    return pl.ds(x * p + h * ny + yg * SUB, SUB)
+
+                keep = range(half - 3, nh) if up else range(half + 3)
+                inside = [u_ref[rows(h), :] for h in keep]
+                us = end_line(inside, [face_ref[face(k), :] for k in range(3)], up)
+                for h, value in zip(cells, line_max(us, eps)):
+                    acc_ref[rows(h), :] = acc_in[rows(h), :] - scale * value
+            return carry
+
+        lax.fori_loop(0, nx, line, 0)
+
+    by_parity(is_even("ha"), face_a, run)
+
+
+def edge_mask(up):
+    first, last, _ = axis_flags("gx")
+    return last if up else first
+
+
+def x_half(center, face, edge, up, eps, flows):
+    nx = len(center)
+    half = nx // 2
+    cells = list(range(half, nx) if up else range(half - 1, -1, -1))
+    us = end_line(center[half - 3 :] if up else center[: half + 3], face, up, edge)
+    turned_flows = (lambda i: flows(cells[i])) if up else (lambda i: -flows(cells[i]))
+    return dict(zip(cells, line_upwind(us, eps, turned_flows)))
+
+
+def x_first_kernel(u_ref, face_ref, wind_ref, speed_ref, acc_in, acc_ref, *, sizes, eps):
+    nx, nh, ny = sizes
+    p = pitch(sizes)
+    head = lax.axis_index("ha") * nh
+
+    def run(up):
+        edge = edge_mask(up)
+
+        def line(h, carry):
+            speed = speed_ref[pl.ds(head + h, 1), :]
+            for yg in range(ny // SUB):
+
+                def rows(x):
+                    return pl.ds(x * p + h * ny + yg * SUB, SUB)
+
+                def face(k):
+                    return pl.ds(pl.multiple_of((k * nh + h) * ny + yg * SUB, SUB), SUB)
+
+                center = [u_ref[rows(x), :] for x in range(nx)]
+                flows = lambda x: speed + wind_ref[pl.ds(x * ny + yg * SUB, SUB), :]
+                got = x_half(center, [face_ref[face(k), :] for k in range(3)], edge, up, eps, flows)
+                for x, value in got.items():
+                    acc_ref[rows(x), :] = acc_in[rows(x), :] + value
+            return carry
+
+        lax.fori_loop(0, nh, line, 0)
+
+    by_parity(is_even("gx"), True, run)
 
 
 def x_kernel(*refs, sizes, eps, stage):
     nx, nh, ny = sizes
     p = pitch(sizes)
     it = iter(refs)
-    u_ref, a_ref, b_ref, wind_ref, speed_ref, acc_in, terms_ref, rate_ref = (next(it) for _ in range(8))
+    u_ref, face_ref, wind_ref, speed_ref, acc_in, terms_ref, rate_ref = (next(it) for _ in range(7))
     first_ref = next(it) if stage > 1 else u_ref
     next_ref = next(it)
     turned_ref = next(it) if stage < 3 else None
@@ -224,53 +295,58 @@
             at = pl.ds(pl.multiple_of(h * ny, SUB), ny)
             return pltpu.make_async_copy(done_ref.at[:, at, :], next_ref.at[:, at, :], sems.at[h])
 
-    first, last, even = axis_flags("gx")
     head = lax.axis_index("ha") * nh
     step = CFL_NUMBER / rate_ref[...]
     planes = nx * ny // LANES
     per = LANES // ny
 
-    def line(h, carry):
-        if stage < 3:
-            turn(next_ref, turned_ref, jnp.maximum(h - 1, 0), sizes)
-        terms = []
-        for g in range(planes):
-            base = (h * planes + g) * SUB * TERMS
-            mat = jnp.concatenate([terms_ref[pl.ds(base + s * TERMS, BLOCK), :] for s in range(SUB)], axis=0)
-            terms.append(mat.T)
-        speed = speed_ref[pl.ds(head + h, 1), :]
-        for yg in range(ny // SUB):
-
-            def rows(x):
-                return pl.ds(x * p + h * ny + yg * SUB, SUB)
-
-            def face(k):
-                return pl.ds(pl.multiple_of((k * nh + h) * ny + yg * SUB, SUB), SUB)
-
-            center = [u_ref[rows(x), :] for x in range(nx)]
-            low, high = sided(even, lambda ref: [ref[face(k), :] for k in range(3)], a_ref, b_ref)
-            low, high = edge_fix(low, center[:2], center[-2:], high, (first, last))
-            flows = lambda x: speed + wind_ref[pl.ds(x * ny + yg * SUB, SUB), :]
-            for x, value in enumerate(line_upwind(low + center + high, eps, flows)):
-                at = (x % per) * ny + yg * SUB
-                total = (acc_in[rows(x), :] + terms[x // per][at : at + SUB]) + value
-                change = step * jnp.minimum(total, 0.0)
-                if stage == 1:
-                    new = center[x] + change
-                elif stage == 2:
-                    new = 0.75 * first_ref[rows(x), :] + 0.25 * (center[x] + change)
-                else:
-                    start = first_ref[rows(x), :]
-                    new = (2.0 / 3.0) * ((center[x] - start) + change)
-                if stage < 3:
-                    next_ref[rows(x), :] = new
-                else:
-                    done_ref[x, pl.ds(pl.multiple_of(h * ny + yg * SUB, SUB), SUB), :] = new
-        if stage == 3:
-            out_copy(h).start()
-        return carry
-
-    lax.fori_loop(0, nh, line, 0)
+    def run(up):
+        edge = edge_mask(up)
+
+        def line(h, carry):
+            if stage < 3:
+                turn(next_ref, turned_ref, jnp.maximum(h - 1, 0), sizes)
+            terms = []
+            for g in range(planes):
+                base = (h * planes + g) * SUB * TERMS
+                mat = jnp.concatenate([terms_ref[pl.ds(base + s * TERMS, BLOCK), :] for s in range(SUB)], axis=0)
+                terms.append(mat.T)
+            speed = speed_ref[pl.ds(head + h, 1), :]
+            for yg in range(ny // SUB):
+
+                def rows(x):
+                    return pl.ds(x * p + h * ny + yg * SUB, SUB)
+
+                def face(k):
+                    return pl.ds(pl.multiple_of((k * nh + h) * ny + yg * SUB, SUB), SUB)
+
+                center = [u_ref[rows(x), :] for x in range(nx)]
+                flows = lambda x: speed + wind_ref[pl.ds(x * ny + yg * SUB, SUB), :]
+                got = x_half(center, [face_ref[face(k), :] for k in range(3)], edge, up, eps, flows)
+                for x in range(nx):
+                    at = (x % per) * ny + yg * SUB
+                    total = acc_in[rows(x), :] + terms[x // per][at : at + SUB]
+                    if x in got:
+                        total = total + got[x]
+                    change = step * jnp.minimum(total, 0.0)
+                    if stage == 1:
+                        new = center[x] + change
+                    elif stage == 2:
+                        new = 0.75 * first_ref[rows(x), :] + 0.25 * (center[x] + change)
+                    else:
+                        start = first_ref[rows(x), :]
+                        new = (2.0 / 3.0) * ((center[x] - start) + change)
+                    if stage < 3:
+                        next_ref[rows(x), :] = new
+                    else:
+                        done_ref[x, pl.ds(pl.multiple_of(h * ny + yg * SUB, SUB), SUB), :] = new
+            if stage == 3:
+                out_copy(h).start()
+            return carry
+
+        lax.fori_loop(0, nh, line, 0)
+
+    by_parity(is_even("gx"), False, run)
     if stage == 3:
         for h in range(nh):
             out_copy(h).wait()
@@ -383,7 +459,7 @@
 VM = pl.BlockSpec(memory_space=pltpu.VMEM)
 
 
-def call(kernel, ins, outs, flops, keep=True, hbm=0, scratch=()):
+def call(kernel, ins, outs, flops, keep=True, hbm=0, scratch=(), aliases=None):
     shapes = [pltpu.VMEM(s, jnp.float32) if keep else jax.ShapeDtypeStruct(s, jnp.float32) for s in outs]
     ins = [pltpu.with_memory_space_constraint(x, pltpu.HBM) for x in ins[:hbm]] + [pltpu.with_memory_space_constraint(x, pltpu.VMEM) for x in ins[hbm:]]
     return pl.pallas_call(
@@ -392,6 +468,7 @@
         in_specs=[pl.BlockSpec(memory_space=pltpu.HBM)] * hbm + [VM] * (len(ins) - hbm),
         out_specs=[VM if keep else pl.BlockSpec(memory_space=pltpu.HBM)] * len(outs),
         scratch_shapes=list(scratch),
+        input_output_aliases=aliases or {},
         compiler_params=pltpu.CompilerParams(vmem_limit_bytes=VMEM_LIMIT),
         cost_estimate=pl.CostEstimate(flops=flops, transcendentals=0, bytes_accessed=1024),
     )(*ins)
@@ -432,7 +509,7 @@
             value = lax.pmax(value, axis)
         else:
             rounds += [(axis, 1 << k) for k in range(count.bit_length() - 1)]
-    rounds.sort(key=lambda step: step not in (("gx", 1), ("gy", 1)))
+    rounds.sort(key=lambda step: step[0] == "gy")
     for axis, reach in rounds:
         other = lax.ppermute(value, axis, [(i, i ^ reach) for i in range(lax.axis_size(axis))])
         value = jnp.maximum(value, other)
@@ -511,12 +588,21 @@
             functools.partial(y_kernel, sizes=sizes, eps=eps_g), [u, *got_y, wind_y, speed_y], [padded], flops
         )
         (acc,) = call(
-            functools.partial(head_kernel, sizes=sizes, eps=eps_h, scale=TURN_MAX / (6.0 * d_theta)),
-            [u, *got_h, acc],
+            functools.partial(x_first_kernel, sizes=sizes, eps=eps_g),
+            [u, got_x[0], wind_x, speed_x, acc],
             [padded],
             flops,
+            aliases={4: 0},
         )
-        ins = [u, *got_x, wind_x, speed_x, acc, terms, rate]
+        for face_a, got in zip((True, False), got_h):
+            (acc,) = call(
+                functools.partial(head_kernel, sizes=sizes, eps=eps_h, scale=TURN_MAX / (6.0 * d_theta), face_a=face_a),
+                [u, got, acc],
+                [padded],
+                flops,
+                aliases={2: 0},
+            )
+        ins = [u, got_x[1], wind_x, speed_x, acc, terms, rate]
         if stage > 1:
             ins.append(first)
         got = call(

time: 63.6 us -> 62.8 us (0.987)
  waiting for transfers between devices: 16.8 us -> 13.9 us
  Pallas kernels: 20 us -> 21.5 us
    ppermute x15, waiting for transfers between devices: 10.7 us -> 7.45 us  [send(): return lax.ppermute(face, axis, pairs)]
    pallas_call x14 -> x20, Pallas kernels: 20 us -> 21.5 us  [call(): pl.pallas_call(kernel, out_shape=shapes, in_specs=[pl.BlockSpec(memory_sp...]
  transfers between devices with their start and end apart: 18 -> 18, of which waited for: 9 -> 6; matrix products, arithmetic and copies ran while one was open for 0% -> 0% of each run, Pallas kernels for 20% -> 25%
where the time goes in v6:
time: 62.8 us; the launch traced here: 62.2 us
  starting transfers between devices  26.6 us (42%)
  Pallas kernels  21.5 us (34%)
  waiting for transfers between devices  13.9 us (22%)
    ppermute x15, starting transfers between devices, send(): return lax.ppermute(face, axis, pairs)  25.4 us
    pallas_call x20, Pallas kernels, call(): pl.pallas_call(kernel, out_shape=shapes, in_specs=[pl.BlockSpec(memory_sp...  21.5 us
    ppermute x15, waiting for transfers between devices, send(): return lax.ppermute(face, axis, pairs)  7.45 us
    ppermute x3, waiting for transfers between devices, all_max(): lax.ppermute(value, axis, [(i, i ^ reach) for i in range(lax.axis_size(ax...  6.43 us
  transfers between devices with their start and end apart: 18, of which 6 were waited for; matrix products, arithmetic and copies ran while one was open for 0% of the time, Pallas kernels for 25%

profile of v6, /device:TPU:4, one launch (start us, length us, event | category | flops | bytes accessed | tf_op | source)
XLA Modules:
  0.0 62.2 jit_solution(8347197342552920537)
XLA Ops:
  0.0 1.5 %shard_map.47 = (f32[8,128]{1,0:T(8,128)S(1)}, f32[480,128]{1,0:T(8,128)S(1)}, f32[480,128]{1,0:T(8,128)S(1)}, f32[384,128]{1,0:T(8,128)S(1)}, f32[384,128]{1,0:T(8,128)S(1)}) custom-call(f32[1280,128]{1,0:T(8,128)} %bitcast.6, f32[2,8,16]{2,1,0:T(8,128)} %wind_ref.3), custom_call_target="tpu_custom_call" | custom-call | flops 1000 | bytes 1024 | tf_op jit(solution)/shard_map/pallas_call | solution.py:465
  1.5 1.6 %collective-permute-start.3 = (f32[480,128]{1,0:T(8,128)S(1)}, f32[480,128]{1,0:T(8,128)S(1)}, u32[]{:S(2)}, u32[]{:S(2)}) collective-permute-start(f32[480,128]{1,0:T(8,128)S(1)} %get-tuple-element.34), channel_id=1, source_target_pairs={{0,8},{8,0},{16,24},{24,16},{1,9},{9,1},{17,25},{25,17},{2,10},{10... | collective-permute-start | bytes 737288 | tf_op jit(solution)/shard_map/ppermute | solution.py:486
  3.1 1.9 %collective-permute-start = (f32[480,128]{1,0:T(8,128)S(1)}, f32[480,128]{1,0:T(8,128)S(1)}, u32[]{:S(2)}, u32[]{:S(2)}) collective-permute-start(f32[480,128]{1,0:T(8,128)S(1)} %get-tuple-element.30), channel_id=1, source_target_pairs={{8,16},{16,8},{9,17},{17,9},{10,18},{18,10},{11,19},{19,11},{12,20... | collective-permute-start | bytes 737288 | tf_op jit(solution)/shard_map/ppermute | solution.py:486
  5.0 2.1 %collective-permute-start.2 = (f32[384,128]{1,0:T(8,128)S(1)}, f32[384,128]{1,0:T(8,128)S(1)}, u32[]{:S(2)}, u32[]{:S(2)}) collective-permute-start(f32[384,128]{1,0:T(8,128)S(1)} %get-tuple-element.33), channel_id=1, source_target_pairs={{0,1},{1,0},{2,3},{3,2},{4,5},{5,4},{6,7},{7,6},{8,9},{9,8},{10,11... | collective-permute-start | bytes 589832 | tf_op jit(solution)/shard_map/ppermute | solution.py:486
  7.1 2.5 %collective-permute-start.1 = (f32[384,128]{1,0:T(8,128)S(1)}, f32[384,128]{1,0:T(8,128)S(1)}, u32[]{:S(2)}, u32[]{:S(2)}) collective-permute-start(f32[384,128]{1,0:T(8,128)S(1)} %get-tuple-element.32), channel_id=1, source_target_pairs={{1,2},{2,1},{3,0},{0,3},{5,6},{6,5},{7,4},{4,7},{9,10},{10,9},{11,... | collective-permute-start | bytes 589832 | tf_op jit(solution)/shard_map/ppermute | solution.py:486
  9.6 4.1 %collective-permute-done.5 = f32[8,128]{1,0:T(8,128)S(1)} collective-permute-done((f32[8,128]{1,0:T(8,128)S(1)}, f32[8,128]{1,0:T(8,128)S(1)}, u32[]{:S(2)}, u32[]{:S(2)}) %collective-permute-start.5) | collective-permute-done | bytes 4128 | tf_op jit(solution)/shard_map/ppermute | solution.py:514
  13.6 1.2 %collective-permute-start.6 = (f32[8,128]{1,0:T(8,128)S(1)}, f32[8,128]{1,0:T(8,128)S(1)}, u32[]{:S(2)}, u32[]{:S(2)}) collective-permute-start(f32[8,128]{1,0:T(8,128)S(1)} %max.9), channel_id=1, source_target_pairs={{0,16},{8,24},{16,0},{24,8},{1,17},{9,25},{17,1},{25,9},{2,18},{10... | collective-permute-start | bytes 12296 | tf_op jit(solution)/shard_map/ppermute | solution.py:514
  14.9 2.4 %collective-permute-done.6 = f32[8,128]{1,0:T(8,128)S(1)} collective-permute-done((f32[8,128]{1,0:T(8,128)S(1)}, f32[8,128]{1,0:T(8,128)S(1)}, u32[]{:S(2)}, u32[]{:S(2)}) %collective-permute-start.6) | collective-permute-done | bytes 4128 | tf_op jit(solution)/shard_map/ppermute | solution.py:514
  17.3 1.5 %shard_map.46 = (f32[1312,128]{1,0:T(8,128)S(1)}, f32[2880,128]{1,0:T(8,128)S(1)}, f32[128,128]{1,0:T(8,128)S(1)}, f32[128,128]{1,0:T(8,128)S(1)}, f32[240,128]{1,0:T(8,128)S(1)}) custom-call(f32[1280,128]{1,0:T(8,128)} %bitcast.7, f32[2,8,16]{2,1,0:T(8,128)} %wind_ref.3), custom_call_target="tpu_custom_call" | custom-call | flops 1000 | bytes 1024 | tf_op jit(solution)/shard_map/pallas_call | solution.py:465
  19.3 1.2 %shard_map.52.refs_5_ = f32[1600,128]{1,0:T(8,128)S(1)} custom-call(f32[2880,128]{1,0:T(8,128)S(1)} %get-tuple-element.37.turned_ref), custom_call_target="tpu_custom_call" | custom-call | flops 6553600 | bytes 1024 | tf_op jit(solution)/shard_map/pallas_call | solution.py:465
  20.6 1.2 %shard_map.48.acc_in = f32[1312,128]{1,0:T(8,128)S(1)} custom-call(f32[1312,128]{1,0:T(8,128)S(1)} %get-tuple-element.29.u_ref.refs_0_.refs_7_, f32[240,128]{1,0:T(8,128)S(1)} %collective-permute-done.4.a_ref.b_ref, f32[240,128]{1,0:T(8,128)S(1)} %collective-permute-done.4.a_ref.b_ref, f32[128,128]{1,0:T(8,128)S(1)} %get-tuple-element.36.wind_ref, ...), custom_call_target="tpu_custom_call" | custom-call | flops 6553600 | bytes 1024 | tf_op jit(solution)/shard_map/pallas_call | solution.py:465
  21.8 0.8 %shard_map.49.acc_in = f32[1312,128]{1,0:T(8,128)S(1)} custom-call(f32[1312,128]{1,0:T(8,128)S(1)} %get-tuple-element.29.u_ref.refs_0_.refs_7_, f32[480,128]{1,0:T(8,128)S(1)} %collective-permute-done.3.face_ref, f32[128,128]{1,0:T(8,128)S(1)} %get-tuple-element.31.wind_ref.refs_2_, f32[40,128]{1,0:T(8,128)S(1)} %copy-done, ...), custom_call_target="tpu_custom_call", output_to_operand_aliasing={{}: (4, {})} | custom-call | flops 6553600 | bytes 1024 | tf_op jit(solution)/shard_map/pallas_call | solution.py:465
  22.7 0.7 %shard_map.50.acc_in = f32[1312,128]{1,0:T(8,128)S(1)} custom-call(f32[1312,128]{1,0:T(8,128)S(1)} %get-tuple-element.29.u_ref.refs_0_.refs_7_, f32[384,128]{1,0:T(8,128)S(1)} %collective-permute-done.2.face_ref, f32[1312,128]{1,0:T(8,128)S(1)} %shard_map.49.acc_in), custom_call_target="tpu_custom_call", output_to_operand_aliasing={{}: (2, {})} | custom-call | flops 6553600 | bytes 1024 | tf_op jit(solution)/shard_map/pallas_call | solution.py:465
  24.2 1.2 %shard_map.53 = (f32[1312,128]{1,0:T(8,128)S(1)}, f32[2880,128]{1,0:T(8,128)S(1)}, f32[480,128]{1,0:T(8,128)S(1)}, f32[480,128]{1,0:T(8,128)S(1)}, f32[384,128]{...) custom-call(f32[1312,128]{1,0:T(8,128)S(1)} %get-tuple-element.29.u_ref.refs_0_.refs_7_, ...), custom_call_target="tpu_custom_call" | custom-call | flops 6553600 | bytes 1024 | tf_op jit(solution)/shard_map/pallas_call | solution.py:465
  25.4 2.5 %collective-permute-start.11 = (f32[480,128]{1,0:T(8,128)S(1)}, f32[480,128]{1,0:T(8,128)S(1)}, u32[]{:S(2)}, u32[]{:S(2)}) collective-permute-start(f32[480,128]{1,0:T(8,128)S(1)} %get-tuple-element.43), channel_id=1, source_target_pairs={{0,8},{8,0},{16,24},{24,16},{1,9},{9,1},{17,25},{25,17},{2,10},{10... | collective-permute-start | bytes 737288 | tf_op jit(solution)/shard_map/ppermute | solution.py:486
  28.0 2.1 %collective-permute-start.8 = (f32[480,128]{1,0:T(8,128)S(1)}, f32[480,128]{1,0:T(8,128)S(1)}, u32[]{:S(2)}, u32[]{:S(2)}) collective-permute-start(f32[480,128]{1,0:T(8,128)S(1)} %get-tuple-element.40), channel_id=1, source_target_pairs={{8,16},{16,8},{9,17},{17,9},{10,18},{18,10},{11,19},{19,11},{12,20... | collective-permute-start | bytes 737288 | tf_op jit(solution)/shard_map/ppermute | solution.py:486
  30.1 1.9 %collective-permute-start.10 = (f32[384,128]{1,0:T(8,128)S(1)}, f32[384,128]{1,0:T(8,128)S(1)}, u32[]{:S(2)}, u32[]{:S(2)}) collective-permute-start(f32[384,128]{1,0:T(8,128)S(1)} %get-tuple-element.42), channel_id=1, source_target_pairs={{0,1},{1,0},{2,3},{3,2},{4,5},{5,4},{6,7},{7,6},{8,9},{9,8},{10,11... | collective-permute-start | bytes 589832 | tf_op jit(solution)/shard_map/ppermute | solution.py:486
  32.0 2.5 %collective-permute-start.9 = (f32[384,128]{1,0:T(8,128)S(1)}, f32[384,128]{1,0:T(8,128)S(1)}, u32[]{:S(2)}, u32[]{:S(2)}) collective-permute-start(f32[384,128]{1,0:T(8,128)S(1)} %get-tuple-element.41), channel_id=1, source_target_pairs={{1,2},{2,1},{3,0},{0,3},{5,6},{6,5},{7,4},{4,7},{9,10},{10,9},{11,... | collective-permute-start | bytes 589832 | tf_op jit(solution)/shard_map/ppermute | solution.py:486
  34.5 1.2 %shard_map.58.refs_5_ = f32[1600,128]{1,0:T(8,128)S(1)} custom-call(f32[2880,128]{1,0:T(8,128)S(1)} %get-tuple-element.45.turned_ref), custom_call_target="tpu_custom_call" | custom-call | flops 6553600 | bytes 1024 | tf_op jit(solution)/shard_map/pallas_call | solution.py:465
  35.8 1.2 %shard_map.54.acc_in = f32[1312,128]{1,0:T(8,128)S(1)} custom-call(f32[1312,128]{1,0:T(8,128)S(1)} %get-tuple-element.39.u_ref.refs_0_, f32[240,128]{1,0:T(8,128)S(1)} %collective-permute-done.12.a_ref.b_ref, f32[240,128]{1,0:T(8,128)S(1)} %collective-permute-done.12.a_ref.b_ref, f32[128,128]{1,0:T(8,128)S(1)} %get-tuple-element.36.wind_ref, ...), custom_call_target="tpu_custom_call" | custom-call | flops 6553600 | bytes 1024 | tf_op jit(solution)/shard_map/pallas_call | solution.py:465
  37.0 0.8 %shard_map.55.acc_in = f32[1312,128]{1,0:T(8,128)S(1)} custom-call(f32[1312,128]{1,0:T(8,128)S(1)} %get-tuple-element.39.u_ref.refs_0_, f32[480,128]{1,0:T(8,128)S(1)} %collective-permute-done.11.face_ref, f32[128,128]{1,0:T(8,128)S(1)} %get-tuple-element.31.wind_ref.refs_2_, f32[40,128]{1,0:T(8,128)S(1)} %copy-done, ...), custom_call_target="tpu_custom_call", output_to_operand_aliasing={{}: (4, {})} | custom-call | flops 6553600 | bytes 1024 | tf_op jit(solution)/shard_map/pallas_call | solution.py:465
  37.8 0.7 %shard_map.56.acc_in = f32[1312,128]{1,0:T(8,128)S(1)} custom-call(f32[1312,128]{1,0:T(8,128)S(1)} %get-tuple-element.39.u_ref.refs_0_, f32[384,128]{1,0:T(8,128)S(1)} %collective-permute-done.10.face_ref, f32[1312,128]{1,0:T(8,128)S(1)} %shard_map.55.acc_in), custom_call_target="tpu_custom_call", output_to_operand_aliasing={{}: (2, {})} | custom-call | flops 6553600 | bytes 1024 | tf_op jit(solution)/shard_map/pallas_call | solution.py:465
  38.6 4.5 %collective-permute-done.9.face_ref = f32[384,128]{1,0:T(8,128)S(1)} collective-permute-done((f32[384,128]{1,0:T(8,128)S(1)}, f32[384,128]{1,0:T(8,128)S(1)}, u32[]{:S(2)}, u32[]{:S(2)}) %collective-permute-start.9) | collective-permute-done | bytes 196640 | tf_op jit(solution)/shard_map/ppermute | solution.py:486
  43.8 1.2 %shard_map.59 = (f32[1312,128]{1,0:T(8,128)S(1)}, f32[2880,128]{1,0:T(8,128)S(1)}, f32[480,128]{1,0:T(8,128)S(1)}, f32[480,128]{1,0:T(8,128)S(1)}, f32[384,128]{...) custom-call(f32[1312,128]{1,0:T(8,128)S(1)} %get-tuple-element.39.u_ref.refs_0_, ...), custom_call_target="tpu_custom_call" | custom-call | flops 6553600 | bytes 1024 | tf_op jit(solution)/shard_map/pallas_call | solution.py:465
  45.1 4.4 %collective-permute-start.13 = (f32[480,128]{1,0:T(8,128)S(1)}, f32[480,128]{1,0:T(8,128)S(1)}, u32[]{:S(2)}, u32[]{:S(2)}) collective-permute-start(f32[480,128]{1,0:T(8,128)S(1)} %get-tuple-element.47), channel_id=1, source_target_pairs={{8,16},{16,8},{9,17},{17,9},{10,18},{18,10},{11,19},{19,11},{12,20... | collective-permute-start | bytes 737288 | tf_op jit(solution)/shard_map/ppermute | solution.py:486
  50.1 2.6 %collective-permute-start.14 = (f32[384,128]{1,0:T(8,128)S(1)}, f32[384,128]{1,0:T(8,128)S(1)}, u32[]{:S(2)}, u32[]{:S(2)}) collective-permute-start(f32[384,128]{1,0:T(8,128)S(1)} %get-tuple-element.48), channel_id=1, source_target_pairs={{1,2},{2,1},{3,0},{0,3},{5,6},{6,5},{7,4},{4,7},{9,10},{10,9},{11,... | collective-permute-start | bytes 589832 | tf_op jit(solution)/shard_map/ppermute | solution.py:486
  52.8 1.2 %shard_map.64.refs_5_ = f32[1600,128]{1,0:T(8,128)S(1)} custom-call(f32[2880,128]{1,0:T(8,128)S(1)} %get-tuple-element.52.turned_ref), custom_call_target="tpu_custom_call" | custom-call | flops 6553600 | bytes 1024 | tf_op jit(solution)/shard_map/pallas_call | solution.py:465
  54.1 1.2 %shard_map.60.acc_in = f32[1312,128]{1,0:T(8,128)S(1)} custom-call(f32[1312,128]{1,0:T(8,128)S(1)} %get-tuple-element.46.u_ref.refs_0_, f32[240,128]{1,0:T(8,128)S(1)} %collective-permute-done.17.a_ref.b_ref, f32[240,128]{1,0:T(8,128)S(1)} %collective-permute-done.17.a_ref.b_ref, f32[128,128]{1,0:T(8,128)S(1)} %get-tuple-element.36.wind_ref, ...), custom_call_target="tpu_custom_call" | custom-call | flops 6553600 | bytes 1024 | tf_op jit(solution)/shard_map/pallas_call | solution.py:465
  55.3 0.8 %shard_map.61.acc_in = f32[1312,128]{1,0:T(8,128)S(1)} custom-call(f32[1312,128]{1,0:T(8,128)S(1)} %get-tuple-element.46.u_ref.refs_0_, f32[480,128]{1,0:T(8,128)S(1)} %collective-permute-done.16.face_ref, f32[128,128]{1,0:T(8,128)S(1)} %get-tuple-element.31.wind_ref.refs_2_, f32[40,128]{1,0:T(8,128)S(1)} %copy-done, ...), custom_call_target="tpu_custom_call", output_to_operand_aliasing={{}: (4, {})} | custom-call | flops 6553600 | bytes 1024 | tf_op jit(solution)/shard_map/pallas_call | solution.py:465
  56.1 2.8 %collective-permute-done.15.face_ref = f32[384,128]{1,0:T(8,128)S(1)} collective-permute-done((f32[384,128]{1,0:T(8,128)S(1)}, f32[384,128]{1,0:T(8,128)S(1)}, u32[]{:S(2)}, u32[]{:S(2)}) %collective-permute-start.15) | collective-permute-done | bytes 196640 | tf_op jit(solution)/shard_map/ppermute | solution.py:486
  59.6 0.7 %shard_map.63.refs_4_ = f32[1312,128]{1,0:T(8,128)S(1)} custom-call(f32[1312,128]{1,0:T(8,128)S(1)} %get-tuple-element.46.u_ref.refs_0_, f32[384,128]{1,0:T(8,128)S(1)} %collective-permute-done.14.face_ref, f32[1312,128]{1,0:T(8,128)S(1)} %shard_map.62.acc_in), custom_call_target="tpu_custom_call", output_to_operand_aliasing={{}: (2, {})} | custom-call | flops 6553600 | bytes 1024 | tf_op jit(solution)/shard_map/pallas_call | solution.py:465
  60.4 1.8 %shard_map.65 = f32[8,160,128]{2,1,0:T(8,128)} custom-call(f32[1312,128]{1,0:T(8,128)S(1)} %get-tuple-element.46.u_ref.refs_0_, f32[480,128]{1,0:T(8,128)S(1)} %collective-permute-done.13.refs_1_, f32[128,128]{1,0:T(8,128)S(1)} %get-tuple-element.31.wind_ref.refs_2_, f32[40,128]{1,0:T(8,128)S(1)} %copy-done, f32[1312,128]{1,0:T(8,128)S(1)} %shard_map.63.refs_4_, ...), custom_call_target="tpu_custom_call" | custom-call | flops 6553600 | bytes 1024 | tf_op jit(solution)/shard_map/pallas_call | solution.py:465
  (31 shorter events, 3.7 us)
Async XLA Ops:
  1.5 20.3 %collective-permute-start.3 = (f32[480,128]{1,0:T(8,128)S(1)}, f32[480,128]{1,0:T(8,128)S(1)}, u32[]{:S(2)}, u32[]{:S(2)}) collective-permute-start(f32[480,128]{1,0:T(8,128)S(1)} %get-tuple-element.34), channel_id=1, source_target_pairs={{0,8},{8,0},{16,24},{24,16},{1,9},{9,1},{17,25},{25,17},{2,10},{10... | collective-permute-start | bytes 737288 | tf_op jit(solution)/shard_map/ppermute | solution.py:486
  3.1 21.1 %collective-permute-start = (f32[480,128]{1,0:T(8,128)S(1)}, f32[480,128]{1,0:T(8,128)S(1)}, u32[]{:S(2)}, u32[]{:S(2)}) collective-permute-start(f32[480,128]{1,0:T(8,128)S(1)} %get-tuple-element.30), channel_id=1, source_target_pairs={{8,16},{16,8},{9,17},{17,9},{10,18},{18,10},{11,19},{19,11},{12,20... | collective-permute-start | bytes 737288 | tf_op jit(solution)/shard_map/ppermute | solution.py:486
  5.0 17.7 %collective-permute-start.2 = (f32[384,128]{1,0:T(8,128)S(1)}, f32[384,128]{1,0:T(8,128)S(1)}, u32[]{:S(2)}, u32[]{:S(2)}) collective-permute-start(f32[384,128]{1,0:T(8,128)S(1)} %get-tuple-element.33), channel_id=1, source_target_pairs={{0,1},{1,0},{2,3},{3,2},{4,5},{5,4},{6,7},{7,6},{8,9},{9,8},{10,11... | collective-permute-start | bytes 589832 | tf_op jit(solution)/shard_map/ppermute | solution.py:486
  7.1 16.3 %collective-permute-start.1 = (f32[384,128]{1,0:T(8,128)S(1)}, f32[384,128]{1,0:T(8,128)S(1)}, u32[]{:S(2)}, u32[]{:S(2)}) collective-permute-start(f32[384,128]{1,0:T(8,128)S(1)} %get-tuple-element.32), channel_id=1, source_target_pairs={{1,2},{2,1},{3,0},{0,3},{5,6},{6,5},{7,4},{4,7},{9,10},{10,9},{11,... | collective-permute-start | bytes 589832 | tf_op jit(solution)/shard_map/ppermute | solution.py:486
  9.6 4.1 %collective-permute-start.5 = (f32[8,128]{1,0:T(8,128)S(1)}, f32[8,128]{1,0:T(8,128)S(1)}, u32[]{:S(2)}, u32[]{:S(2)}) collective-permute-start(f32[8,128]{1,0:T(8,128)S(1)} %get-tuple-element.38), channel_id=1, source_target_pairs={{0,8},{8,0},{16,24},{24,16},{1,9},{9,1},{17,25},{25,17},{2,10},{10... | collective-permute-start | bytes 12296 | tf_op jit(solution)/shard_map/ppermute | solution.py:514
  13.6 3.6 %collective-permute-start.6 = (f32[8,128]{1,0:T(8,128)S(1)}, f32[8,128]{1,0:T(8,128)S(1)}, u32[]{:S(2)}, u32[]{:S(2)}) collective-permute-start(f32[8,128]{1,0:T(8,128)S(1)} %max.9), channel_id=1, source_target_pairs={{0,16},{8,24},{16,0},{24,8},{1,17},{9,25},{17,1},{25,9},{2,18},{10... | collective-permute-start | bytes 12296 | tf_op jit(solution)/shard_map/ppermute | solution.py:514
  17.3 3.3 %copy-start.1 = (f32[40,128]{1,0:T(8,128)S(1)}, f32[40,128]{1,0:T(8,128)}, u32[]{:S(2)}) copy-start(f32[40,128]{1,0:T(8,128)} %constant.5.clone.speed_ref) | copy-start | bytes 61444
  17.3 1.5 %collective-permute-start.7 = (f32[8,128]{1,0:T(8,128)S(1)}, f32[8,128]{1,0:T(8,128)S(1)}, u32[]{:S(2)}, u32[]{:S(2)}) collective-permute-start(f32[8,128]{1,0:T(8,128)S(1)} %max.10), channel_id=1, source_target_pairs={{0,4},{4,0},{1,5},{5,1},{2,6},{6,2},{3,7},{7,3},{8,12},{12,8},{9,1... | collective-permute-start | bytes 12296 | tf_op jit(solution)/shard_map/ppermute | solution.py:514
  18.8 1.8 %collective-permute-start.4 = (f32[240,128]{1,0:T(8,128)S(1)}, f32[240,128]{1,0:T(8,128)S(1)}, u32[]{:S(2)}, u32[]{:S(2)}) collective-permute-start(f32[240,128]{1,0:T(8,128)S(1)} %get-tuple-element.35), channel_id=1, source_target_pairs={{0,4},{4,0},{1,5},{5,1},{2,6},{6,2},{3,7},{7,3},{8,12},{12,8},{9,1... | collective-permute-start | bytes 368648 | tf_op jit(solution)/shard_map/ppermute | solution.py:486
  19.3 2.5 %copy-start = (f32[40,128]{1,0:T(8,128)S(1)}, f32[40,128]{1,0:T(8,128)}, u32[]{:S(2)}) copy-start(f32[40,128]{1,0:T(8,128)} %constant.4.clone.speed_ref.refs_3_) | copy-start | bytes 61444
  25.4 11.6 %collective-permute-start.11 = (f32[480,128]{1,0:T(8,128)S(1)}, f32[480,128]{1,0:T(8,128)S(1)}, u32[]{:S(2)}, u32[]{:S(2)}) collective-permute-start(f32[480,128]{1,0:T(8,128)S(1)} %get-tuple-element.43), channel_id=1, source_target_pairs={{0,8},{8,0},{16,24},{24,16},{1,9},{9,1},{17,25},{25,17},{2,10},{10... | collective-permute-start | bytes 737288 | tf_op jit(solution)/shard_map/ppermute | solution.py:486
  28.0 15.8 %collective-permute-start.8 = (f32[480,128]{1,0:T(8,128)S(1)}, f32[480,128]{1,0:T(8,128)S(1)}, u32[]{:S(2)}, u32[]{:S(2)}) collective-permute-start(f32[480,128]{1,0:T(8,128)S(1)} %get-tuple-element.40), channel_id=1, source_target_pairs={{8,16},{16,8},{9,17},{17,9},{10,18},{18,10},{11,19},{19,11},{12,20... | collective-permute-start | bytes 737288 | tf_op jit(solution)/shard_map/ppermute | solution.py:486
  30.1 7.7 %collective-permute-start.10 = (f32[384,128]{1,0:T(8,128)S(1)}, f32[384,128]{1,0:T(8,128)S(1)}, u32[]{:S(2)}, u32[]{:S(2)}) collective-permute-start(f32[384,128]{1,0:T(8,128)S(1)} %get-tuple-element.42), channel_id=1, source_target_pairs={{0,1},{1,0},{2,3},{3,2},{4,5},{5,4},{6,7},{7,6},{8,9},{9,8},{10,11... | collective-permute-start | bytes 589832 | tf_op jit(solution)/shard_map/ppermute | solution.py:486
  32.0 11.1 %collective-permute-start.9 = (f32[384,128]{1,0:T(8,128)S(1)}, f32[384,128]{1,0:T(8,128)S(1)}, u32[]{:S(2)}, u32[]{:S(2)}) collective-permute-start(f32[384,128]{1,0:T(8,128)S(1)} %get-tuple-element.41), channel_id=1, source_target_pairs={{1,2},{2,1},{3,0},{0,3},{5,6},{6,5},{7,4},{4,7},{9,10},{10,9},{11,... | collective-permute-start | bytes 589832 | tf_op jit(solution)/shard_map/ppermute | solution.py:486
  34.5 1.3 %collective-permute-start.12 = (f32[240,128]{1,0:T(8,128)S(1)}, f32[240,128]{1,0:T(8,128)S(1)}, u32[]{:S(2)}, u32[]{:S(2)}) collective-permute-start(f32[240,128]{1,0:T(8,128)S(1)} %get-tuple-element.44), channel_id=1, source_target_pairs={{0,4},{4,0},{1,5},{5,1},{2,6},{6,2},{3,7},{7,3},{8,12},{12,8},{9,1... | collective-permute-start | bytes 368648 | tf_op jit(solution)/shard_map/ppermute | solution.py:486
  45.1 10.3 %collective-permute-start.16 = (f32[480,128]{1,0:T(8,128)S(1)}, f32[480,128]{1,0:T(8,128)S(1)}, u32[]{:S(2)}, u32[]{:S(2)}) collective-permute-start(f32[480,128]{1,0:T(8,128)S(1)} %get-tuple-element.50), channel_id=1, source_target_pairs={{0,8},{8,0},{16,24},{24,16},{1,9},{9,1},{17,25},{25,17},{2,10},{10... | collective-permute-start | bytes 737288 | tf_op jit(solution)/shard_map/ppermute | solution.py:486
  45.1 15.3 %collective-permute-start.13 = (f32[480,128]{1,0:T(8,128)S(1)}, f32[480,128]{1,0:T(8,128)S(1)}, u32[]{:S(2)}, u32[]{:S(2)}) collective-permute-start(f32[480,128]{1,0:T(8,128)S(1)} %get-tuple-element.47), channel_id=1, source_target_pairs={{8,16},{16,8},{9,17},{17,9},{10,18},{18,10},{11,19},{19,11},{12,20... | collective-permute-start | bytes 737288 | tf_op jit(solution)/shard_map/ppermute | solution.py:486
  49.5 9.4 %collective-permute-start.15 = (f32[384,128]{1,0:T(8,128)S(1)}, f32[384,128]{1,0:T(8,128)S(1)}, u32[]{:S(2)}, u32[]{:S(2)}) collective-permute-start(f32[384,128]{1,0:T(8,128)S(1)} %get-tuple-element.49), channel_id=1, source_target_pairs={{0,1},{1,0},{2,3},{3,2},{4,5},{5,4},{6,7},{7,6},{8,9},{9,8},{10,11... | collective-permute-start | bytes 589832 | tf_op jit(solution)/shard_map/ppermute | solution.py:486
  50.1 9.5 %collective-permute-start.14 = (f32[384,128]{1,0:T(8,128)S(1)}, f32[384,128]{1,0:T(8,128)S(1)}, u32[]{:S(2)}, u32[]{:S(2)}) collective-permute-start(f32[384,128]{1,0:T(8,128)S(1)} %get-tuple-element.48), channel_id=1, source_target_pairs={{1,2},{2,1},{3,0},{0,3},{5,6},{6,5},{7,4},{4,7},{9,10},{10,9},{11,... | collective-permute-start | bytes 589832 | tf_op jit(solution)/shard_map/ppermute | solution.py:486
  52.8 1.3 %collective-permute-start.17 = (f32[240,128]{1,0:T(8,128)S(1)}, f32[240,128]{1,0:T(8,128)S(1)}, u32[]{:S(2)}, u32[]{:S(2)}) collective-permute-start(f32[240,128]{1,0:T(8,128)S(1)} %get-tuple-element.51), channel_id=1, source_target_pairs={{0,4},{4,0},{1,5},{5,1},{2,6},{6,2},{3,7},{7,3},{8,12},{12,8},{9,1... | collective-permute-start | bytes 368648 | tf_op jit(solution)/shard_map/ppermute | solution.py:486

commit v7 on v6

--- a/solution.py
+++ b/solution.py
@@ -482,8 +482,8 @@
     count = lax.axis_size(axis)
     ends = count if closed else count - 1
 
-    def send(face, pairs):
-        return lax.ppermute(face, axis, pairs)
+    def send(face, pairs, over=axis):
+        return lax.ppermute(face, over, pairs)
 
     if not paired(axis):
         got_b = send(face_a, [(i, (i + 1) % count) for i in range(ends)])
@@ -494,7 +494,13 @@
         pairs = []
         for i in range(start, ends, 2):
             pairs += [(i, (i + 1) % count), ((i + 1) % count, i)]
-        return send(face, pairs) if pairs else None
+        alone = sorted(set(range(count)) - {i for i, _ in pairs})
+        side = lax.axis_size("gy")
+        if not pairs or not alone or axis != "gx" or side % 2:
+            return send(face, pairs) if pairs else None
+        every = [(i * side + k, j * side + k) for i, j in pairs for k in range(side)]
+        every += [(i * side + k, i * side + (k ^ 1)) for i in alone for k in range(side)]
+        return send(face, sorted(every), (axis, "gy"))
 
     got_b = swap(face_b, 1) if face_b is not None else None
     got_a = swap(face_a, 0)

time: 62.8 us -> 62.7 us (level)
  the two profiles are of different devices: /device:TPU:4 before, /device:TPU:0 now
where the time goes in v7:
time: 62.7 us; the launch traced here: 62.4 us
  starting transfers between devices  22.5 us (36%)
  Pallas kernels  21.4 us (34%)
  waiting for transfers between devices  18.2 us (29%)
    pallas_call x20, Pallas kernels, call(): pl.pallas_call(kernel, out_shape=shapes, in_specs=[pl.BlockSpec(memory_sp...  21.4 us
    ppermute x15, starting transfers between devices, send(): return lax.ppermute(face, over, pairs)  18.8 us
    ppermute x15, waiting for transfers between devices, send(): return lax.ppermute(face, over, pairs)  11.1 us
    ppermute x3, waiting for transfers between devices, all_max(): lax.ppermute(value, axis, [(i, i ^ reach) for i in range(lax.axis_size(ax...  7.1 us
    ppermute x3, starting transfers between devices, all_max(): lax.ppermute(value, axis, [(i, i ^ reach) for i in range(lax.axis_size(ax...  3.76 us
  transfers between devices with their start and end apart: 18, of which 8 were waited for; matrix products, arithmetic and copies ran while one was open for 0% of the time, Pallas kernels for 25%

profile of v7, /device:TPU:0, one launch (start us, length us, event | category | flops | bytes accessed | tf_op | source)
XLA Modules:
  0.0 62.4 jit_solution(14991986514679847649)
XLA Ops:
  0.0 1.5 %shard_map.47 = (f32[8,128]{1,0:T(8,128)S(1)}, f32[480,128]{1,0:T(8,128)S(1)}, f32[480,128]{1,0:T(8,128)S(1)}, f32[384,128]{1,0:T(8,128)S(1)}, f32[384,128]{1,0:T(8,128)S(1)}) custom-call(f32[1280,128]{1,0:T(8,128)} %bitcast.6, f32[2,8,16]{2,1,0:T(8,128)} %wind_ref.3), custom_call_target="tpu_custom_call" | custom-call | flops 1000 | bytes 1024 | tf_op jit(solution)/shard_map/pallas_call | solution.py:465
  1.5 3.0 %collective-permute-start.3 = (f32[480,128]{1,0:T(8,128)S(1)}, f32[480,128]{1,0:T(8,128)S(1)}, u32[]{:S(2)}, u32[]{:S(2)}) collective-permute-start(f32[480,128]{1,0:T(8,128)S(1)} %get-tuple-element.34), channel_id=1, source_target_pairs={{0,8},{8,0},{16,24},{24,16},{1,9},{9,1},{17,25},{25,17},{2,10},{10... | collective-permute-start | bytes 737288 | tf_op jit(solution)/shard_map/ppermute | solution.py:486
  4.5 1.6 %collective-permute-start.2 = (f32[384,128]{1,0:T(8,128)S(1)}, f32[384,128]{1,0:T(8,128)S(1)}, u32[]{:S(2)}, u32[]{:S(2)}) collective-permute-start(f32[384,128]{1,0:T(8,128)S(1)} %get-tuple-element.33), channel_id=1, source_target_pairs={{0,1},{1,0},{2,3},{3,2},{4,5},{5,4},{6,7},{7,6},{8,9},{9,8},{10,11... | collective-permute-start | bytes 589832 | tf_op jit(solution)/shard_map/ppermute | solution.py:486
  6.1 2.5 %collective-permute-start.1 = (f32[384,128]{1,0:T(8,128)S(1)}, f32[384,128]{1,0:T(8,128)S(1)}, u32[]{:S(2)}, u32[]{:S(2)}) collective-permute-start(f32[384,128]{1,0:T(8,128)S(1)} %get-tuple-element.32), channel_id=1, source_target_pairs={{1,2},{2,1},{3,0},{0,3},{5,6},{6,5},{7,4},{4,7},{9,10},{10,9},{11,... | collective-permute-start | bytes 589832 | tf_op jit(solution)/shard_map/ppermute | solution.py:486
  8.6 3.0 %collective-permute-start.5 = (f32[8,128]{1,0:T(8,128)S(1)}, f32[8,128]{1,0:T(8,128)S(1)}, u32[]{:S(2)}, u32[]{:S(2)}) collective-permute-start(f32[8,128]{1,0:T(8,128)S(1)} %get-tuple-element.38), channel_id=1, source_target_pairs={{0,8},{8,0},{16,24},{24,16},{1,9},{9,1},{17,25},{25,17},{2,10},{10... | collective-permute-start | bytes 12296 | tf_op jit(solution)/shard_map/ppermute | solution.py:520
  11.6 4.3 %collective-permute-done.5 = f32[8,128]{1,0:T(8,128)S(1)} collective-permute-done((f32[8,128]{1,0:T(8,128)S(1)}, f32[8,128]{1,0:T(8,128)S(1)}, u32[]{:S(2)}, u32[]{:S(2)}) %collective-permute-start.5) | collective-permute-done | bytes 4128 | tf_op jit(solution)/shard_map/ppermute | solution.py:520
  15.9 0.8 %collective-permute-start.6 = (f32[8,128]{1,0:T(8,128)S(1)}, f32[8,128]{1,0:T(8,128)S(1)}, u32[]{:S(2)}, u32[]{:S(2)}) collective-permute-start(f32[8,128]{1,0:T(8,128)S(1)} %max.9), channel_id=1, source_target_pairs={{0,16},{8,24},{16,0},{24,8},{1,17},{9,25},{17,1},{25,9},{2,18},{10... | collective-permute-start | bytes 12296 | tf_op jit(solution)/shard_map/ppermute | solution.py:520
  16.6 2.8 %collective-permute-done.6 = f32[8,128]{1,0:T(8,128)S(1)} collective-permute-done((f32[8,128]{1,0:T(8,128)S(1)}, f32[8,128]{1,0:T(8,128)S(1)}, u32[]{:S(2)}, u32[]{:S(2)}) %collective-permute-start.6) | collective-permute-done | bytes 4128 | tf_op jit(solution)/shard_map/ppermute | solution.py:520
  19.5 1.5 %shard_map.46 = (f32[1312,128]{1,0:T(8,128)S(1)}, f32[2880,128]{1,0:T(8,128)S(1)}, f32[128,128]{1,0:T(8,128)S(1)}, f32[128,128]{1,0:T(8,128)S(1)}, f32[240,128]{1,0:T(8,128)S(1)}) custom-call(f32[1280,128]{1,0:T(8,128)} %bitcast.7, f32[2,8,16]{2,1,0:T(8,128)} %wind_ref.3), custom_call_target="tpu_custom_call" | custom-call | flops 1000 | bytes 1024 | tf_op jit(solution)/shard_map/pallas_call | solution.py:465
  21.6 1.2 %shard_map.52.refs_5_ = f32[1600,128]{1,0:T(8,128)S(1)} custom-call(f32[2880,128]{1,0:T(8,128)S(1)} %get-tuple-element.37.turned_ref), custom_call_target="tpu_custom_call" | custom-call | flops 6553600 | bytes 1024 | tf_op jit(solution)/shard_map/pallas_call | solution.py:465
  22.8 1.2 %shard_map.48.acc_in = f32[1312,128]{1,0:T(8,128)S(1)} custom-call(f32[1312,128]{1,0:T(8,128)S(1)} %get-tuple-element.29.u_ref.refs_0_.refs_7_, f32[240,128]{1,0:T(8,128)S(1)} %collective-permute-done.4.a_ref.b_ref, f32[240,128]{1,0:T(8,128)S(1)} %collective-permute-done.4.a_ref.b_ref, f32[128,128]{1,0:T(8,128)S(1)} %get-tuple-element.36.wind_ref, ...), custom_call_target="tpu_custom_call" | custom-call | flops 6553600 | bytes 1024 | tf_op jit(solution)/shard_map/pallas_call | solution.py:465
  24.1 0.8 %shard_map.49.acc_in = f32[1312,128]{1,0:T(8,128)S(1)} custom-call(f32[1312,128]{1,0:T(8,128)S(1)} %get-tuple-element.29.u_ref.refs_0_.refs_7_, f32[480,128]{1,0:T(8,128)S(1)} %collective-permute-done.3.face_ref, f32[128,128]{1,0:T(8,128)S(1)} %get-tuple-element.31.wind_ref.refs_2_, f32[40,128]{1,0:T(8,128)S(1)} %copy-done, ...), custom_call_target="tpu_custom_call", output_to_operand_aliasing={{}: (4, {})} | custom-call | flops 6553600 | bytes 1024 | tf_op jit(solution)/shard_map/pallas_call | solution.py:465
  26.4 1.2 %shard_map.53 = (f32[1312,128]{1,0:T(8,128)S(1)}, f32[2880,128]{1,0:T(8,128)S(1)}, f32[480,128]{1,0:T(8,128)S(1)}, f32[480,128]{1,0:T(8,128)S(1)}, f32[384,128]{...) custom-call(f32[1312,128]{1,0:T(8,128)S(1)} %get-tuple-element.29.u_ref.refs_0_.refs_7_, ...), custom_call_target="tpu_custom_call" | custom-call | flops 6553600 | bytes 1024 | tf_op jit(solution)/shard_map/pallas_call | solution.py:465
  27.6 1.3 %collective-permute-start.11 = (f32[480,128]{1,0:T(8,128)S(1)}, f32[480,128]{1,0:T(8,128)S(1)}, u32[]{:S(2)}, u32[]{:S(2)}) collective-permute-start(f32[480,128]{1,0:T(8,128)S(1)} %get-tuple-element.43), channel_id=1, source_target_pairs={{0,8},{8,0},{16,24},{24,16},{1,9},{9,1},{17,25},{25,17},{2,10},{10... | collective-permute-start | bytes 737288 | tf_op jit(solution)/shard_map/ppermute | solution.py:486
  29.0 1.6 %collective-permute-start.10 = (f32[384,128]{1,0:T(8,128)S(1)}, f32[384,128]{1,0:T(8,128)S(1)}, u32[]{:S(2)}, u32[]{:S(2)}) collective-permute-start(f32[384,128]{1,0:T(8,128)S(1)} %get-tuple-element.42), channel_id=1, source_target_pairs={{0,1},{1,0},{2,3},{3,2},{4,5},{5,4},{6,7},{7,6},{8,9},{9,8},{10,11... | collective-permute-start | bytes 589832 | tf_op jit(solution)/shard_map/ppermute | solution.py:486
  30.5 2.5 %collective-permute-start.9 = (f32[384,128]{1,0:T(8,128)S(1)}, f32[384,128]{1,0:T(8,128)S(1)}, u32[]{:S(2)}, u32[]{:S(2)}) collective-permute-start(f32[384,128]{1,0:T(8,128)S(1)} %get-tuple-element.41), channel_id=1, source_target_pairs={{1,2},{2,1},{3,0},{0,3},{5,6},{6,5},{7,4},{4,7},{9,10},{10,9},{11,... | collective-permute-start | bytes 589832 | tf_op jit(solution)/shard_map/ppermute | solution.py:486
  33.0 1.2 %shard_map.58.refs_5_ = f32[1600,128]{1,0:T(8,128)S(1)} custom-call(f32[2880,128]{1,0:T(8,128)S(1)} %get-tuple-element.45.turned_ref), custom_call_target="tpu_custom_call" | custom-call | flops 6553600 | bytes 1024 | tf_op jit(solution)/shard_map/pallas_call | solution.py:465
  34.3 1.2 %shard_map.54.acc_in = f32[1312,128]{1,0:T(8,128)S(1)} custom-call(f32[1312,128]{1,0:T(8,128)S(1)} %get-tuple-element.39.u_ref.refs_0_, f32[240,128]{1,0:T(8,128)S(1)} %collective-permute-done.12.a_ref.b_ref, f32[240,128]{1,0:T(8,128)S(1)} %collective-permute-done.12.a_ref.b_ref, f32[128,128]{1,0:T(8,128)S(1)} %get-tuple-element.36.wind_ref, ...), custom_call_target="tpu_custom_call" | custom-call | flops 6553600 | bytes 1024 | tf_op jit(solution)/shard_map/pallas_call | solution.py:465
  35.6 1.0 %collective-permute-done.11.face_ref = f32[480,128]{1,0:T(8,128)S(1)} collective-permute-done((f32[480,128]{1,0:T(8,128)S(1)}, f32[480,128]{1,0:T(8,128)S(1)}, u32[]{:S(2)}, u32[]{:S(2)}) %collective-permute-start.11) | collective-permute-done | bytes 245792 | tf_op jit(solution)/shard_map/ppermute | solution.py:486
  36.5 0.8 %shard_map.55.acc_in = f32[1312,128]{1,0:T(8,128)S(1)} custom-call(f32[1312,128]{1,0:T(8,128)S(1)} %get-tuple-element.39.u_ref.refs_0_, f32[480,128]{1,0:T(8,128)S(1)} %collective-permute-done.11.face_ref, f32[128,128]{1,0:T(8,128)S(1)} %get-tuple-element.31.wind_ref.refs_2_, f32[40,128]{1,0:T(8,128)S(1)} %copy-done, ...), custom_call_target="tpu_custom_call", output_to_operand_aliasing={{}: (4, {})} | custom-call | flops 6553600 | bytes 1024 | tf_op jit(solution)/shard_map/pallas_call | solution.py:465
  37.3 0.7 %shard_map.56.acc_in = f32[1312,128]{1,0:T(8,128)S(1)} custom-call(f32[1312,128]{1,0:T(8,128)S(1)} %get-tuple-element.39.u_ref.refs_0_, f32[384,128]{1,0:T(8,128)S(1)} %collective-permute-done.10.face_ref, f32[1312,128]{1,0:T(8,128)S(1)} %shard_map.55.acc_in), custom_call_target="tpu_custom_call", output_to_operand_aliasing={{}: (2, {})} | custom-call | flops 6553600 | bytes 1024 | tf_op jit(solution)/shard_map/pallas_call | solution.py:465
  38.1 4.5 %collective-permute-done.9.face_ref = f32[384,128]{1,0:T(8,128)S(1)} collective-permute-done((f32[384,128]{1,0:T(8,128)S(1)}, f32[384,128]{1,0:T(8,128)S(1)}, u32[]{:S(2)}, u32[]{:S(2)}) %collective-permute-start.9) | collective-permute-done | bytes 196640 | tf_op jit(solution)/shard_map/ppermute | solution.py:486
  43.4 1.2 %shard_map.59 = (f32[1312,128]{1,0:T(8,128)S(1)}, f32[2880,128]{1,0:T(8,128)S(1)}, f32[480,128]{1,0:T(8,128)S(1)}, f32[480,128]{1,0:T(8,128)S(1)}, f32[384,128]{...) custom-call(f32[1312,128]{1,0:T(8,128)S(1)} %get-tuple-element.39.u_ref.refs_0_, ...), custom_call_target="tpu_custom_call" | custom-call | flops 6553600 | bytes 1024 | tf_op jit(solution)/shard_map/pallas_call | solution.py:465
  44.6 2.5 %collective-permute-start.16 = (f32[480,128]{1,0:T(8,128)S(1)}, f32[480,128]{1,0:T(8,128)S(1)}, u32[]{:S(2)}, u32[]{:S(2)}) collective-permute-start(f32[480,128]{1,0:T(8,128)S(1)} %get-tuple-element.50), channel_id=1, source_target_pairs={{0,8},{8,0},{16,24},{24,16},{1,9},{9,1},{17,25},{25,17},{2,10},{10... | collective-permute-start | bytes 737288 | tf_op jit(solution)/shard_map/ppermute | solution.py:486
  47.7 2.6 %collective-permute-start.14 = (f32[384,128]{1,0:T(8,128)S(1)}, f32[384,128]{1,0:T(8,128)S(1)}, u32[]{:S(2)}, u32[]{:S(2)}) collective-permute-start(f32[384,128]{1,0:T(8,128)S(1)} %get-tuple-element.48), channel_id=1, source_target_pairs={{1,2},{2,1},{3,0},{0,3},{5,6},{6,5},{7,4},{4,7},{9,10},{10,9},{11,... | collective-permute-start | bytes 589832 | tf_op jit(solution)/shard_map/ppermute | solution.py:486
  50.4 1.2 %shard_map.64.refs_5_ = f32[1600,128]{1,0:T(8,128)S(1)} custom-call(f32[2880,128]{1,0:T(8,128)S(1)} %get-tuple-element.52.turned_ref), custom_call_target="tpu_custom_call" | custom-call | flops 6553600 | bytes 1024 | tf_op jit(solution)/shard_map/pallas_call | solution.py:465
  51.7 1.2 %shard_map.60.acc_in = f32[1312,128]{1,0:T(8,128)S(1)} custom-call(f32[1312,128]{1,0:T(8,128)S(1)} %get-tuple-element.46.u_ref.refs_0_, f32[240,128]{1,0:T(8,128)S(1)} %collective-permute-done.17.a_ref.b_ref, f32[240,128]{1,0:T(8,128)S(1)} %collective-permute-done.17.a_ref.b_ref, f32[128,128]{1,0:T(8,128)S(1)} %get-tuple-element.36.wind_ref, ...), custom_call_target="tpu_custom_call" | custom-call | flops 6553600 | bytes 1024 | tf_op jit(solution)/shard_map/pallas_call | solution.py:465
  52.9 1.0 %collective-permute-done.16.face_ref = f32[480,128]{1,0:T(8,128)S(1)} collective-permute-done((f32[480,128]{1,0:T(8,128)S(1)}, f32[480,128]{1,0:T(8,128)S(1)}, u32[]{:S(2)}, u32[]{:S(2)}) %collective-permute-start.16) | collective-permute-done | bytes 245792 | tf_op jit(solution)/shard_map/ppermute | solution.py:486
  53.9 0.8 %shard_map.61.acc_in = f32[1312,128]{1,0:T(8,128)S(1)} custom-call(f32[1312,128]{1,0:T(8,128)S(1)} %get-tuple-element.46.u_ref.refs_0_, f32[480,128]{1,0:T(8,128)S(1)} %collective-permute-done.16.face_ref, f32[128,128]{1,0:T(8,128)S(1)} %get-tuple-element.31.wind_ref.refs_2_, f32[40,128]{1,0:T(8,128)S(1)} %copy-done, ...), custom_call_target="tpu_custom_call", output_to_operand_aliasing={{}: (4, {})} | custom-call | flops 6553600 | bytes 1024 | tf_op jit(solution)/shard_map/pallas_call | solution.py:465
  54.7 0.7 %shard_map.62.acc_in = f32[1312,128]{1,0:T(8,128)S(1)} custom-call(f32[1312,128]{1,0:T(8,128)S(1)} %get-tuple-element.46.u_ref.refs_0_, f32[384,128]{1,0:T(8,128)S(1)} %collective-permute-done.15.face_ref, f32[1312,128]{1,0:T(8,128)S(1)} %shard_map.61.acc_in), custom_call_target="tpu_custom_call", output_to_operand_aliasing={{}: (2, {})} | custom-call | flops 6553600 | bytes 1024 | tf_op jit(solution)/shard_map/pallas_call | solution.py:465
  55.5 4.4 %collective-permute-done.14.face_ref = f32[384,128]{1,0:T(8,128)S(1)} collective-permute-done((f32[384,128]{1,0:T(8,128)S(1)}, f32[384,128]{1,0:T(8,128)S(1)}, u32[]{:S(2)}, u32[]{:S(2)}) %collective-permute-start.14) | collective-permute-done | bytes 196640 | tf_op jit(solution)/shard_map/ppermute | solution.py:486
  60.6 1.8 %shard_map.65 = f32[8,160,128]{2,1,0:T(8,128)} custom-call(f32[1312,128]{1,0:T(8,128)S(1)} %get-tuple-element.46.u_ref.refs_0_, f32[480,128]{1,0:T(8,128)S(1)} %collective-permute-done.13.refs_1_, f32[128,128]{1,0:T(8,128)S(1)} %get-tuple-element.31.wind_ref.refs_2_, f32[40,128]{1,0:T(8,128)S(1)} %copy-done, f32[1312,128]{1,0:T(8,128)S(1)} %shard_map.63.refs_4_, ...), custom_call_target="tpu_custom_call" | custom-call | flops 6553600 | bytes 1024 | tf_op jit(solution)/shard_map/pallas_call | solution.py:465
  (31 shorter events, 4.3 us)
Async XLA Ops:
  1.5 22.5 %collective-permute-start.3 = (f32[480,128]{1,0:T(8,128)S(1)}, f32[480,128]{1,0:T(8,128)S(1)}, u32[]{:S(2)}, u32[]{:S(2)}) collective-permute-start(f32[480,128]{1,0:T(8,128)S(1)} %get-tuple-element.34), channel_id=1, source_target_pairs={{0,8},{8,0},{16,24},{24,16},{1,9},{9,1},{17,25},{25,17},{2,10},{10... | collective-permute-start | bytes 737288 | tf_op jit(solution)/shard_map/ppermute | solution.py:486
  4.5 21.9 %collective-permute-start = (f32[480,128]{1,0:T(8,128)S(1)}, f32[480,128]{1,0:T(8,128)S(1)}, u32[]{:S(2)}, u32[]{:S(2)}) collective-permute-start(f32[480,128]{1,0:T(8,128)S(1)} %get-tuple-element.30), channel_id=1, source_target_pairs={{0,4},{4,0},{8,16},{12,20},{16,8},{20,12},{24,28},{28,24},{1,5},{5... | collective-permute-start | bytes 737288 | tf_op jit(solution)/shard_map/ppermute | solution.py:486
  4.5 20.3 %collective-permute-start.2 = (f32[384,128]{1,0:T(8,128)S(1)}, f32[384,128]{1,0:T(8,128)S(1)}, u32[]{:S(2)}, u32[]{:S(2)}) collective-permute-start(f32[384,128]{1,0:T(8,128)S(1)} %get-tuple-element.33), channel_id=1, source_target_pairs={{0,1},{1,0},{2,3},{3,2},{4,5},{5,4},{6,7},{7,6},{8,9},{9,8},{10,11... | collective-permute-start | bytes 589832 | tf_op jit(solution)/shard_map/ppermute | solution.py:486
  6.1 19.5 %collective-permute-start.1 = (f32[384,128]{1,0:T(8,128)S(1)}, f32[384,128]{1,0:T(8,128)S(1)}, u32[]{:S(2)}, u32[]{:S(2)}) collective-permute-start(f32[384,128]{1,0:T(8,128)S(1)} %get-tuple-element.32), channel_id=1, source_target_pairs={{1,2},{2,1},{3,0},{0,3},{5,6},{6,5},{7,4},{4,7},{9,10},{10,9},{11,... | collective-permute-start | bytes 589832 | tf_op jit(solution)/shard_map/ppermute | solution.py:486
  8.6 7.3 %collective-permute-start.5 = (f32[8,128]{1,0:T(8,128)S(1)}, f32[8,128]{1,0:T(8,128)S(1)}, u32[]{:S(2)}, u32[]{:S(2)}) collective-permute-start(f32[8,128]{1,0:T(8,128)S(1)} %get-tuple-element.38), channel_id=1, source_target_pairs={{0,8},{8,0},{16,24},{24,16},{1,9},{9,1},{17,25},{25,17},{2,10},{10... | collective-permute-start | bytes 12296 | tf_op jit(solution)/shard_map/ppermute | solution.py:520
  15.9 3.6 %collective-permute-start.6 = (f32[8,128]{1,0:T(8,128)S(1)}, f32[8,128]{1,0:T(8,128)S(1)}, u32[]{:S(2)}, u32[]{:S(2)}) collective-permute-start(f32[8,128]{1,0:T(8,128)S(1)} %max.9), channel_id=1, source_target_pairs={{0,16},{8,24},{16,0},{24,8},{1,17},{9,25},{17,1},{25,9},{2,18},{10... | collective-permute-start | bytes 12296 | tf_op jit(solution)/shard_map/ppermute | solution.py:520
  19.5 3.3 %copy-start.1 = (f32[40,128]{1,0:T(8,128)S(1)}, f32[40,128]{1,0:T(8,128)}, u32[]{:S(2)}) copy-start(f32[40,128]{1,0:T(8,128)} %constant.5.clone.speed_ref) | copy-start | bytes 61444
  19.5 1.5 %collective-permute-start.7 = (f32[8,128]{1,0:T(8,128)S(1)}, f32[8,128]{1,0:T(8,128)S(1)}, u32[]{:S(2)}, u32[]{:S(2)}) collective-permute-start(f32[8,128]{1,0:T(8,128)S(1)} %max.10), channel_id=1, source_target_pairs={{0,4},{4,0},{1,5},{5,1},{2,6},{6,2},{3,7},{7,3},{8,12},{12,8},{9,1... | collective-permute-start | bytes 12296 | tf_op jit(solution)/shard_map/ppermute | solution.py:520
  21.0 1.8 %collective-permute-start.4 = (f32[240,128]{1,0:T(8,128)S(1)}, f32[240,128]{1,0:T(8,128)S(1)}, u32[]{:S(2)}, u32[]{:S(2)}) collective-permute-start(f32[240,128]{1,0:T(8,128)S(1)} %get-tuple-element.35), channel_id=1, source_target_pairs={{0,4},{4,0},{1,5},{5,1},{2,6},{6,2},{3,7},{7,3},{8,12},{12,8},{9,1... | collective-permute-start | bytes 368648 | tf_op jit(solution)/shard_map/ppermute | solution.py:486
  21.6 2.5 %copy-start = (f32[40,128]{1,0:T(8,128)S(1)}, f32[40,128]{1,0:T(8,128)}, u32[]{:S(2)}) copy-start(f32[40,128]{1,0:T(8,128)} %constant.4.clone.speed_ref.refs_3_) | copy-start | bytes 61444
  27.6 8.9 %collective-permute-start.11 = (f32[480,128]{1,0:T(8,128)S(1)}, f32[480,128]{1,0:T(8,128)S(1)}, u32[]{:S(2)}, u32[]{:S(2)}) collective-permute-start(f32[480,128]{1,0:T(8,128)S(1)} %get-tuple-element.43), channel_id=1, source_target_pairs={{0,8},{8,0},{16,24},{24,16},{1,9},{9,1},{17,25},{25,17},{2,10},{10... | collective-permute-start | bytes 737288 | tf_op jit(solution)/shard_map/ppermute | solution.py:486
  29.0 14.4 %collective-permute-start.8 = (f32[480,128]{1,0:T(8,128)S(1)}, f32[480,128]{1,0:T(8,128)S(1)}, u32[]{:S(2)}, u32[]{:S(2)}) collective-permute-start(f32[480,128]{1,0:T(8,128)S(1)} %get-tuple-element.40), channel_id=1, source_target_pairs={{0,4},{4,0},{8,16},{12,20},{16,8},{20,12},{24,28},{28,24},{1,5},{5... | collective-permute-start | bytes 737288 | tf_op jit(solution)/shard_map/ppermute | solution.py:486
  29.0 8.4 %collective-permute-start.10 = (f32[384,128]{1,0:T(8,128)S(1)}, f32[384,128]{1,0:T(8,128)S(1)}, u32[]{:S(2)}, u32[]{:S(2)}) collective-permute-start(f32[384,128]{1,0:T(8,128)S(1)} %get-tuple-element.42), channel_id=1, source_target_pairs={{0,1},{1,0},{2,3},{3,2},{4,5},{5,4},{6,7},{7,6},{8,9},{9,8},{10,11... | collective-permute-start | bytes 589832 | tf_op jit(solution)/shard_map/ppermute | solution.py:486
  30.5 12.1 %collective-permute-start.9 = (f32[384,128]{1,0:T(8,128)S(1)}, f32[384,128]{1,0:T(8,128)S(1)}, u32[]{:S(2)}, u32[]{:S(2)}) collective-permute-start(f32[384,128]{1,0:T(8,128)S(1)} %get-tuple-element.41), channel_id=1, source_target_pairs={{1,2},{2,1},{3,0},{0,3},{5,6},{6,5},{7,4},{4,7},{9,10},{10,9},{11,... | collective-permute-start | bytes 589832 | tf_op jit(solution)/shard_map/ppermute | solution.py:486
  33.0 1.3 %collective-permute-start.12 = (f32[240,128]{1,0:T(8,128)S(1)}, f32[240,128]{1,0:T(8,128)S(1)}, u32[]{:S(2)}, u32[]{:S(2)}) collective-permute-start(f32[240,128]{1,0:T(8,128)S(1)} %get-tuple-element.44), channel_id=1, source_target_pairs={{0,4},{4,0},{1,5},{5,1},{2,6},{6,2},{3,7},{7,3},{8,12},{12,8},{9,1... | collective-permute-start | bytes 368648 | tf_op jit(solution)/shard_map/ppermute | solution.py:486
  44.6 9.4 %collective-permute-start.16 = (f32[480,128]{1,0:T(8,128)S(1)}, f32[480,128]{1,0:T(8,128)S(1)}, u32[]{:S(2)}, u32[]{:S(2)}) collective-permute-start(f32[480,128]{1,0:T(8,128)S(1)} %get-tuple-element.50), channel_id=1, source_target_pairs={{0,8},{8,0},{16,24},{24,16},{1,9},{9,1},{17,25},{25,17},{2,10},{10... | collective-permute-start | bytes 737288 | tf_op jit(solution)/shard_map/ppermute | solution.py:486
  47.1 13.5 %collective-permute-start.13 = (f32[480,128]{1,0:T(8,128)S(1)}, f32[480,128]{1,0:T(8,128)S(1)}, u32[]{:S(2)}, u32[]{:S(2)}) collective-permute-start(f32[480,128]{1,0:T(8,128)S(1)} %get-tuple-element.47), channel_id=1, source_target_pairs={{0,4},{4,0},{8,16},{12,20},{16,8},{20,12},{24,28},{28,24},{1,5},{5... | collective-permute-start | bytes 737288 | tf_op jit(solution)/shard_map/ppermute | solution.py:486
  47.1 7.6 %collective-permute-start.15 = (f32[384,128]{1,0:T(8,128)S(1)}, f32[384,128]{1,0:T(8,128)S(1)}, u32[]{:S(2)}, u32[]{:S(2)}) collective-permute-start(f32[384,128]{1,0:T(8,128)S(1)} %get-tuple-element.49), channel_id=1, source_target_pairs={{0,1},{1,0},{2,3},{3,2},{4,5},{5,4},{6,7},{7,6},{8,9},{9,8},{10,11... | collective-permute-start | bytes 589832 | tf_op jit(solution)/shard_map/ppermute | solution.py:486
  47.7 12.1 %collective-permute-start.14 = (f32[384,128]{1,0:T(8,128)S(1)}, f32[384,128]{1,0:T(8,128)S(1)}, u32[]{:S(2)}, u32[]{:S(2)}) collective-permute-start(f32[384,128]{1,0:T(8,128)S(1)} %get-tuple-element.48), channel_id=1, source_target_pairs={{1,2},{2,1},{3,0},{0,3},{5,6},{6,5},{7,4},{4,7},{9,10},{10,9},{11,... | collective-permute-start | bytes 589832 | tf_op jit(solution)/shard_map/ppermute | solution.py:486
  50.4 1.3 %collective-permute-start.17 = (f32[240,128]{1,0:T(8,128)S(1)}, f32[240,128]{1,0:T(8,128)S(1)}, u32[]{:S(2)}, u32[]{:S(2)}) collective-permute-start(f32[240,128]{1,0:T(8,128)S(1)} %get-tuple-element.51), channel_id=1, source_target_pairs={{0,4},{4,0},{1,5},{5,1},{2,6},{6,2},{3,7},{7,3},{8,12},{12,8},{9,1... | collective-permute-start | bytes 368648 | tf_op jit(solution)/shard_map/ppermute | solution.py:486

commit v8 on v7

--- a/solution.py
+++ b/solution.py
@@ -33,20 +33,17 @@
         base = t[r] * t[r] + ((0.75 * p[r - 1]) * p[r] + eps)
         if r <= n - 1:
             s = base + p[r] * z
-            alpha[r] = pl.reciprocal(s * s, approx=APPROX)
+            alpha[r] = pl.reciprocal(s * s)
             a3[r] = (1.0 / 3.0) * alpha[r]
         if r >= 1:
             s = base - p[r - 1] * z
-            gamma[r] = pl.reciprocal(s * s, approx=APPROX)
+            gamma[r] = pl.reciprocal(s * s)
             g3[r] = (1.0 / 3.0) * gamma[r]
         if 0 <= r <= n:
-            beta[r] = pl.reciprocal(0.5 * (base * base), approx=APPROX)
+            beta[r] = pl.reciprocal(0.5 * (base * base))
     f = {m: t[m] - t[m + 1] for m in range(-1, n + 1)}
     f2 = {m: f[m] + f[m] for m in range(-1, n + 1)}
     return n, q, p, alpha, beta, gamma, a3, g3, f, f2
-
-
-APPROX = True
 
 
 def line_max(us, eps):
@@ -55,11 +52,9 @@
     outs = []
     for i in range(n):
         er = (g3[i + 2] * f2[i + 1] + alpha[i] * f[i]) * pl.reciprocal(
-            g3[i + 2] + beta[i + 1] + alpha[i], approx=APPROX
-        )
+            g3[i + 2] + beta[i + 1] + alpha[i])
         el = (a3[i - 1] * f2[i - 1] + gamma[i + 1] * f[i]) * pl.reciprocal(
-            a3[i - 1] + beta[i] + gamma[i + 1], approx=APPROX
-        )
+            a3[i - 1] + beta[i] + gamma[i + 1])
         p2 = p[i] + p[i]
         outs.append(jnp.minimum((p2 - q6[i + 1]) + (p[i + 1] + er), (p2 + q6[i]) + (p[i - 1] + el)))
     return outs
@@ -77,7 +72,7 @@
         f1 = jnp.where(right, f2[i + 1], f2[i - 1])
         pn = jnp.where(right, p[i + 1], p[i - 1])
         qn = jnp.where(right, q[i + 1], q[i])
-        e = (w1 * f1 + w3 * f[i]) * pl.reciprocal(w1 + w2 + w3, approx=APPROX)
+        e = (w1 * f1 + w3 * f[i]) * pl.reciprocal(w1 + w2 + w3)
         x = pn + (p[i] + p[i]) + e
         outs.append(flow * qn - jnp.abs((1.0 / 6.0) * flow) * x)
     return outs

time: 62.7 us -> 62.7 us (level)
  no operation moved by 1% of the time
where the time goes in v8:
time: 62.7 us; the launch traced here: 62.4 us
  starting transfers between devices  22.5 us (36%)
  Pallas kernels  21.4 us (34%)
  waiting for transfers between devices  18.2 us (29%)
    pallas_call x20, Pallas kernels, call(): pl.pallas_call(kernel, out_shape=shapes, in_specs=[pl.BlockSpec(memory_sp...  21.4 us
    ppermute x15, starting transfers between devices, send(): return lax.ppermute(face, over, pairs)  18.8 us
    ppermute x15, waiting for transfers between devices, send(): return lax.ppermute(face, over, pairs)  11.1 us
    ppermute x3, waiting for transfers between devices, all_max(): lax.ppermute(value, axis, [(i, i ^ reach) for i in range(lax.axis_size(ax...  7.1 us
    ppermute x3, starting transfers between devices, all_max(): lax.ppermute(value, axis, [(i, i ^ reach) for i in range(lax.axis_size(ax...  3.76 us
  transfers between devices with their start and end apart: 18, of which 8 were waited for; matrix products, arithmetic and copies ran while one was open for 0% of the time, Pallas kernels for 25%

profile of v8, /device:TPU:0, one launch (start us, length us, event | category | flops | bytes accessed | tf_op | source)
XLA Modules:
  0.0 62.4 jit_solution(14991986514679847649)
XLA Ops:
  0.0 1.5 %shard_map.47 = (f32[8,128]{1,0:T(8,128)S(1)}, f32[480,128]{1,0:T(8,128)S(1)}, f32[480,128]{1,0:T(8,128)S(1)}, f32[384,128]{1,0:T(8,128)S(1)}, f32[384,128]{1,0:T(8,128)S(1)}) custom-call(f32[1280,128]{1,0:T(8,128)} %bitcast.6, f32[2,8,16]{2,1,0:T(8,128)} %wind_ref.3), custom_call_target="tpu_custom_call" | custom-call | flops 1000 | bytes 1024 | tf_op jit(solution)/shard_map/pallas_call | solution.py:460
  1.5 3.0 %collective-permute-start.3 = (f32[480,128]{1,0:T(8,128)S(1)}, f32[480,128]{1,0:T(8,128)S(1)}, u32[]{:S(2)}, u32[]{:S(2)}) collective-permute-start(f32[480,128]{1,0:T(8,128)S(1)} %get-tuple-element.34), channel_id=1, source_target_pairs={{0,8},{8,0},{16,24},{24,16},{1,9},{9,1},{17,25},{25,17},{2,10},{10... | collective-permute-start | bytes 737288 | tf_op jit(solution)/shard_map/ppermute | solution.py:481
  4.5 1.6 %collective-permute-start.2 = (f32[384,128]{1,0:T(8,128)S(1)}, f32[384,128]{1,0:T(8,128)S(1)}, u32[]{:S(2)}, u32[]{:S(2)}) collective-permute-start(f32[384,128]{1,0:T(8,128)S(1)} %get-tuple-element.33), channel_id=1, source_target_pairs={{0,1},{1,0},{2,3},{3,2},{4,5},{5,4},{6,7},{7,6},{8,9},{9,8},{10,11... | collective-permute-start | bytes 589832 | tf_op jit(solution)/shard_map/ppermute | solution.py:481
  6.1 2.5 %collective-permute-start.1 = (f32[384,128]{1,0:T(8,128)S(1)}, f32[384,128]{1,0:T(8,128)S(1)}, u32[]{:S(2)}, u32[]{:S(2)}) collective-permute-start(f32[384,128]{1,0:T(8,128)S(1)} %get-tuple-element.32), channel_id=1, source_target_pairs={{1,2},{2,1},{3,0},{0,3},{5,6},{6,5},{7,4},{4,7},{9,10},{10,9},{11,... | collective-permute-start | bytes 589832 | tf_op jit(solution)/shard_map/ppermute | solution.py:481
  8.6 3.0 %collective-permute-start.5 = (f32[8,128]{1,0:T(8,128)S(1)}, f32[8,128]{1,0:T(8,128)S(1)}, u32[]{:S(2)}, u32[]{:S(2)}) collective-permute-start(f32[8,128]{1,0:T(8,128)S(1)} %get-tuple-element.38), channel_id=1, source_target_pairs={{0,8},{8,0},{16,24},{24,16},{1,9},{9,1},{17,25},{25,17},{2,10},{10... | collective-permute-start | bytes 12296 | tf_op jit(solution)/shard_map/ppermute | solution.py:515
  11.6 4.3 %collective-permute-done.5 = f32[8,128]{1,0:T(8,128)S(1)} collective-permute-done((f32[8,128]{1,0:T(8,128)S(1)}, f32[8,128]{1,0:T(8,128)S(1)}, u32[]{:S(2)}, u32[]{:S(2)}) %collective-permute-start.5) | collective-permute-done | bytes 4128 | tf_op jit(solution)/shard_map/ppermute | solution.py:515
  15.9 0.8 %collective-permute-start.6 = (f32[8,128]{1,0:T(8,128)S(1)}, f32[8,128]{1,0:T(8,128)S(1)}, u32[]{:S(2)}, u32[]{:S(2)}) collective-permute-start(f32[8,128]{1,0:T(8,128)S(1)} %max.9), channel_id=1, source_target_pairs={{0,16},{8,24},{16,0},{24,8},{1,17},{9,25},{17,1},{25,9},{2,18},{10... | collective-permute-start | bytes 12296 | tf_op jit(solution)/shard_map/ppermute | solution.py:515
  16.6 2.8 %collective-permute-done.6 = f32[8,128]{1,0:T(8,128)S(1)} collective-permute-done((f32[8,128]{1,0:T(8,128)S(1)}, f32[8,128]{1,0:T(8,128)S(1)}, u32[]{:S(2)}, u32[]{:S(2)}) %collective-permute-start.6) | collective-permute-done | bytes 4128 | tf_op jit(solution)/shard_map/ppermute | solution.py:515
  19.5 1.5 %shard_map.46 = (f32[1312,128]{1,0:T(8,128)S(1)}, f32[2880,128]{1,0:T(8,128)S(1)}, f32[128,128]{1,0:T(8,128)S(1)}, f32[128,128]{1,0:T(8,128)S(1)}, f32[240,128]{1,0:T(8,128)S(1)}) custom-call(f32[1280,128]{1,0:T(8,128)} %bitcast.7, f32[2,8,16]{2,1,0:T(8,128)} %wind_ref.3), custom_call_target="tpu_custom_call" | custom-call | flops 1000 | bytes 1024 | tf_op jit(solution)/shard_map/pallas_call | solution.py:460
  21.6 1.2 %shard_map.52.refs_5_ = f32[1600,128]{1,0:T(8,128)S(1)} custom-call(f32[2880,128]{1,0:T(8,128)S(1)} %get-tuple-element.37.turned_ref), custom_call_target="tpu_custom_call" | custom-call | flops 6553600 | bytes 1024 | tf_op jit(solution)/shard_map/pallas_call | solution.py:460
  22.8 1.2 %shard_map.48.acc_in = f32[1312,128]{1,0:T(8,128)S(1)} custom-call(f32[1312,128]{1,0:T(8,128)S(1)} %get-tuple-element.29.u_ref.refs_0_.refs_7_, f32[240,128]{1,0:T(8,128)S(1)} %collective-permute-done.4.a_ref.b_ref, f32[240,128]{1,0:T(8,128)S(1)} %collective-permute-done.4.a_ref.b_ref, f32[128,128]{1,0:T(8,128)S(1)} %get-tuple-element.36.wind_ref, ...), custom_call_target="tpu_custom_call" | custom-call | flops 6553600 | bytes 1024 | tf_op jit(solution)/shard_map/pallas_call | solution.py:460
  24.1 0.8 %shard_map.49.acc_in = f32[1312,128]{1,0:T(8,128)S(1)} custom-call(f32[1312,128]{1,0:T(8,128)S(1)} %get-tuple-element.29.u_ref.refs_0_.refs_7_, f32[480,128]{1,0:T(8,128)S(1)} %collective-permute-done.3.face_ref, f32[128,128]{1,0:T(8,128)S(1)} %get-tuple-element.31.wind_ref.refs_2_, f32[40,128]{1,0:T(8,128)S(1)} %copy-done, ...), custom_call_target="tpu_custom_call", output_to_operand_aliasing={{}: (4, {})} | custom-call | flops 6553600 | bytes 1024 | tf_op jit(solution)/shard_map/pallas_call | solution.py:460
  26.4 1.2 %shard_map.53 = (f32[1312,128]{1,0:T(8,128)S(1)}, f32[2880,128]{1,0:T(8,128)S(1)}, f32[480,128]{1,0:T(8,128)S(1)}, f32[480,128]{1,0:T(8,128)S(1)}, f32[384,128]{...) custom-call(f32[1312,128]{1,0:T(8,128)S(1)} %get-tuple-element.29.u_ref.refs_0_.refs_7_, ...), custom_call_target="tpu_custom_call" | custom-call | flops 6553600 | bytes 1024 | tf_op jit(solution)/shard_map/pallas_call | solution.py:460
  27.6 1.3 %collective-permute-start.11 = (f32[480,128]{1,0:T(8,128)S(1)}, f32[480,128]{1,0:T(8,128)S(1)}, u32[]{:S(2)}, u32[]{:S(2)}) collective-permute-start(f32[480,128]{1,0:T(8,128)S(1)} %get-tuple-element.43), channel_id=1, source_target_pairs={{0,8},{8,0},{16,24},{24,16},{1,9},{9,1},{17,25},{25,17},{2,10},{10... | collective-permute-start | bytes 737288 | tf_op jit(solution)/shard_map/ppermute | solution.py:481
  29.0 1.6 %collective-permute-start.10 = (f32[384,128]{1,0:T(8,128)S(1)}, f32[384,128]{1,0:T(8,128)S(1)}, u32[]{:S(2)}, u32[]{:S(2)}) collective-permute-start(f32[384,128]{1,0:T(8,128)S(1)} %get-tuple-element.42), channel_id=1, source_target_pairs={{0,1},{1,0},{2,3},{3,2},{4,5},{5,4},{6,7},{7,6},{8,9},{9,8},{10,11... | collective-permute-start | bytes 589832 | tf_op jit(solution)/shard_map/ppermute | solution.py:481
  30.5 2.5 %collective-permute-start.9 = (f32[384,128]{1,0:T(8,128)S(1)}, f32[384,128]{1,0:T(8,128)S(1)}, u32[]{:S(2)}, u32[]{:S(2)}) collective-permute-start(f32[384,128]{1,0:T(8,128)S(1)} %get-tuple-element.41), channel_id=1, source_target_pairs={{1,2},{2,1},{3,0},{0,3},{5,6},{6,5},{7,4},{4,7},{9,10},{10,9},{11,... | collective-permute-start | bytes 589832 | tf_op jit(solution)/shard_map/ppermute | solution.py:481
  33.0 1.2 %shard_map.58.refs_5_ = f32[1600,128]{1,0:T(8,128)S(1)} custom-call(f32[2880,128]{1,0:T(8,128)S(1)} %get-tuple-element.45.turned_ref), custom_call_target="tpu_custom_call" | custom-call | flops 6553600 | bytes 1024 | tf_op jit(solution)/shard_map/pallas_call | solution.py:460
  34.3 1.2 %shard_map.54.acc_in = f32[1312,128]{1,0:T(8,128)S(1)} custom-call(f32[1312,128]{1,0:T(8,128)S(1)} %get-tuple-element.39.u_ref.refs_0_, f32[240,128]{1,0:T(8,128)S(1)} %collective-permute-done.12.a_ref.b_ref, f32[240,128]{1,0:T(8,128)S(1)} %collective-permute-done.12.a_ref.b_ref, f32[128,128]{1,0:T(8,128)S(1)} %get-tuple-element.36.wind_ref, ...), custom_call_target="tpu_custom_call" | custom-call | flops 6553600 | bytes 1024 | tf_op jit(solution)/shard_map/pallas_call | solution.py:460
  35.6 1.0 %collective-permute-done.11.face_ref = f32[480,128]{1,0:T(8,128)S(1)} collective-permute-done((f32[480,128]{1,0:T(8,128)S(1)}, f32[480,128]{1,0:T(8,128)S(1)}, u32[]{:S(2)}, u32[]{:S(2)}) %collective-permute-start.11) | collective-permute-done | bytes 245792 | tf_op jit(solution)/shard_map/ppermute | solution.py:481
  36.5 0.8 %shard_map.55.acc_in = f32[1312,128]{1,0:T(8,128)S(1)} custom-call(f32[1312,128]{1,0:T(8,128)S(1)} %get-tuple-element.39.u_ref.refs_0_, f32[480,128]{1,0:T(8,128)S(1)} %collective-permute-done.11.face_ref, f32[128,128]{1,0:T(8,128)S(1)} %get-tuple-element.31.wind_ref.refs_2_, f32[40,128]{1,0:T(8,128)S(1)} %copy-done, ...), custom_call_target="tpu_custom_call", output_to_operand_aliasing={{}: (4, {})} | custom-call | flops 6553600 | bytes 1024 | tf_op jit(solution)/shard_map/pallas_call | solution.py:460
  37.3 0.7 %shard_map.56.acc_in = f32[1312,128]{1,0:T(8,128)S(1)} custom-call(f32[1312,128]{1,0:T(8,128)S(1)} %get-tuple-element.39.u_ref.refs_0_, f32[384,128]{1,0:T(8,128)S(1)} %collective-permute-done.10.face_ref, f32[1312,128]{1,0:T(8,128)S(1)} %shard_map.55.acc_in), custom_call_target="tpu_custom_call", output_to_operand_aliasing={{}: (2, {})} | custom-call | flops 6553600 | bytes 1024 | tf_op jit(solution)/shard_map/pallas_call | solution.py:460
  38.1 4.5 %collective-permute-done.9.face_ref = f32[384,128]{1,0:T(8,128)S(1)} collective-permute-done((f32[384,128]{1,0:T(8,128)S(1)}, f32[384,128]{1,0:T(8,128)S(1)}, u32[]{:S(2)}, u32[]{:S(2)}) %collective-permute-start.9) | collective-permute-done | bytes 196640 | tf_op jit(solution)/shard_map/ppermute | solution.py:481
  43.4 1.2 %shard_map.59 = (f32[1312,128]{1,0:T(8,128)S(1)}, f32[2880,128]{1,0:T(8,128)S(1)}, f32[480,128]{1,0:T(8,128)S(1)}, f32[480,128]{1,0:T(8,128)S(1)}, f32[384,128]{...) custom-call(f32[1312,128]{1,0:T(8,128)S(1)} %get-tuple-element.39.u_ref.refs_0_, ...), custom_call_target="tpu_custom_call" | custom-call | flops 6553600 | bytes 1024 | tf_op jit(solution)/shard_map/pallas_call | solution.py:460
  44.6 2.5 %collective-permute-start.16 = (f32[480,128]{1,0:T(8,128)S(1)}, f32[480,128]{1,0:T(8,128)S(1)}, u32[]{:S(2)}, u32[]{:S(2)}) collective-permute-start(f32[480,128]{1,0:T(8,128)S(1)} %get-tuple-element.50), channel_id=1, source_target_pairs={{0,8},{8,0},{16,24},{24,16},{1,9},{9,1},{17,25},{25,17},{2,10},{10... | collective-permute-start | bytes 737288 | tf_op jit(solution)/shard_map/ppermute | solution.py:481
  47.7 2.6 %collective-permute-start.14 = (f32[384,128]{1,0:T(8,128)S(1)}, f32[384,128]{1,0:T(8,128)S(1)}, u32[]{:S(2)}, u32[]{:S(2)}) collective-permute-start(f32[384,128]{1,0:T(8,128)S(1)} %get-tuple-element.48), channel_id=1, source_target_pairs={{1,2},{2,1},{3,0},{0,3},{5,6},{6,5},{7,4},{4,7},{9,10},{10,9},{11,... | collective-permute-start | bytes 589832 | tf_op jit(solution)/shard_map/ppermute | solution.py:481
  50.4 1.2 %shard_map.64.refs_5_ = f32[1600,128]{1,0:T(8,128)S(1)} custom-call(f32[2880,128]{1,0:T(8,128)S(1)} %get-tuple-element.52.turned_ref), custom_call_target="tpu_custom_call" | custom-call | flops 6553600 | bytes 1024 | tf_op jit(solution)/shard_map/pallas_call | solution.py:460
  51.7 1.2 %shard_map.60.acc_in = f32[1312,128]{1,0:T(8,128)S(1)} custom-call(f32[1312,128]{1,0:T(8,128)S(1)} %get-tuple-element.46.u_ref.refs_0_, f32[240,128]{1,0:T(8,128)S(1)} %collective-permute-done.17.a_ref.b_ref, f32[240,128]{1,0:T(8,128)S(1)} %collective-permute-done.17.a_ref.b_ref, f32[128,128]{1,0:T(8,128)S(1)} %get-tuple-element.36.wind_ref, ...), custom_call_target="tpu_custom_call" | custom-call | flops 6553600 | bytes 1024 | tf_op jit(solution)/shard_map/pallas_call | solution.py:460
  52.9 1.0 %collective-permute-done.16.face_ref = f32[480,128]{1,0:T(8,128)S(1)} collective-permute-done((f32[480,128]{1,0:T(8,128)S(1)}, f32[480,128]{1,0:T(8,128)S(1)}, u32[]{:S(2)}, u32[]{:S(2)}) %collective-permute-start.16) | collective-permute-done | bytes 245792 | tf_op jit(solution)/shard_map/ppermute | solution.py:481
  53.9 0.8 %shard_map.61.acc_in = f32[1312,128]{1,0:T(8,128)S(1)} custom-call(f32[1312,128]{1,0:T(8,128)S(1)} %get-tuple-element.46.u_ref.refs_0_, f32[480,128]{1,0:T(8,128)S(1)} %collective-permute-done.16.face_ref, f32[128,128]{1,0:T(8,128)S(1)} %get-tuple-element.31.wind_ref.refs_2_, f32[40,128]{1,0:T(8,128)S(1)} %copy-done, ...), custom_call_target="tpu_custom_call", output_to_operand_aliasing={{}: (4, {})} | custom-call | flops 6553600 | bytes 1024 | tf_op jit(solution)/shard_map/pallas_call | solution.py:460
  54.7 0.7 %shard_map.62.acc_in = f32[1312,128]{1,0:T(8,128)S(1)} custom-call(f32[1312,128]{1,0:T(8,128)S(1)} %get-tuple-element.46.u_ref.refs_0_, f32[384,128]{1,0:T(8,128)S(1)} %collective-permute-done.15.face_ref, f32[1312,128]{1,0:T(8,128)S(1)} %shard_map.61.acc_in), custom_call_target="tpu_custom_call", output_to_operand_aliasing={{}: (2, {})} | custom-call | flops 6553600 | bytes 1024 | tf_op jit(solution)/shard_map/pallas_call | solution.py:460
  55.5 4.4 %collective-permute-done.14.face_ref = f32[384,128]{1,0:T(8,128)S(1)} collective-permute-done((f32[384,128]{1,0:T(8,128)S(1)}, f32[384,128]{1,0:T(8,128)S(1)}, u32[]{:S(2)}, u32[]{:S(2)}) %collective-permute-start.14) | collective-permute-done | bytes 196640 | tf_op jit(solution)/shard_map/ppermute | solution.py:481
  60.6 1.8 %shard_map.65 = f32[8,160,128]{2,1,0:T(8,128)} custom-call(f32[1312,128]{1,0:T(8,128)S(1)} %get-tuple-element.46.u_ref.refs_0_, f32[480,128]{1,0:T(8,128)S(1)} %collective-permute-done.13.refs_1_, f32[128,128]{1,0:T(8,128)S(1)} %get-tuple-element.31.wind_ref.refs_2_, f32[40,128]{1,0:T(8,128)S(1)} %copy-done, f32[1312,128]{1,0:T(8,128)S(1)} %shard_map.63.refs_4_, ...), custom_call_target="tpu_custom_call" | custom-call | flops 6553600 | bytes 1024 | tf_op jit(solution)/shard_map/pallas_call | solution.py:460
  (31 shorter events, 4.3 us)
Async XLA Ops:
  1.5 22.5 %collective-permute-start.3 = (f32[480,128]{1,0:T(8,128)S(1)}, f32[480,128]{1,0:T(8,128)S(1)}, u32[]{:S(2)}, u32[]{:S(2)}) collective-permute-start(f32[480,128]{1,0:T(8,128)S(1)} %get-tuple-element.34), channel_id=1, source_target_pairs={{0,8},{8,0},{16,24},{24,16},{1,9},{9,1},{17,25},{25,17},{2,10},{10... | collective-permute-start | bytes 737288 | tf_op jit(solution)/shard_map/ppermute | solution.py:481
  4.5 21.9 %collective-permute-start = (f32[480,128]{1,0:T(8,128)S(1)}, f32[480,128]{1,0:T(8,128)S(1)}, u32[]{:S(2)}, u32[]{:S(2)}) collective-permute-start(f32[480,128]{1,0:T(8,128)S(1)} %get-tuple-element.30), channel_id=1, source_target_pairs={{0,4},{4,0},{8,16},{12,20},{16,8},{20,12},{24,28},{28,24},{1,5},{5... | collective-permute-start | bytes 737288 | tf_op jit(solution)/shard_map/ppermute | solution.py:481
  4.5 20.3 %collective-permute-start.2 = (f32[384,128]{1,0:T(8,128)S(1)}, f32[384,128]{1,0:T(8,128)S(1)}, u32[]{:S(2)}, u32[]{:S(2)}) collective-permute-start(f32[384,128]{1,0:T(8,128)S(1)} %get-tuple-element.33), channel_id=1, source_target_pairs={{0,1},{1,0},{2,3},{3,2},{4,5},{5,4},{6,7},{7,6},{8,9},{9,8},{10,11... | collective-permute-start | bytes 589832 | tf_op jit(solution)/shard_map/ppermute | solution.py:481
  6.1 19.5 %collective-permute-start.1 = (f32[384,128]{1,0:T(8,128)S(1)}, f32[384,128]{1,0:T(8,128)S(1)}, u32[]{:S(2)}, u32[]{:S(2)}) collective-permute-start(f32[384,128]{1,0:T(8,128)S(1)} %get-tuple-element.32), channel_id=1, source_target_pairs={{1,2},{2,1},{3,0},{0,3},{5,6},{6,5},{7,4},{4,7},{9,10},{10,9},{11,... | collective-permute-start | bytes 589832 | tf_op jit(solution)/shard_map/ppermute | solution.py:481
  8.6 7.3 %collective-permute-start.5 = (f32[8,128]{1,0:T(8,128)S(1)}, f32[8,128]{1,0:T(8,128)S(1)}, u32[]{:S(2)}, u32[]{:S(2)}) collective-permute-start(f32[8,128]{1,0:T(8,128)S(1)} %get-tuple-element.38), channel_id=1, source_target_pairs={{0,8},{8,0},{16,24},{24,16},{1,9},{9,1},{17,25},{25,17},{2,10},{10... | collective-permute-start | bytes 12296 | tf_op jit(solution)/shard_map/ppermute | solution.py:515
  15.9 3.6 %collective-permute-start.6 = (f32[8,128]{1,0:T(8,128)S(1)}, f32[8,128]{1,0:T(8,128)S(1)}, u32[]{:S(2)}, u32[]{:S(2)}) collective-permute-start(f32[8,128]{1,0:T(8,128)S(1)} %max.9), channel_id=1, source_target_pairs={{0,16},{8,24},{16,0},{24,8},{1,17},{9,25},{17,1},{25,9},{2,18},{10... | collective-permute-start | bytes 12296 | tf_op jit(solution)/shard_map/ppermute | solution.py:515
  19.5 3.3 %copy-start.1 = (f32[40,128]{1,0:T(8,128)S(1)}, f32[40,128]{1,0:T(8,128)}, u32[]{:S(2)}) copy-start(f32[40,128]{1,0:T(8,128)} %constant.5.clone.speed_ref) | copy-start | bytes 61444
  19.5 1.5 %collective-permute-start.7 = (f32[8,128]{1,0:T(8,128)S(1)}, f32[8,128]{1,0:T(8,128)S(1)}, u32[]{:S(2)}, u32[]{:S(2)}) collective-permute-start(f32[8,128]{1,0:T(8,128)S(1)} %max.10), channel_id=1, source_target_pairs={{0,4},{4,0},{1,5},{5,1},{2,6},{6,2},{3,7},{7,3},{8,12},{12,8},{9,1... | collective-permute-start | bytes 12296 | tf_op jit(solution)/shard_map/ppermute | solution.py:515
  21.0 1.8 %collective-permute-start.4 = (f32[240,128]{1,0:T(8,128)S(1)}, f32[240,128]{1,0:T(8,128)S(1)}, u32[]{:S(2)}, u32[]{:S(2)}) collective-permute-start(f32[240,128]{1,0:T(8,128)S(1)} %get-tuple-element.35), channel_id=1, source_target_pairs={{0,4},{4,0},{1,5},{5,1},{2,6},{6,2},{3,7},{7,3},{8,12},{12,8},{9,1... | collective-permute-start | bytes 368648 | tf_op jit(solution)/shard_map/ppermute | solution.py:481
  21.6 2.5 %copy-start = (f32[40,128]{1,0:T(8,128)S(1)}, f32[40,128]{1,0:T(8,128)}, u32[]{:S(2)}) copy-start(f32[40,128]{1,0:T(8,128)} %constant.4.clone.speed_ref.refs_3_) | copy-start | bytes 61444
  27.6 8.9 %collective-permute-start.11 = (f32[480,128]{1,0:T(8,128)S(1)}, f32[480,128]{1,0:T(8,128)S(1)}, u32[]{:S(2)}, u32[]{:S(2)}) collective-permute-start(f32[480,128]{1,0:T(8,128)S(1)} %get-tuple-element.43), channel_id=1, source_target_pairs={{0,8},{8,0},{16,24},{24,16},{1,9},{9,1},{17,25},{25,17},{2,10},{10... | collective-permute-start | bytes 737288 | tf_op jit(solution)/shard_map/ppermute | solution.py:481
  29.0 14.4 %collective-permute-start.8 = (f32[480,128]{1,0:T(8,128)S(1)}, f32[480,128]{1,0:T(8,128)S(1)}, u32[]{:S(2)}, u32[]{:S(2)}) collective-permute-start(f32[480,128]{1,0:T(8,128)S(1)} %get-tuple-element.40), channel_id=1, source_target_pairs={{0,4},{4,0},{8,16},{12,20},{16,8},{20,12},{24,28},{28,24},{1,5},{5... | collective-permute-start | bytes 737288 | tf_op jit(solution)/shard_map/ppermute | solution.py:481
  29.0 8.4 %collective-permute-start.10 = (f32[384,128]{1,0:T(8,128)S(1)}, f32[384,128]{1,0:T(8,128)S(1)}, u32[]{:S(2)}, u32[]{:S(2)}) collective-permute-start(f32[384,128]{1,0:T(8,128)S(1)} %get-tuple-element.42), channel_id=1, source_target_pairs={{0,1},{1,0},{2,3},{3,2},{4,5},{5,4},{6,7},{7,6},{8,9},{9,8},{10,11... | collective-permute-start | bytes 589832 | tf_op jit(solution)/shard_map/ppermute | solution.py:481
  30.5 12.1 %collective-permute-start.9 = (f32[384,128]{1,0:T(8,128)S(1)}, f32[384,128]{1,0:T(8,128)S(1)}, u32[]{:S(2)}, u32[]{:S(2)}) collective-permute-start(f32[384,128]{1,0:T(8,128)S(1)} %get-tuple-element.41), channel_id=1, source_target_pairs={{1,2},{2,1},{3,0},{0,3},{5,6},{6,5},{7,4},{4,7},{9,10},{10,9},{11,... | collective-permute-start | bytes 589832 | tf_op jit(solution)/shard_map/ppermute | solution.py:481
  33.0 1.3 %collective-permute-start.12 = (f32[240,128]{1,0:T(8,128)S(1)}, f32[240,128]{1,0:T(8,128)S(1)}, u32[]{:S(2)}, u32[]{:S(2)}) collective-permute-start(f32[240,128]{1,0:T(8,128)S(1)} %get-tuple-element.44), channel_id=1, source_target_pairs={{0,4},{4,0},{1,5},{5,1},{2,6},{6,2},{3,7},{7,3},{8,12},{12,8},{9,1... | collective-permute-start | bytes 368648 | tf_op jit(solution)/shard_map/ppermute | solution.py:481
  44.6 9.4 %collective-permute-start.16 = (f32[480,128]{1,0:T(8,128)S(1)}, f32[480,128]{1,0:T(8,128)S(1)}, u32[]{:S(2)}, u32[]{:S(2)}) collective-permute-start(f32[480,128]{1,0:T(8,128)S(1)} %get-tuple-element.50), channel_id=1, source_target_pairs={{0,8},{8,0},{16,24},{24,16},{1,9},{9,1},{17,25},{25,17},{2,10},{10... | collective-permute-start | bytes 737288 | tf_op jit(solution)/shard_map/ppermute | solution.py:481
  47.1 13.5 %collective-permute-start.13 = (f32[480,128]{1,0:T(8,128)S(1)}, f32[480,128]{1,0:T(8,128)S(1)}, u32[]{:S(2)}, u32[]{:S(2)}) collective-permute-start(f32[480,128]{1,0:T(8,128)S(1)} %get-tuple-element.47), channel_id=1, source_target_pairs={{0,4},{4,0},{8,16},{12,20},{16,8},{20,12},{24,28},{28,24},{1,5},{5... | collective-permute-start | bytes 737288 | tf_op jit(solution)/shard_map/ppermute | solution.py:481
  47.1 7.6 %collective-permute-start.15 = (f32[384,128]{1,0:T(8,128)S(1)}, f32[384,128]{1,0:T(8,128)S(1)}, u32[]{:S(2)}, u32[]{:S(2)}) collective-permute-start(f32[384,128]{1,0:T(8,128)S(1)} %get-tuple-element.49), channel_id=1, source_target_pairs={{0,1},{1,0},{2,3},{3,2},{4,5},{5,4},{6,7},{7,6},{8,9},{9,8},{10,11... | collective-permute-start | bytes 589832 | tf_op jit(solution)/shard_map/ppermute | solution.py:481
  47.7 12.1 %collective-permute-start.14 = (f32[384,128]{1,0:T(8,128)S(1)}, f32[384,128]{1,0:T(8,128)S(1)}, u32[]{:S(2)}, u32[]{:S(2)}) collective-permute-start(f32[384,128]{1,0:T(8,128)S(1)} %get-tuple-element.48), channel_id=1, source_target_pairs={{1,2},{2,1},{3,0},{0,3},{5,6},{6,5},{7,4},{4,7},{9,10},{10,9},{11,... | collective-permute-start | bytes 589832 | tf_op jit(solution)/shard_map/ppermute | solution.py:481
  50.4 1.3 %collective-permute-start.17 = (f32[240,128]{1,0:T(8,128)S(1)}, f32[240,128]{1,0:T(8,128)S(1)}, u32[]{:S(2)}, u32[]{:S(2)}) collective-permute-start(f32[240,128]{1,0:T(8,128)S(1)} %get-tuple-element.51), channel_id=1, source_target_pairs={{0,4},{4,0},{1,5},{5,1},{2,6},{6,2},{3,7},{7,3},{8,12},{12,8},{9,1... | collective-permute-start | bytes 368648 | tf_op jit(solution)/shard_map/ppermute | solution.py:481
